TPU v7x, 32 devices: a whole 2x2x4 slice. The times are simulated.
32 devices in a mesh: grp: 2 (over y), seq: 16 (over z, x, core).
Axes of the slice: x: 2, y: 2, z: 4, core: 2. Of those that a mesh axis runs over, the one named last changes fastest.
Arguments:
- hidden: bfloat16 [16, 4096], P('grp'), parts along dimension 0, may hold values from -6 to 6
- mix_gain: float32 [4096], replicated, may hold values from 0.5 to 1.5
- in_gate_input: bfloat16 [4096, 2048], P(None, 'seq'), may hold values from -0.09375 to 0.09375
- in_step: bfloat16 [4096, 16], P(None, 'seq'), may hold values from -0.09375 to 0.09375
- in_groups: bfloat16 [4096, 2048], P(None, 'seq'), may hold values from -0.09375 to 0.09375
- conv_input: bfloat16 [16, 3, 1024], P('grp', None, 'seq'), parts along dimension 0, may hold values from -6 to 6
- conv_groups: bfloat16 [16, 3, 2048], P('grp', None, 'seq'), parts along dimension 0, may hold values from -6 to 6
- taps_input: float32 [5, 1024], P(None, 'seq'), may hold values from -0.6 to 0.6
- taps_groups: float32 [5, 2048], P(None, 'seq'), may hold values from -0.6 to 0.6
- decay_rate: float32 [16], P('seq'), may hold values from 1 to 16
- step_bias: float32 [16], P('seq'), may hold values from -4 to -1
- skip_gain: float32 [16], P('seq'), may hold values from 0.1 to 1.9
- norm_gain: float32 [1024], P('seq'), may hold values from 0.5 to 1.5
- out_mixer: bfloat16 [1024, 4096], P('seq'), may hold values from -0.1875 to 0.1875
- ssm_state: float32 [16, 16, 64, 128], P('grp', 'seq'), parts along dimension 0, may hold values from -6 to 6
- attn_gain: float32 [4096], P('seq'), may hold values from 0.5 to 1.5
- w_qkv: bfloat16 [4096, 6144], P('seq'), may hold values from -0.09375 to 0.09375
- w_out: bfloat16 [4096, 4096], P(None, 'seq'), may hold values from -0.09375 to 0.09375
- kv_cache: bfloat16 [64, 128, 2048], P(('grp', 'seq')), parts along dimension 0, may hold values from -310 to 310
- page_table: int32 [16, 4], P('grp'), parts along dimension 0, may hold values from 0 to 31, as said below
- lengths: int32 [16], P('grp'), parts along dimension 0, may hold values from 1 to 512
Outputs:
- final: bfloat16 [16, 4096], P('grp', 'seq'), parts along dimension 0
- new_state: float32 [16, 16, 64, 128], P('grp', 'seq'), parts along dimension 0
- new_kv: bfloat16 [16, 2048], P('grp'), parts along dimension 0
There are 2 independent parts, one for each index of `grp`. A program takes and returns all parts, laid end to end along the dimension named above; an argument that names none is the same for every part. Nothing has to cross between parts.
Inputs may be any that keep to these rules, and one draw needn't show every extreme that they name: `page_table`: each number 0 to 31 appears exactly once.
All inputs are finite; a program needn't handle non-finite values.
Results may differ from a plain program's by a relative error of at most 0.018.
Values may be sent and summed in bfloat16 or wider, within the bound.
No kernel may reach another device: no remote copies, remote signals or barrier semaphores. Data moves between devices by JAX's collectives and lax.ppermute only.
A program may use at most 64 MiB of HBM per device.

v0:
```python
import jax
import jax.numpy as jnp
from jax import lax
from jax.sharding import PartitionSpec as P

QH = 32
KVH = 8
HD = 128
STATE = 128
GROUPS = 8


epsilon = 1e-05
lowest = -1e30


def merged(array, axis, combine):
    everything = jax.tree.map(
        lambda part, kind: lax.all_gather(part.astype(kind), axis),
        array,
        (jnp.bfloat16, jnp.bfloat16, jnp.bfloat16),
    )

    def take(k):
        return jax.tree.map(lambda part, own: part[k].astype(own.dtype), everything, array)

    return lax.fori_loop(
        1, lax.axis_size(axis), lambda k, so_far: combine(so_far, take(k)), take(0)
    )


def conv_step(state, fresh, taps):
    window = jnp.concatenate([state.astype(jnp.float32), fresh[:, None, :]], axis=1)
    summed = jnp.sum(window * taps[:-1][None], axis=1) + taps[-1][None]
    return jax.nn.silu(summed)


def merge_pair(first, second):
    peak = jnp.maximum(first[0], second[0])
    first_factor = jnp.exp(first[0] - peak)
    second_factor = jnp.exp(second[0] - peak)
    total = first[1] * first_factor + second[1] * second_factor
    values = first[2] * first_factor[..., None] + second[2] * second_factor[..., None]
    return (peak, total, values)


def finish(peak_prior, total_prior, values_prior, query_rows, key_rows, value_rows, scale):
    own = jnp.sum(query_rows.astype(jnp.float32) * key_rows.astype(jnp.float32), axis=-1) * scale
    peak = jnp.maximum(peak_prior, own)
    old_factor = jnp.exp(peak_prior - peak)
    own_weight = jnp.exp(own - peak)
    summed = values_prior * old_factor[..., None] + own_weight[..., None] * value_rows.astype(
        jnp.float32
    )
    return (summed / (total_prior * old_factor + own_weight)[..., None]).astype(jnp.bfloat16)


def shards(
    hidden,
    mix_gain,
    in_gate_input,
    in_step,
    in_groups,
    conv_input,
    conv_groups,
    taps_input,
    taps_groups,
    decay_rate,
    step_bias,
    skip_gain,
    norm_gain,
    out_mixer,
    ssm_state,
    attn_gain,
    w_qkv,
    w_out,
    kv_cache,
    page_table,
    lengths,
):
    highest = lax.Precision.HIGHEST
    count_seq = lax.axis_size("seq")
    position = lax.axis_index("seq")
    requests = hidden.shape[0]
    width = hidden.shape[1]
    heads_here = in_step.shape[1]
    head_width = in_gate_input.shape[1] // (2 * heads_here)
    heads_total = heads_here * count_seq
    per_group = heads_total // GROUPS
    stream = hidden.astype(jnp.float32)
    normed = (
        stream * lax.rsqrt(jnp.mean(stream * stream, axis=-1, keepdims=True) + epsilon) * mix_gain
    ).astype(jnp.bfloat16)
    gate_input = jnp.dot(normed, in_gate_input, preferred_element_type=jnp.float32).reshape(
        requests, heads_here, 2, head_width
    )
    gate_part = gate_input[:, :, 0]
    input_part = gate_input[:, :, 1].reshape(requests, heads_here * head_width)
    step_raw = jnp.dot(normed, in_step, preferred_element_type=jnp.float32)
    group_raw = jnp.dot(normed, in_groups, preferred_element_type=jnp.float32)
    conv_out = conv_step(conv_input, input_part, taps_input).reshape(
        requests, heads_here, head_width
    )
    group_conv = conv_step(conv_groups, group_raw, taps_groups).astype(jnp.bfloat16)
    group_all = lax.all_gather(group_conv, "seq", axis=1, tiled=True).astype(jnp.float32)
    inject = group_all[:, : GROUPS * STATE].reshape(requests, GROUPS, STATE)
    readout = group_all[:, GROUPS * STATE :].reshape(requests, GROUPS, STATE)
    head_ids = position * heads_here + jnp.arange(heads_here, dtype=jnp.int32)
    select = (head_ids[:, None] % GROUPS == jnp.arange(GROUPS, dtype=jnp.int32)[None, :]).astype(
        jnp.float32
    )
    inject_heads = jnp.einsum("hg,rgn->rhn", select, inject, precision=highest)
    readout_heads = jnp.einsum("hg,rgn->rhn", select, readout, precision=highest)
    step_size = jax.nn.softplus(step_raw + step_bias)
    decay = jnp.exp(-decay_rate * step_size)
    new_state = (
        decay[:, :, None, None] * ssm_state
        + (step_size[:, :, None] * conv_out)[:, :, :, None] * inject_heads[:, :, None, :]
    )
    ssm_out = (
        jnp.einsum("rhpn,rhn->rhp", new_state, readout_heads, precision=highest)
        + skip_gain[None, :, None] * conv_out
    )
    gated = ssm_out * jax.nn.silu(gate_part)
    head_squares = jnp.sum(gated * gated, axis=-1)
    all_squares = lax.all_gather(head_squares, "seq", axis=1, tiled=True)
    group_means = jnp.sum(all_squares.reshape(requests, per_group, GROUPS), axis=1) / (
        per_group * head_width
    )
    own_means = jnp.einsum("hg,rg->rh", select, group_means, precision=highest)
    normed_mix = (
        gated
        * lax.rsqrt(own_means + epsilon)[..., None]
        * norm_gain.reshape(heads_here, head_width)
    ).astype(jnp.bfloat16)
    mixer_term = jnp.dot(
        normed_mix.reshape(requests, heads_here * head_width),
        out_mixer,
        preferred_element_type=jnp.float32,
    )
    mixer = lax.psum_scatter(mixer_term, "seq", scatter_dimension=1, tiled=True)
    columns = width // count_seq
    stream_cols = lax.dynamic_slice_in_dim(stream, position * columns, columns, 1)
    middle = (stream_cols + mixer).astype(jnp.bfloat16)
    middle_f = middle.astype(jnp.float32)
    scaled = (middle_f * attn_gain).astype(jnp.bfloat16)
    partial_proj = jnp.dot(scaled, w_qkv, preferred_element_type=jnp.float32)
    partial_sq = jnp.sum(middle_f * middle_f, axis=-1)
    projected, total_sq = lax.psum((partial_proj, partial_sq), "seq")
    qkv = (projected * lax.rsqrt(total_sq / width + epsilon)[:, None]).astype(jnp.bfloat16)
    group_size = QH // KVH
    queries = qkv[:, : QH * HD]
    fresh_keys = qkv[:, QH * HD : (QH + KVH) * HD].reshape(requests, KVH, HD)
    fresh_values = qkv[:, (QH + KVH) * HD :].reshape(requests, KVH, HD)
    new_kv = qkv[:, QH * HD :]
    scale = 1.0 / HD**0.5
    pages_here = kv_cache.shape[0]
    page_len = kv_cache.shape[1]
    pages_req = page_table.shape[1]
    slots = position * pages_here + jnp.arange(pages_here, dtype=jnp.int32)
    matches = page_table[None, :, :] == slots[:, None, None]
    owner_hit = jnp.any(matches, axis=2)
    owner = owner_hit.astype(jnp.bfloat16)
    logical = jnp.sum(
        jnp.any(matches, axis=1) * jnp.arange(pages_req, dtype=jnp.int32)[None, :], axis=1
    )
    page_length = jnp.sum(jnp.where(owner_hit, lengths[None, :], 0), axis=1)
    token_pos = logical[:, None] * page_len + jnp.arange(page_len, dtype=jnp.int32)[None, :]
    live = token_pos < page_length[:, None]
    page_queries = jnp.dot(owner, queries, preferred_element_type=jnp.float32).astype(jnp.bfloat16)
    page_queries = page_queries.reshape(pages_here, KVH, group_size, HD)
    cached = kv_cache.reshape(pages_here, page_len, 2, KVH, HD)
    scores = (
        jnp.einsum(
            "pgjd,ptgd->pgjt", page_queries, cached[:, :, 0], preferred_element_type=jnp.float32
        )
        * scale
    )
    live_mask = live[:, None, None, :]
    masked = jnp.where(live_mask, scores, lowest)
    page_peak = jnp.max(masked, axis=-1)
    weights = jnp.where(live_mask, jnp.exp(masked - page_peak[..., None]), 0.0)
    page_total = jnp.sum(weights, axis=-1)
    page_values = jnp.einsum(
        "pgjt,ptgd->pgjd",
        weights.astype(jnp.bfloat16),
        cached[:, :, 1],
        preferred_element_type=jnp.float32,
    )
    owner_mask = owner_hit[:, :, None, None]
    request_peak = jnp.max(jnp.where(owner_mask, page_peak[:, None], lowest), axis=0)
    factor = jnp.where(owner_mask, jnp.exp(page_peak[:, None] - request_peak[None]), 0.0)
    request_total = jnp.einsum("prgj,pgj->rgj", factor, page_total, precision=highest)
    request_values = jnp.einsum("prgj,pgjd->rgjd", factor, page_values, precision=highest)
    request_peak = request_peak.reshape(requests, QH)
    request_total = request_total.reshape(requests, QH)
    request_values = request_values.reshape(requests, QH, HD)
    query_rows = queries.reshape(requests, QH, HD)
    key_rows = jnp.repeat(fresh_keys, group_size, axis=1)
    value_rows = jnp.repeat(fresh_values, group_size, axis=1)
    peak_all, total_all, values_all = merged(
        (request_peak, request_total, request_values), "seq", merge_pair
    )
    attended = finish(
        peak_all, total_all, values_all, query_rows, key_rows, value_rows, scale
    ).reshape(requests, QH * HD)
    final = (middle_f + jnp.dot(attended, w_out, preferred_element_type=jnp.float32)).astype(
        jnp.bfloat16
    )
    return (final, new_state, new_kv)


def solution(mesh):
    placed = (
        P("grp", None),
        P(),
        P(None, "seq"),
        P(None, "seq"),
        P(None, "seq"),
        P("grp", None, "seq"),
        P("grp", None, "seq"),
        P(None, "seq"),
        P(None, "seq"),
        P("seq"),
        P("seq"),
        P("seq"),
        P("seq"),
        P("seq", None),
        P("grp", "seq", None, None),
        P("seq"),
        P("seq", None),
        P(None, "seq"),
        P(("grp", "seq"), None, None),
        P("grp", None),
        P("grp"),
    )
    return jax.shard_map(
        shards,
        mesh=mesh,
        in_specs=placed,
        out_specs=(P("grp", "seq"), P("grp", "seq", None, None), P("grp", None)),
        check_vma=False,
    )
```

profile of v0, /device:TPU:0, one launch (start us, length us, event | category | flops | bytes accessed | tf_op | source)
XLA Modules:
  0.0 282.0 jit_solution(5698425340825484725)
XLA Ops:
  12.0 1.6 convolution_bitcast_fusion.1
  13.6 23.2 %all_gather.18 = bf16[8,2048]{1,0:T(8,128)(2,1)S(1)} all-gather(bf16[8,128]{1,0:T(8,128)(2,1)S(1)} %multiply_convert_fusion.3), channel_id=1, replica_groups=mesh['grp'=2,'seq'=16] {'seq'}, dimensions={1}, use_global_device_ids=true | all-gather | bytes 34816 | tf_op jit(solution)/shard_map/all_gather | solution.py:105
  36.8 1.6 fusion.68
  41.4 1.1 multiply_exponential_fusion
  42.5 1.1 multiply_add_fusion
  44.3 17.4 %all-gather = f32[16,1,8]{2,1,0:T(1,128)S(1)} all-gather(f32[1,1,8]{2,1,0:T(1,128)S(1)} %bitcast.157), channel_id=1, replica_groups=mesh['grp'=2,'seq'=16] {'seq'}, dimensions={0}, use_global_device_ids=true | all-gather | bytes 544 | tf_op jit(solution)/shard_map/all_gather | solution.py:126
  62.0 1.9 fusion.46
  65.1 2.3 copy.80
  67.5 50.7 %reduce-scatter.2.cloned.1.call-done = f32[8,256]{1,0:T(8,128)} async-done(((f32[8,4096]{1,0:T(8,128)}), f32[8,256]{1,0:T(8,128)}) %reduce-scatter.2.cloned.1.call-update) | async-done | bytes 8208 | tf_op jit(solution)/shard_map/reduce_scatter | solution.py:141
  119.0 1.2 fusion.42
  120.3 29.5 %psum.15 = f32[8]{0:T(128)S(1)} all-reduce(f32[8]{0:T(128)S(1)} %get-tuple-element.214), channel_id=1, replica_groups=mesh['grp'=2,'seq'=16] {'seq'}, use_global_device_ids=true, to_apply=%region_12.13 | all-reduce | flops 8 | bytes 64 | tf_op jit(solution)/shard_map/psum | solution.py:149
  149.8 61.6 %all-reduce.2.cloned.1.call-done = f32[8,6144]{1,0:T(8,128)} async-done(((f32[8,6144]{1,0:T(8,128)}), f32[8,6144]{1,0:T(8,128)}) %all-reduce.2.cloned.1.call-update) | async-done | bytes 196624 | tf_op jit(solution)/shard_map/psum | solution.py:149
  211.4 1.0 multiply_convert_fusion
  212.6 1.4 fusion.73
  214.1 1.5 fusion.8
  218.7 19.5 %all_gather.21 = bf16[16,8,32]{2,1,0:T(8,128)(2,1)S(1)} all-gather(bf16[1,8,32]{2,1,0:T(8,128)(2,1)S(1)} %copy.84), channel_id=1, replica_groups=mesh['grp'=2,'seq'=16] {'seq'}, dimensions={0}, use_global_device_ids=true | all-gather | bytes 8704 | tf_op jit(solution)/shard_map/all_gather | solution.py:19
  238.2 17.8 %all_gather.20 = bf16[16,8,32]{2,1,0:T(8,128)(2,1)S(1)} all-gather(bf16[1,8,32]{2,1,0:T(8,128)(2,1)S(1)} %copy.83), channel_id=1, replica_groups=mesh['grp'=2,'seq'=16] {'seq'}, dimensions={0}, use_global_device_ids=true | all-gather | bytes 8704 | tf_op jit(solution)/shard_map/all_gather | solution.py:19
  256.9 15.8 %while.19 = (s32[]{:T(128)}, f32[8,32]{1,0:T(8,128)S(1)}, f32[8,32]{1,0:T(8,128)S(1)}, f32[8,32,128]{2,1,0:T(8,128)S(1)}, bf16[16,8,32]{2,1,0:T(8,128)(2,1)S(1)}...) while((s32[]{:T(128)}, f32[8,32]{1,0:T(8,128)S(1)}, ...), condition=%wide.region_17.18_spmd, body=%wide.region_16.17_spmd.sunk | while | flops 133125 | bytes 337047 | solution.py:27
  256.9 1.0 fusion.87
  258.0 1.0 fusion.87
  259.0 1.0 fusion.87
  260.1 1.0 fusion.87
  261.1 1.0 fusion.87
  262.2 1.0 fusion.87
  263.2 1.0 fusion.87
  264.3 1.0 fusion.87
  265.3 1.0 fusion.87
  266.4 1.0 fusion.87
  267.4 1.0 fusion.87
  268.5 1.0 fusion.87
  269.6 1.0 fusion.87
  272.9 2.6 fusion.4
  (95 shorter events, 15.8 us)
Async XLA Ops:
  7.2 111.9 %copy-start = (bf16[256,6144]{1,0:T(8,128)(2,1)S(1)}, bf16[256,6144]{1,0:T(8,128)(2,1)}, u32[]{:S(2)}) copy-start(bf16[256,6144]{1,0:T(8,128)(2,1)} %param.39) | copy-start | bytes 9437188
  7.2 56.9 %copy-start.1 = (bf16[8,4096]{1,0:T(8,128)(2,1)S(1)}, bf16[8,4096]{1,0:T(8,128)(2,1)}, u32[]{:S(2)}) copy-start(bf16[8,4096]{1,0:T(8,128)(2,1)} %param.23) | copy-start | bytes 196612
  7.2 54.9 %copy-start.5 = (f32[64]{0:T(128)S(1)}, f32[64]{0:T(128)}, u32[]{:S(2)}) copy-start(f32[64]{0:T(128)} %param.35) | copy-start | bytes 772
  7.2 57.5 %copy-start.3 = (s32[8,4]{0,1:T(4,128)S(1)}, s32[8,4]{0,1:T(4,128)}, u32[]{:S(2)}) copy-start(s32[8,4]{0,1:T(4,128)} %param.42) | copy-start | bytes 388
  7.2 111.0 %reduce-scatter.2.cloned.1.call-start = ((), (), s32[]{:S(2)}) async-start(), calls=%async_computation.1 | async-start | bytes 139264 | tf_op jit(solution)/shard_map/reduce_scatter | solution.py:141
  12.0 55.4 %copy-start.6 = (s32[8]{0:T(128)S(1)}, s32[8]{0:T(128)}, u32[]{:S(2)}) copy-start(s32[8]{0:T(128)} %param.43) | copy-start | bytes 100
  12.0 107.1 %copy-start.4 = (f32[256]{0:T(256)S(1)}, f32[256]{0:T(256)}, u32[]{:S(2)}) copy-start(f32[256]{0:T(256)} %param.38) | copy-start | bytes 3076
  43.6 76.6 %copy-start.2 = (f32[8,1,64,128]{3,2,1,0:T(8,128)}, f32[8,1,64,128]{3,2,1,0:T(8,128)S(1)}, u32[]{:S(2)}) copy-start(f32[8,1,64,128]{3,2,1,0:T(8,128)S(1)} %multiply_add_fusion) | copy-start | bytes 786436
  64.0 147.4 %all-reduce.2.cloned.1.call-start = ((), (), s32[]{:S(2)}) async-start(), calls=%async_computation.2 | async-start | bytes 393216 | tf_op jit(solution)/shard_map/psum | solution.py:149
  120.3 135.7 %all-gather.3.cloned.1.call-start = ((), (), s32[]{:S(2)}) async-start(), calls=%async_computation.3 | async-start | bytes 1114112 | tf_op jit(solution)/shard_map/all_gather | solution.py:19
Sparse Core Ops, SparseCore 0:
  64.1 54.0 reduce-scatter.1
  121.6 89.7 all-reduce.1
  217.1 36.9 all-gather.2
where the time goes:
time: 284 us; the launch traced here: 282 us
  waiting for transfers between devices  112 us (39%)
  blocking collectives  107 us (38%)
  other arithmetic  23.6 us (8%)
  between operations  15.9 us (6%)
  matrix products  14.8 us (5%)
  local copies, waits for them, and re-layouts  7.37 us (3%)
    psum x1, waiting for transfers between devices, shards(): projected, total_sq = lax.psum((partial_proj, partial_sq), 'seq')  61.6 us
    reduce_scatter x1, waiting for transfers between devices, shards(): mixer = lax.psum_scatter(mixer_term, 'seq', scatter_dimension=1, tiled=True)  50.7 us
    all_gather x2, blocking collectives, merged(): lax.all_gather(part.astype(kind), axis)  37.3 us
    psum x1, blocking collectives, shards(): projected, total_sq = lax.psum((partial_proj, partial_sq), 'seq')  29.5 us
    all_gather x1, blocking collectives, shards(): lax.all_gather(group_conv, 'seq', axis=1, tiled=True).astype(jnp.float32)  23.2 us
    all_gather x1, blocking collectives, shards(): all_squares = lax.all_gather(head_squares, 'seq', axis=1, tiled=True)  17.4 us
    add x15, other arithmetic, merge_pair(): first[2] * first_factor[..., None] + second[2] * second_factor[..., None]  15 us
  transfers between devices with their start and end apart: 3, of which 2 were waited for; matrix products, arithmetic and copies ran while one was open for 2% of the time, Pallas kernels for 0%

commit v1 on v0

v1 whole, which is shorter than its diff:
```python
import jax
import jax.numpy as jnp
from jax import lax
from jax.sharding import PartitionSpec as P

QH = 32
KVH = 8
HD = 128
STATE = 128
GROUPS = 8
LANES = 128

epsilon = 1e-05
lowest = -1e30


def conv_step(state, fresh, taps):
    window = jnp.concatenate([state.astype(jnp.float32), fresh[:, None, :]], axis=1)
    summed = jnp.sum(window * taps[:-1][None], axis=1) + taps[-1][None]
    return jax.nn.silu(summed)


def split(value, parts):
    pieces = []
    rest = value
    for _ in range(parts):
        piece = lax.reduce_precision(rest, 8, 7)
        pieces.append(piece.astype(jnp.bfloat16))
        rest = rest - piece
    return pieces


def group_vectors(group_conv, heads_here, requests):
    count = lax.axis_size("seq")
    position = lax.axis_index("seq")
    if heads_here == 1 and group_conv.shape[1] == STATE and count == 2 * GROUPS:
        swap = [(i, (i + GROUPS) % count) for i in range(count)]
        other = lax.ppermute(group_conv, "seq", swap)
        first = position < GROUPS
        inject = jnp.where(first, group_conv, other)
        readout = jnp.where(first, other, group_conv)
        return (
            inject.astype(jnp.float32)[:, None, :],
            readout.astype(jnp.float32)[:, None, :],
        )
    group_all = lax.all_gather(group_conv, "seq", axis=1, tiled=True).astype(jnp.float32)
    inject = group_all[:, : GROUPS * STATE].reshape(requests, GROUPS, STATE)
    readout = group_all[:, GROUPS * STATE :].reshape(requests, GROUPS, STATE)
    head_ids = position * heads_here + jnp.arange(heads_here, dtype=jnp.int32)
    return inject[:, head_ids % GROUPS], readout[:, head_ids % GROUPS]


def shards(
    hidden,
    mix_gain,
    in_gate_input,
    in_step,
    in_groups,
    conv_input,
    conv_groups,
    taps_input,
    taps_groups,
    decay_rate,
    step_bias,
    skip_gain,
    norm_gain,
    out_mixer,
    ssm_state,
    attn_gain,
    w_qkv,
    w_out,
    kv_cache,
    page_table,
    lengths,
):
    count_seq = lax.axis_size("seq")
    position = lax.axis_index("seq")
    requests = hidden.shape[0]
    width = hidden.shape[1]
    heads_here = in_step.shape[1]
    head_width = in_gate_input.shape[1] // (2 * heads_here)
    heads_total = heads_here * count_seq
    per_group = heads_total // GROUPS
    columns = width // count_seq
    stream = hidden.astype(jnp.float32)
    normed = (
        stream * lax.rsqrt(jnp.mean(stream * stream, axis=-1, keepdims=True) + epsilon) * mix_gain
    ).astype(jnp.bfloat16)
    group_raw = jnp.dot(normed, in_groups, preferred_element_type=jnp.float32)
    group_conv = conv_step(conv_groups, group_raw, taps_groups).astype(jnp.bfloat16)
    inject_heads, readout_heads = group_vectors(group_conv, heads_here, requests)
    gate_input = jnp.dot(normed, in_gate_input, preferred_element_type=jnp.float32).reshape(
        requests, heads_here, 2, head_width
    )
    gate_part = gate_input[:, :, 0]
    input_part = gate_input[:, :, 1].reshape(requests, heads_here * head_width)
    step_raw = jnp.dot(normed, in_step, preferred_element_type=jnp.float32)
    conv_out = conv_step(conv_input, input_part, taps_input).reshape(
        requests, heads_here, head_width
    )
    step_size = jax.nn.softplus(step_raw + step_bias)
    decay = jnp.exp(-decay_rate * step_size)
    new_state = (
        decay[:, :, None, None] * ssm_state
        + (step_size[:, :, None] * conv_out)[:, :, :, None] * inject_heads[:, :, None, :]
    )
    ssm_out = (
        jnp.sum(new_state * readout_heads[:, :, None, :], axis=-1)
        + skip_gain[None, :, None] * conv_out
    )
    gated = ssm_out * jax.nn.silu(gate_part)
    head_squares = jnp.sum(gated * gated, axis=-1)
    weighted = (gated * norm_gain.reshape(heads_here, head_width)).astype(jnp.bfloat16)
    products = jnp.einsum(
        "rhp,hpd->hrd",
        weighted,
        out_mixer.reshape(heads_here, head_width, width),
        preferred_element_type=jnp.float32,
    ).astype(jnp.bfloat16)
    products = products.reshape(heads_here, requests, count_seq, columns).transpose(2, 0, 1, 3)
    marks = jnp.stack(split(head_squares.T, 2), axis=-1)
    marks = jnp.pad(marks, ((0, 0), (0, 0), (0, LANES - 2)))
    marks = jnp.broadcast_to(marks[None], (count_seq,) + marks.shape)
    received = lax.all_to_all(jnp.concatenate([products, marks], axis=-1), "seq", 0, 0)
    received = received.astype(jnp.float32)
    squares = (received[..., columns] + received[..., columns + 1]).reshape(
        per_group, GROUPS, requests
    )
    scales = lax.rsqrt(jnp.sum(squares, axis=0) / (per_group * head_width) + epsilon)
    mixer = jnp.sum(
        received[..., :columns].reshape(per_group, GROUPS, requests, columns)
        * scales[None, :, :, None],
        axis=(0, 1),
    )
    stream_cols = lax.dynamic_slice_in_dim(stream, position * columns, columns, 1)
    middle = (stream_cols + mixer).astype(jnp.bfloat16)
    middle_f = middle.astype(jnp.float32)
    scaled = (middle_f * attn_gain).astype(jnp.bfloat16)
    partial_sq = jnp.sum(middle_f * middle_f, axis=-1)
    pages_here = kv_cache.shape[0]
    page_len = kv_cache.shape[1]
    pages_req = page_table.shape[1]
    pages_all = pages_here * count_seq
    matches = page_table[None, :, :] == jnp.arange(pages_all, dtype=jnp.int32)[:, None, None]
    owner = jnp.any(matches, axis=2)
    page_rows = jnp.dot(
        owner.astype(jnp.bfloat16), scaled, preferred_element_type=jnp.float32
    ).astype(jnp.bfloat16)
    page_proj = jnp.dot(page_rows, w_qkv, preferred_element_type=jnp.float32).astype(jnp.bfloat16)
    page_sq = jnp.sum(jnp.where(owner, partial_sq[None, :], 0.0), axis=1)
    sq_parts = jnp.pad(jnp.stack(split(page_sq, 2), axis=-1), ((0, 0), (0, LANES - 2)))
    sent = jnp.concatenate([page_proj, sq_parts], axis=-1).reshape(count_seq, pages_here, -1)
    arrived = jnp.sum(lax.all_to_all(sent, "seq", 0, 0).astype(jnp.float32), axis=0)
    qkv_width = w_qkv.shape[1]
    total_sq = arrived[:, qkv_width] + arrived[:, qkv_width + 1]
    qkv = (arrived[:, :qkv_width] * lax.rsqrt(total_sq / width + epsilon)[:, None]).astype(
        jnp.bfloat16
    )
    group_size = QH // KVH
    queries = qkv[:, : QH * HD].reshape(pages_here, KVH, group_size, HD)
    fresh_kv = qkv[:, QH * HD :]
    fresh_keys = fresh_kv[:, : KVH * HD].reshape(pages_here, KVH, 1, HD).astype(jnp.float32)
    fresh_values = fresh_kv[:, KVH * HD :].reshape(pages_here, KVH, 1, HD).astype(jnp.float32)
    scale = 1.0 / HD**0.5
    slots = position * pages_here + jnp.arange(pages_here, dtype=jnp.int32)
    own_matches = page_table[None, :, :] == slots[:, None, None]
    logical = jnp.sum(
        jnp.any(own_matches, axis=1) * jnp.arange(pages_req, dtype=jnp.int32)[None, :], axis=1
    )
    page_length = jnp.sum(jnp.where(jnp.any(own_matches, axis=2), lengths[None, :], 0), axis=1)
    token_pos = logical[:, None] * page_len + jnp.arange(page_len, dtype=jnp.int32)[None, :]
    live = (token_pos < page_length[:, None])[:, None, None, :]
    leads = (logical == 0)[:, None, None]
    cached = kv_cache.reshape(pages_here, page_len, 2, KVH, HD)
    scores = (
        jnp.einsum("pgjd,ptgd->pgjt", queries, cached[:, :, 0], preferred_element_type=jnp.float32)
        * scale
    )
    own = jnp.sum(queries.astype(jnp.float32) * fresh_keys, axis=-1) * scale
    masked = jnp.where(live, scores, lowest)
    own = jnp.where(leads, own, lowest)
    peak = jnp.maximum(jnp.max(masked, axis=-1), own)
    weights = jnp.where(live, jnp.exp(masked - peak[..., None]), 0.0)
    own_weight = jnp.where(leads, jnp.exp(own - peak), 0.0)
    total = jnp.sum(weights, axis=-1) + own_weight
    values = jnp.einsum(
        "pgjt,ptgd->pgjd",
        weights.astype(jnp.bfloat16),
        cached[:, :, 1],
        preferred_element_type=jnp.float32,
    )
    values = values + own_weight[..., None] * fresh_values
    some = total > 0.0
    safe = jnp.where(some, total, 1.0)
    values = (values / safe[..., None]).astype(jnp.bfloat16)
    logsum = jnp.where(some, peak + jnp.log(safe), lowest)
    logs = jnp.concatenate(split(logsum.reshape(1, pages_here * QH), 3), axis=0)
    logs = jnp.pad(logs, ((0, 5), (0, LANES - pages_here * QH)))
    value_rows = pages_here * QH
    kv_rows = pages_here * 2 * KVH
    package = jnp.concatenate(
        [values.reshape(value_rows, HD), fresh_kv.reshape(kv_rows, HD), logs], axis=0
    )
    package = jnp.broadcast_to(package[None], (count_seq,) + package.shape)
    everything = lax.all_to_all(package, "seq", 0, 0)
    all_values = everything[:, :value_rows].reshape(pages_all, QH, HD)
    all_kv = everything[:, value_rows : value_rows + kv_rows].reshape(pages_all, 2 * KVH * HD)
    all_logs = everything[:, value_rows + kv_rows :, : pages_here * QH].astype(jnp.float32)
    all_logs = (all_logs[:, 0] + all_logs[:, 1] + all_logs[:, 2]).reshape(pages_all, QH)
    new_kv = all_kv[page_table[:, 0]]
    req_logs = all_logs[page_table]
    top = jnp.max(req_logs, axis=1, keepdims=True)
    factors = jnp.exp(req_logs - top)
    summed = jnp.sum(factors[..., None] * all_values[page_table].astype(jnp.float32), axis=1)
    attended = (summed / jnp.sum(factors, axis=1)[..., None]).astype(jnp.bfloat16)
    final = (
        middle_f
        + jnp.dot(
            attended.reshape(requests, QH * HD), w_out, preferred_element_type=jnp.float32
        )
    ).astype(jnp.bfloat16)
    return (final, new_state, new_kv)


def solution(mesh):
    placed = (
        P("grp", None),
        P(),
        P(None, "seq"),
        P(None, "seq"),
        P(None, "seq"),
        P("grp", None, "seq"),
        P("grp", None, "seq"),
        P(None, "seq"),
        P(None, "seq"),
        P("seq"),
        P("seq"),
        P("seq"),
        P("seq"),
        P("seq", None),
        P("grp", "seq", None, None),
        P("seq"),
        P("seq", None),
        P(None, "seq"),
        P(("grp", "seq"), None, None),
        P("grp", None),
        P("grp"),
    )
    return jax.shard_map(
        shards,
        mesh=mesh,
        in_specs=placed,
        out_specs=(P("grp", "seq"), P("grp", "seq", None, None), P("grp", None)),
        check_vma=False,
    )
```

time: 284 us -> 93.7 us (0.33)
  blocking collectives: 107 us -> 0 us
  waiting for transfers between devices: 112 us -> 24.6 us
  starting transfers between devices: 0.12 us -> 15.9 us
  between operations: 15.9 us -> 2.94 us
  local copies, waits for them, and re-layouts: 7.37 us -> 17.5 us
  other arithmetic: 23.6 us -> 19.1 us
    all_gather x4 -> x0, blocking collectives: 77.9 us -> none  [the longest x2 37.3 us: merged(): lax.all_gather(part.astype(kind), axis)]
    psum x1 -> x0, waiting for transfers between devices: 61.6 us -> none  [shards(): projected, total_sq = lax.psum((partial_proj, partial_sq), 'seq')]
    reduce_scatter x1 -> x0, waiting for transfers between devices: 50.7 us -> none  [shards(): mixer = lax.psum_scatter(mixer_term, 'seq', scatter_dimension=1, tiled=True)]
    psum x1 -> x0, blocking collectives: 29.5 us -> none  [shards(): projected, total_sq = lax.psum((partial_proj, partial_sq), 'seq')]
    all_to_all x0 -> x3, waiting for transfers between devices: none -> 24.6 us  [the longest x1 11.9 us: shards(): everything = lax.all_to_all(package, 'seq', 0, 0)]
    add x32 -> x2, other arithmetic: 16.4 us -> 0.12 us  [the longest x1 0.08 us: shards(): received[..., columns] + received[..., columns + 1]]
    all_to_all x0 -> x3, starting transfers between devices: none -> 11.8 us  [the longest x1 4.21 us: shards(): everything = lax.all_to_all(package, 'seq', 0, 0)]
    reduce_sum x5 -> x11, other arithmetic: 0.53 us -> 5.47 us  [the longest x1 1.8 us: shards(): jnp.sum(new_state * readout_heads[:, :, None, :], axis=-1)]
  transfers between devices with their start and end apart: 3 -> 4, of which waited for: 2 -> 3; matrix products, arithmetic and copies ran while one was open for 2% -> 16% of each run, Pallas kernels for 0% -> 0%
where the time goes in v1:
time: 93.7 us; the launch traced here: 92.4 us
  waiting for transfers between devices  24.6 us (26%)
  other arithmetic  19.1 us (20%)
  local copies, waits for them, and re-layouts  17.5 us (19%)
  starting transfers between devices  15.9 us (17%)
  matrix products  12.4 us (13%)
  between operations  2.94 us (3%)
    all_to_all x1, waiting for transfers between devices, shards(): everything = lax.all_to_all(package, 'seq', 0, 0)  11.9 us
    all_to_all x1, waiting for transfers between devices, shards(): lax.all_to_all(jnp.concatenate([products, marks], axis=-1), 'seq', 0, 0)  6.67 us
    all_to_all x1, waiting for transfers between devices, shards(): lax.all_to_all(sent, 'seq', 0, 0).astype(jnp.float32)  6.01 us
    all_to_all x1, starting transfers between devices, shards(): everything = lax.all_to_all(package, 'seq', 0, 0)  4.21 us
    ppermute x1, starting transfers between devices, group_vectors(): other = lax.ppermute(group_conv, 'seq', swap)  4.13 us
    all_to_all x1, starting transfers between devices, shards(): lax.all_to_all(jnp.concatenate([products, marks], axis=-1), 'seq', 0, 0)  3.88 us
    all_to_all x1, starting transfers between devices, shards(): lax.all_to_all(sent, 'seq', 0, 0).astype(jnp.float32)  3.68 us
    unnamed x18, local copies, waits for them, and re-layouts  3.28 us
  transfers between devices with their start and end apart: 4, of which 3 were waited for; matrix products, arithmetic and copies ran while one was open for 16% of the time, Pallas kernels for 0%

profile of v1, /device:TPU:0, one launch (start us, length us, event | category | flops | bytes accessed | tf_op | source)
XLA Modules:
  0.0 92.4 jit_solution(14956873482904575970)
XLA Ops:
  0.7 0.8 slice_bitcast_fusion.4
  1.5 0.8 slice.80
  2.3 1.0 %multiply_reduce_fusion.1 = f32[8]{0:T(128)S(1)} fusion(bf16[8,4096]{1,0:T(8,128)(2,1)} %param.21), kind=kLoop, calls=%fused_computation.30 | loop fusion | flops 98296 | bytes 65568 | tf_op jit(solution)/shard_map/reduce_sum | solution.py:87
  4.0 1.6 %convolution_bitcast_fusion = f32[8,1,128]{2,0,1:T(8,128)S(1)} fusion(bf16[4096,128]{1,0:T(8,128)(2,1)} %param.25, f32[4096]{0:T(1024)} %param.22, f32[8]{0:T(128)S(1)} %add_rsqrt_fusion.1, bf16[8,4096]{1,0:T(8,128)(2,1)} %param.21), kind=kOutput, calls=%fused_computation.13 | convolution fusion | flops 8519680 | bytes 1134624 | tf_op jit(solution)/shard_map/dot_general | solution.py:89
  5.6 4.1 %collective-permute-start = (bf16[8,128]{1,0:T(8,128)(2,1)S(1)}, bf16[8,128]{1,0:T(8,128)(2,1)S(1)}, u32[]{:S(2)}, u32[]{:S(2)}) collective-permute-start(bf16[8,128]{1,0:T(8,128)(2,1)S(1)} %multiply_convert_fusion.1), channel_id=1, source_target_pairs={{0,8},{1,9},{2,10},{3,11},{4,12},{5,13},{6,14},{7,15},{8,0},{9,1},... | collective-permute-start | bytes 6152 | tf_op jit(solution)/shard_map/ppermute | solution.py:38
  12.5 1.6 %fusion.65 = f32[8,128]{1,0:T(8,128)S(1)} fusion(bf16[4096,128]{1,0:T(8,128)(2,1)} %param.23, f32[4096]{0:T(1024)} %param.22, f32[8]{0:T(128)S(1)} %add_rsqrt_fusion.1, bf16[8,4096]{1,0:T(8,128)(2,1)} %param.21), kind=kOutput, calls=%fused_computation.149 | convolution fusion | flops 8519680 | bytes 1134624 | tf_op jit(solution)/shard_map/dot_general | solution.py:92
  14.8 1.1 %multiply_exponential_fusion = (f32[8]{0:T(128)S(1)}, f32[8]{0:T(128)S(1)}) fusion(f32[]{:T(128)} %bitcast, f32[]{:T(128)} %bitcast.101, bf16[4096,1]{0,1:T(2,128)(2,1)} %param.24, f32[4096]{0:T(1024)} %param.22, f32[8]{0:T(128)S(1)} %add_rsqrt_fusion.1, bf16[8,4096]{1,0:T(8,128)(2,1)} %param.21), kind=kOutput, calls=%fused_computation.143 | convolution fusion | flops 196672 | bytes 90216 | tf_op jit(solution)/shard_map/dot_general | solution.py:97
  16.0 1.5 %compare_reduce_fusion.1 = (pred[2,4]{1,0:T(4,128)(4,1)S(1)}, pred[2,8]{1,0:T(4,128)(4,1)}) fusion(s32[8,4]{0,1:T(4,128)} %param.40, s32[2]{0:T(128)S(1)} %iota_add_fusion), kind=kLoop, calls=%fused_computation.76 | loop fusion | flops 168 | bytes 160 | tf_op jit(solution)/shard_map/reduce_or | solution.py:168
  17.5 1.5 %convert_element_type.190 = f32[8,4096]{1,0:T(8,128)} convert(bf16[8,4096]{1,0:T(8,128)(2,1)} %param.21) | non-fusion elementwise | flops 32768 | bytes 196608 | tf_op jit(solution)/shard_map/convert_element_type | solution.py:85
  19.6 1.8 %multiply_reduce_fusion = (f32[8,64]{1,0:T(8,128)S(1)}, f32[8,1,64,128]{3,2,1,0:T(8,128)}) fusion(f32[8,128]{1,0:T(8,128)S(1)} %get-tuple-element.21, f32[8,128]{1,0:T(8,128)S(1)} %get-tuple-element.20, f32[8,64]{1,0:T(8,128)S(1)} %broadcast_multiply_fusion.1, f32[8,1,64,128]{3,2,1,0:T(8,128)} %param.35, f32[8]{0:T(128)S(1)} %get-tuple-element.28), kind=kLoop, calls=%fused_computation.24 | loop fusion | flops 327168 | bytes 536608 | tf_op jit(solution)/shard_map/reduce_sum | solution.py:108
  21.7 1.3 %convolution_convert_fusion.1 = bf16[8,4096]{1,0:T(8,128)(2,1)S(1)} fusion(bf16[64,4096]{1,0:T(8,128)(2,1)} %param.34, f32[8,64]{1,0:T(8,128)S(1)} %get-tuple-element.13, f32[8,1,1,64]{3,0,2,1:T(8,128)S(1)} %bitcast.111, f32[8,64]{1,0:T(8,128)S(1)} %fusion.20, f32[64]{0:T(128)S(1)} %copy-done.7, f32[64]{0:T(128)S(1)} %slice_bitcast_fusion.5, f32[]{:T(128)} %bitcast.102), kind=kOutput, calls=%fused_computation.4 | convolution fusion | flops 4234240 | bytes 596484 | tf_op jit(solution)/shard_map/rhp,hpd->hrd/dot_general | solution.py:114
  23.6 3.9 %all-to-all-start = ((bf16[16,1,8,384]{3,2,1,0:T(8,128)(2,1)}), bf16[16,1,8,384]{3,2,1,0:T(8,128)(2,1)S(1)}, u32[]{:S(2)}, u32[]{:S(2)}) async-start(bf16[16,1,8,384]{3,2,1,0:T(8,128)(2,1)} %pad_maximum_fusion), calls=%async_computation | async-start | bytes 196608 | tf_op jit(solution)/shard_map/all_to_all | solution.py:124
  28.2 6.7 %all-to-all-done = bf16[16,1,8,384]{3,2,1,0:T(8,128)(2,1)S(1)} async-done(((bf16[16,1,8,384]{3,2,1,0:T(8,128)(2,1)}), bf16[16,1,8,384]{3,2,1,0:T(8,128)(2,1)S(1)}, u32[]{:S(2)}, u32[]{:S(2)}) %all-to-all-start) | async-done | bytes 98336 | tf_op jit(solution)/shard_map/all_to_all | solution.py:124
  35.4 0.8 fusion.27
  36.8 1.6 %convolution_convert_fusion = bf16[32,6144]{1,0:T(8,128)(2,1)} fusion(bf16[256,6144]{1,0:T(8,128)(2,1)S(1)} %copy-done, pred[32,8]{0,1:T(8,128)(4,1)S(1)} %fusion.24, bf16[8,256]{1,0:T(8,128)(2,1)S(1)} %get-tuple-element.12, f32[256]{0:T(256)S(1)} %copy-done.6), kind=kOutput, calls=%fused_computation.3 | convolution fusion | flops 101005312 | bytes 3544320 | tf_op jit(solution)/shard_map/dot_general | solution.py:149
  38.3 1.0 %fusion.7 = bf16[32,6272]{1,0:T(8,128)(2,1)S(1)} fusion(bf16[32,2]{1,0:T(8,128)(2,1)S(1)} %copy.86, bf16[32,6144]{1,0:T(8,128)(2,1)} %convolution_convert_fusion), kind=kLoop, calls=%fused_computation.23 | loop fusion | flops 1204224 | bytes 794752 | tf_op jit(solution)/shard_map/concatenate | solution.py:152
  39.4 0.9 reshape.589
  40.3 3.7 %all-to-all-start.1 = ((bf16[16,2,6272]{2,1,0:T(2,128)(2,1)}), bf16[16,2,6272]{2,1,0:T(2,128)(2,1)S(1)}, u32[]{:S(2)}, u32[]{:S(2)}) async-start(bf16[16,2,6272]{2,1,0:T(2,128)(2,1)} %reshape.589), calls=%async_computation.1 | async-start | bytes 802816 | tf_op jit(solution)/shard_map/all_to_all | solution.py:153
  45.9 2.3 %copy.87 = bf16[2,128,2048]{1,2,0:T(8,128)(2,1)} copy(bf16[2,128,2048]{2,1,0:T(8,128)(2,1)} %param.39) | data formatting | bytes 2097152 | tf_op args[18]
  50.2 6.0 %all-to-all-done.1 = bf16[16,2,6272]{2,1,0:T(2,128)(2,1)S(1)} async-done(((bf16[16,2,6272]{2,1,0:T(2,128)(2,1)}), bf16[16,2,6272]{2,1,0:T(2,128)(2,1)S(1)}, u32[]{:S(2)}, u32[]{:S(2)}) %all-to-all-start.1) | async-done | bytes 401440 | tf_op jit(solution)/shard_map/all_to_all | solution.py:153
  57.0 1.4 %fusion.68 = (f32[2,8,4]{2,1,0:T(8,128)S(1)}, f32[2,8,4,128]{3,2,1,0:T(4,128)S(1)}) fusion(bf16[2,8,4,128]{3,2,1,0:T(4,128)(2,1)S(1)} %reshape.590, bf16[2,128,2,8,128]{1,4,3,2,0:T(8,128)(2,1)} %bitcast.104, pred[2,128]{1,0:T(4,128)(4,1)} %add_compare_fusion), kind=kOutput, calls=%fused_computation.152 | convolution fusion | flops 2121664 | bytes 574208 | tf_op jit(solution)/shard_map/pgjd,ptgd->pgjt/dot_general | solution.py:176
  58.6 0.8 fusion.17
  60.4 1.5 %fusion.2 = bf16[2,8,4,128]{3,2,1,0:T(4,128)(2,1)S(1)} fusion(bf16[2,128,2,8,128]{1,4,3,2,0:T(8,128)(2,1)} %bitcast.105, f32[2,8,4,128]{3,2,1,0:T(4,128)S(1)} %get-tuple-element.31, f32[2,8,4]{2,1,0:T(8,128)S(1)} %get-tuple-element.7, f32[2,8,128]{2,1,0:T(8,128)S(1)} %get-tuple-element.32, f32[2,8,4]{2,1,0:T(8,128)S(1)} %get-tuple-element.8, ...), kind=kOutput, calls=%fused_computation.10 | convolution fusion | flops 2154496 | bytes 582912 | tf_op jit(solution)/shard_map/pgjt,ptgd->pgjd/dot_general | solution.py:186
  61.9 0.8 broadcast_in_dim.144
  62.7 4.2 %all-to-all-start.2 = ((bf16[16,104,128]{2,1,0:T(8,128)(2,1)}), bf16[16,104,128]{2,1,0:T(8,128)(2,1)}, u32[]{:S(2)}, u32[]{:S(2)}) async-start(bf16[16,104,128]{2,1,0:T(8,128)(2,1)} %broadcast_in_dim.144), calls=%async_computation.2 | async-start | bytes 851968 | tf_op jit(solution)/shard_map/all_to_all | solution.py:205
  67.8 11.9 %all-to-all-done.2 = bf16[16,104,128]{2,1,0:T(8,128)(2,1)} async-done(((bf16[16,104,128]{2,1,0:T(8,128)(2,1)}), bf16[16,104,128]{2,1,0:T(8,128)(2,1)}, u32[]{:S(2)}, u32[]{:S(2)}) %all-to-all-start.2) | async-done | bytes 426016 | tf_op jit(solution)/shard_map/all_to_all | solution.py:205
  81.8 1.7 %slice.126 = bf16[16,64,128]{2,1,0:T(8,128)(2,1)} slice(bf16[16,104,128]{2,1,0:T(8,128)(2,1)} %all-to-all-done.2), slice={[0:16], [0:64], [0:128]} | slice | bytes 524288 | tf_op jit(solution)/shard_map/slice | solution.py:206
  83.4 1.5 %gather_fusion.1 = bf16[32,32,128]{2,1,0:T(8,128)(2,1)S(1)} fusion(bf16[32,32,128]{2,1,0:T(8,128)(2,1)} %bitcast.106, s32[1024]{0:T(1024)S(1)} %pad_clamp_fusion.1), kind=kCustom, calls=%fused_computation.1 | custom fusion | bytes 524416 | tf_op jit(solution)/shard_map/gather | solution.py:214
  85.0 1.6 %slice.127 = bf16[16,32,128]{2,1,0:T(8,128)(2,1)} slice(bf16[16,104,128]{2,1,0:T(8,128)(2,1)} %all-to-all-done.2), slice={[0:16], [64:96], [0:128]} | slice | bytes 262144 | tf_op jit(solution)/shard_map/slice | solution.py:207
  86.5 1.0 %reshape.595 = bf16[32,2048]{1,0:T(8,128)(2,1)S(1)} reshape(bf16[16,32,128]{2,1,0:T(8,128)(2,1)} %slice.127) | data formatting | bytes 262144 | tf_op jit(solution)/shard_map/reshape | solution.py:207
  88.5 2.6 %fusion.3 = bf16[8,256]{1,0:T(8,128)(2,1)} fusion(bf16[4096,256]{1,0:T(8,128)(2,1)} %param.38, bf16[1,8,32,128]{3,2,1,0:T(8,128)(2,1)S(1)} %fusion.13, bf16[8,256]{1,0:T(8,128)(2,1)} %copy-done.1), kind=kOutput, calls=%fused_computation.12 | convolution fusion | flops 16783360 | bytes 2170880 | tf_op jit(solution)/shard_map/dot_general | solution.py:218
  91.1 1.3 %gather_fusion.2 = bf16[8,2048]{1,0:T(8,128)(2,1)} fusion(bf16[32,2048]{1,0:T(8,128)(2,1)S(1)} %reshape.595, s32[1024]{0:T(1024)} %pad_clamp_fusion), kind=kCustom, calls=%fused_computation.2 | custom fusion | bytes 65568 | tf_op jit(solution)/shard_map/gather | solution.py:210
  (90 shorter events, 15.4 us)
Async XLA Ops:
  0.6 36.2 %copy-start = (bf16[256,6144]{1,0:T(8,128)(2,1)S(1)}, bf16[256,6144]{1,0:T(8,128)(2,1)}, u32[]{:S(2)}) copy-start(bf16[256,6144]{1,0:T(8,128)(2,1)} %param.37) | copy-start | bytes 9437188
  0.6 27.5 %copy-start.2 = (s32[8,4]{0,1:T(4,128)S(1)}, s32[8,4]{0,1:T(4,128)}, u32[]{:S(2)}) copy-start(s32[8,4]{0,1:T(4,128)} %param.40) | copy-start | bytes 388
  0.7 21.0 %copy-start.7 = (f32[64]{0:T(128)S(1)}, f32[64]{0:T(128)}, u32[]{:S(2)}) copy-start(f32[64]{0:T(128)} %param.33) | copy-start | bytes 772
  0.7 36.1 %copy-start.6 = (f32[256]{0:T(256)S(1)}, f32[256]{0:T(256)}, u32[]{:S(2)}) copy-start(f32[256]{0:T(256)} %param.36) | copy-start | bytes 3076
  5.6 14.0 %collective-permute-start = (bf16[8,128]{1,0:T(8,128)(2,1)S(1)}, bf16[8,128]{1,0:T(8,128)(2,1)S(1)}, u32[]{:S(2)}, u32[]{:S(2)}) collective-permute-start(bf16[8,128]{1,0:T(8,128)(2,1)S(1)} %multiply_convert_fusion.1), channel_id=1, source_target_pairs={{0,8},{1,9},{2,10},{3,11},{4,12},{5,13},{6,14},{7,15},{8,0},{9,1},... | collective-permute-start | bytes 6152 | tf_op jit(solution)/shard_map/ppermute | solution.py:38
  23.6 11.3 %all-to-all-start = ((bf16[16,1,8,384]{3,2,1,0:T(8,128)(2,1)}), bf16[16,1,8,384]{3,2,1,0:T(8,128)(2,1)S(1)}, u32[]{:S(2)}, u32[]{:S(2)}) async-start(bf16[16,1,8,384]{3,2,1,0:T(8,128)(2,1)} %pad_maximum_fusion), calls=%async_computation | async-start | bytes 196608 | tf_op jit(solution)/shard_map/all_to_all | solution.py:124
  36.2 0.6 copy-start.1
  40.3 26.7 %copy-start.3 = (s32[8,4]{0,1:T(4,128)S(1)}, s32[8,4]{0,1:T(4,128)}, u32[]{:S(2)}) copy-start(s32[8,4]{0,1:T(4,128)} %param.40) | copy-start | bytes 388
  40.3 16.0 %all-to-all-start.1 = ((bf16[16,2,6272]{2,1,0:T(2,128)(2,1)}), bf16[16,2,6272]{2,1,0:T(2,128)(2,1)S(1)}, u32[]{:S(2)}, u32[]{:S(2)}) async-start(bf16[16,2,6272]{2,1,0:T(2,128)(2,1)} %reshape.589), calls=%async_computation.1 | async-start | bytes 802816 | tf_op jit(solution)/shard_map/all_to_all | solution.py:153
  44.6 0.5 copy-start.4
  45.9 12.6 %copy-start.5 = (pred[2]{0:T(512)(128)(4,1)S(1)}, pred[2]{0:T(512)(128)(4,1)}, u32[]{:S(2)}) copy-start(pred[2]{0:T(512)(128)(4,1)} %copy-done.4) | copy-start | bytes 10
  62.7 16.9 %all-to-all-start.2 = ((bf16[16,104,128]{2,1,0:T(8,128)(2,1)}), bf16[16,104,128]{2,1,0:T(8,128)(2,1)}, u32[]{:S(2)}, u32[]{:S(2)}) async-start(bf16[16,104,128]{2,1,0:T(8,128)(2,1)} %broadcast_in_dim.144), calls=%async_computation.2 | async-start | bytes 851968 | tf_op jit(solution)/shard_map/all_to_all | solution.py:205

commit v2 on v1

--- a/solution.py
+++ b/solution.py
@@ -1,6 +1,10 @@
+import functools
+
 import jax
 import jax.numpy as jnp
 from jax import lax
+from jax.experimental import pallas as pl
+from jax.experimental.pallas import tpu as pltpu
 from jax.sharding import PartitionSpec as P
 
 QH = 32
@@ -50,7 +54,7 @@
     return inject[:, head_ids % GROUPS], readout[:, head_ids % GROUPS]
 
 
-def shards(
+def plain_shards(
     hidden,
     mix_gain,
     in_gate_input,
@@ -222,6 +226,449 @@
     return (final, new_state, new_kv)
 
 
+f32 = jnp.float32
+bf16 = jnp.bfloat16
+SUB = 8
+PARTS = 3
+VMEM = pl.BlockSpec(memory_space=pltpu.VMEM)
+SMEM = pl.BlockSpec(memory_space=pltpu.SMEM)
+
+
+def call(kernel, outs, specs, scratch=()):
+    return pl.pallas_call(
+        kernel,
+        out_shape=outs,
+        in_specs=specs,
+        out_specs=jax.tree.map(lambda _: VMEM, outs),
+        scratch_shapes=scratch,
+    )
+
+
+def shape(dims, kind):
+    return jax.ShapeDtypeStruct(dims, kind)
+
+
+def silu(x):
+    return x * jax.nn.sigmoid(x)
+
+
+def pieces(value, parts):
+    out = []
+    for _ in range(parts):
+        piece = value.astype(bf16).astype(f32)
+        out.append(piece)
+        value = value - piece
+    return out
+
+
+def marked(value, parts):
+    lane = lax.broadcasted_iota(jnp.int32, (value.shape[0], LANES), 1)
+    out = jnp.zeros((value.shape[0], LANES), f32)
+    for k, piece in enumerate(pieces(value, parts)):
+        out = jnp.where(lane == k, piece, out)
+    return out
+
+
+def convolve(state_ref, fresh, taps_ref):
+    taps = state_ref.shape[0]
+    total = taps_ref[taps : taps + 1, :] * fresh + taps_ref[taps + 1 : taps + 2, :]
+    for k in range(taps):
+        total = total + taps_ref[k : k + 1, :] * state_ref[k].astype(f32)
+    return silu(total)
+
+
+def group_kernel(hidden, gain, weights, state, taps, group_out, normed_out):
+    stream = hidden[...].astype(f32)
+    mean = jnp.mean(stream * stream, axis=-1, keepdims=True)
+    normed = (stream * lax.rsqrt(mean + epsilon) * gain[...]).astype(bf16)
+    normed_out[...] = normed
+    raw = jnp.dot(normed, weights[...], preferred_element_type=f32)
+    group_out[...] = convolve(state, raw, taps).astype(bf16)
+
+
+def gate_kernel(
+    normed_ref, weights, step_row, state, taps, rate, bias, gate_out, conv_out, step_out, decay_out
+):
+    normed = normed_ref[...]
+    both = jnp.dot(normed, weights[...], preferred_element_type=f32)
+    half = both.shape[1] // 2
+    gate_out[...] = silu(both[:, :half])
+    conv_out[...] = convolve(state, both[:, half:], taps)
+    raw = jnp.sum(
+        normed.astype(f32) * step_row[...].astype(f32), axis=-1, keepdims=True
+    )
+    step = jax.nn.softplus(raw + bias[0])
+    step_out[...] = jnp.broadcast_to(step, step_out.shape)
+    decay_out[...] = jnp.broadcast_to(jnp.exp(-rate[0] * step), decay_out.shape)
+
+
+def chosen(position, own, other):
+    first = position[0] < GROUPS
+    mine, theirs = own[...].astype(f32), other[...].astype(f32)
+    return jnp.where(first, mine, theirs), jnp.where(first, theirs, mine)
+
+
+def mixer_kernel(
+    position, skip, own, other, gate, conv, step, decay, state, weights, gain, sent
+):
+    requests = own.shape[0]
+    inject, readout = chosen(position, own, other)
+    row = lax.broadcasted_iota(jnp.int32, conv.shape, 0)
+    read = jnp.zeros(conv.shape, f32)
+    for r in range(requests):
+        part = lax.dot_general(
+            readout,
+            state[r],
+            (((1,), (1,)), ((), ())),
+            precision=lax.Precision.HIGHEST,
+            preferred_element_type=f32,
+        )
+        read = jnp.where(row == r, part, read)
+    along = jnp.sum(inject * readout, axis=-1, keepdims=True)
+    fresh = conv[...]
+    out = (
+        decay[:, :1] * read
+        + step[:, :1] * fresh * along
+        + skip[0] * fresh
+    )
+    gated = out * gate[...]
+    marks = marked(jnp.sum(gated * gated, axis=-1, keepdims=True), 2).astype(bf16)
+    weighted = (gated * gain[...]).astype(bf16)
+    count = sent.shape[0]
+    columns = weights.shape[1] // count
+    for e in range(count):
+        product = jnp.dot(
+            weighted, weights[:, e * columns : (e + 1) * columns], preferred_element_type=f32
+        )
+        sent[e, :, :columns] = product.astype(bf16)
+        sent[e, :, columns:] = marks
+
+
+def state_kernel(position, own, other, conv, step, decay, state, new_state):
+    inject, _ = chosen(position, own, other)
+    fresh = step[:, :1] * conv[...]
+    new_state[...] = (
+        decay[:, :1][:, :, None] * state[...] + fresh[:, :, None] * inject[:, None, :]
+    )
+
+
+def project_kernel(
+    chunks, head_width, position, received, hidden, gain, weights, table, sent, middle_out
+):
+    count, requests, _ = received.shape
+    columns = weights.shape[0]
+    squares = [received[k, :, columns:].astype(f32) for k in range(count)]
+    mixer = jnp.zeros((requests, columns), f32)
+    for g in range(GROUPS):
+        members = range(g, count, GROUPS)
+        marks = sum(squares[k] for k in members)
+        total = marks[:, :1] + marks[:, 1:2]
+        scale = lax.rsqrt(total / (len(members) * head_width) + epsilon)
+        products = sum(received[k, :, :columns].astype(f32) for k in members)
+        mixer = mixer + scale * products
+    start = pl.multiple_of(position[0] * columns, columns)
+    middle = (hidden[:, pl.ds(start, columns)].astype(f32) + mixer).astype(bf16).astype(f32)
+    middle_out[...] = middle
+    marks = marked(jnp.sum(middle * middle, axis=-1, keepdims=True), 2)
+    extended = jnp.concatenate([middle * gain[...], marks], axis=-1).astype(bf16)
+    rows = count * SUB
+    pages = SUB // chunks
+    index = lax.broadcasted_iota(jnp.int32, (rows, requests), 0)
+    page = (index // SUB) * pages + index % pages
+    hits = page == table[0:1, :]
+    for j in range(1, table.shape[0]):
+        hits = jnp.logical_or(hits, page == table[j : j + 1, :])
+    onehot = jnp.where(hits, 1.0, 0.0).astype(bf16)
+    spread = jnp.dot(onehot, extended, preferred_element_type=f32)
+    lines = spread[:, :columns]
+    which = (lax.broadcasted_iota(jnp.int32, lines.shape, 0) % SUB) // pages
+    lhs = [jnp.where(which == c, lines, 0.0).astype(bf16) for c in range(chunks)]
+    chunk = weights.shape[1] // chunks
+    tile = 256
+    for n in range(0, chunk, tile):
+        total = None
+        for c in range(chunks):
+            part = jnp.dot(
+                lhs[c],
+                weights[:, c * chunk + n : c * chunk + n + tile],
+                preferred_element_type=f32,
+            )
+            total = part if total is None else total + part
+        for e in range(count):
+            sent[e, :, n : n + tile] = total[e * SUB : (e + 1) * SUB].astype(bf16)
+    for e in range(count):
+        sent[e, :, chunk:] = spread[e * SUB : (e + 1) * SUB, columns:].astype(bf16)
+
+
+def attend_kernel(width, position, received, cache, table, lengths, sent, lines):
+    count, _, full = received.shape
+    pages, page_len, _ = cache.shape
+    chunks = SUB // pages
+    chunk = full - LANES
+    tiles = chunk // HD
+    total = received[0].astype(f32)
+    for k in range(1, count):
+        total = total + received[k].astype(f32)
+    squares = total[:, chunk : chunk + 1] + total[:, chunk + 1 : chunk + 2]
+    inverse = lax.rsqrt(squares / width + epsilon)
+    for t in range(tiles):
+        lines[t * SUB : (t + 1) * SUB, :] = (
+            (total[:, t * HD : (t + 1) * HD] * inverse).astype(bf16).astype(f32)
+        )
+
+    def heads(page, first, many):
+        start = (first % tiles) * SUB + (first // tiles) * pages + page
+        return lines[pl.ds(start, many, stride=SUB), :]
+
+    group = QH // KVH
+    scale = 1.0 / HD**0.5
+    lane = lax.broadcasted_iota(jnp.int32, (1, page_len), 1)
+    head_group = lax.broadcasted_iota(jnp.int32, (QH, HD), 0) // group
+    eye = lax.broadcasted_iota(jnp.int32, (QH, LANES), 0)
+    eye_lane = lax.broadcasted_iota(jnp.int32, (QH, LANES), 1)
+    order = lax.broadcasted_iota(jnp.int32, table.shape, 0)
+    value_rows = pages * QH
+    fresh_rows = 2 * KVH
+    log_row = jnp.zeros((1, LANES), f32)
+    for p in range(pages):
+        slot = position[0] * pages + p
+        hit = table[...] == slot
+        logical = jnp.sum(jnp.where(hit, order, 0), axis=(0, 1), keepdims=True)
+        length = jnp.sum(
+            jnp.where(hit, jnp.broadcast_to(lengths[...], hit.shape), 0),
+            axis=(0, 1),
+            keepdims=True,
+        )
+        live = logical * page_len + lane < length
+        leads = logical == 0
+        query = jnp.concatenate([heads(p, g * group, group) for g in range(KVH)], axis=0)
+        keys = [heads(p, QH + g, 1) for g in range(KVH)]
+        values = [heads(p, QH + KVH + g, 1) for g in range(KVH)]
+        key_rows = jnp.concatenate([jnp.broadcast_to(k, (group, HD)) for k in keys], axis=0)
+        value_own = jnp.concatenate([jnp.broadcast_to(v, (group, HD)) for v in values], axis=0)
+        spread = jnp.concatenate(
+            [jnp.where(head_group == g, query, 0.0).astype(bf16) for g in range(KVH)], axis=-1
+        )
+        scores = (
+            lax.dot_general(
+                spread,
+                cache[p, :, : KVH * HD],
+                (((1,), (1,)), ((), ())),
+                preferred_element_type=f32,
+            )
+            * scale
+        )
+        own = jnp.sum(query * key_rows, axis=-1, keepdims=True) * scale
+        masked = jnp.where(live, scores, lowest)
+        own = jnp.where(leads, own, lowest)
+        peak = jnp.maximum(jnp.max(masked, axis=-1, keepdims=True), own)
+        weights = jnp.where(live, jnp.exp(masked - peak), 0.0)
+        own_weight = jnp.where(leads, jnp.exp(own - peak), 0.0)
+        mass = jnp.sum(weights, axis=-1, keepdims=True) + own_weight
+        wide = jnp.dot(
+            weights.astype(bf16), cache[p, :, KVH * HD :], preferred_element_type=f32
+        )
+        summed = own_weight * value_own
+        for g in range(KVH):
+            summed = summed + jnp.where(head_group == g, wide[:, g * HD : (g + 1) * HD], 0.0)
+        some = mass > 0.0
+        safe = jnp.where(some, mass, 1.0)
+        result = (summed / safe).astype(bf16)
+        logs = jnp.where(some, peak + jnp.log(safe), lowest)
+        log_row = log_row + jnp.sum(
+            jnp.where(eye_lane == eye + p * QH, logs, 0.0), axis=0, keepdims=True
+        )
+        fresh = jnp.concatenate(keys + values, axis=0).astype(bf16)
+        for e in range(count):
+            sent[e, p * QH : (p + 1) * QH, :] = result
+            first = value_rows + p * fresh_rows
+            sent[e, first : first + fresh_rows, :] = fresh
+    terms = pieces(log_row, PARTS) + [jnp.zeros((SUB - PARTS, LANES), f32)]
+    terms = jnp.concatenate(terms, axis=0).astype(bf16)
+    for e in range(count):
+        sent[e, value_rows + pages * fresh_rows :, :] = terms
+
+
+def merge_kernel(pages, table, received, weights, middle, final, new_kv, spread, rows, fresh):
+    count, package, _ = received.shape
+    requests, pages_req = table.shape
+    value_rows = pages * QH
+    kv_rows = 2 * KVH
+    last = value_rows + pages * kv_rows
+    logs = jnp.concatenate([received[k, last:, :] for k in range(count)], axis=0)
+    source = lax.broadcasted_iota(jnp.int32, (count * SUB, LANES), 0) // SUB
+    for k in range(count):
+        mask = jnp.where(source == k, 1.0, 0.0).astype(bf16)
+        spread[k] = lax.dot_general(
+            logs, mask, (((0,), (0,)), ((), ())), preferred_element_type=f32
+        )
+    for r in range(requests):
+        peaks, values = [], []
+        for j in range(pages_req):
+            page = table[r, j]
+            device, slot = page // pages, page % pages
+            first = pl.multiple_of(slot * QH, QH)
+            peaks.append(spread[device, pl.ds(first, QH), :])
+            values.append(received[device, pl.ds(first, QH), :].astype(f32))
+        top = functools.reduce(jnp.maximum, peaks)
+        mass = jnp.zeros(top.shape, f32)
+        summed = jnp.zeros(top.shape, f32)
+        for peak, value in zip(peaks, values):
+            factor = jnp.exp(peak - top)
+            mass = mass + factor
+            summed = summed + factor * value
+        rows[r * QH : (r + 1) * QH, :] = summed / mass
+        page = table[r, 0]
+        first = pl.multiple_of(value_rows + (page % pages) * kv_rows, kv_rows)
+        fresh[r * kv_rows : (r + 1) * kv_rows, :] = received[
+            page // pages, pl.ds(first, kv_rows), :
+        ].astype(f32)
+    for c in range(kv_rows):
+        new_kv[:, c * HD : (c + 1) * HD] = fresh[pl.ds(c, requests, stride=kv_rows), :].astype(
+            bf16
+        )
+    attended = jnp.concatenate(
+        [rows[pl.ds(h, requests, stride=QH), :].astype(bf16) for h in range(QH)], axis=-1
+    )
+    total = jnp.dot(attended, weights[...], preferred_element_type=f32)
+    final[...] = (middle[...] + total).astype(bf16)
+
+
+def fused_shards(
+    hidden,
+    mix_gain,
+    in_gate_input,
+    in_step,
+    in_groups,
+    conv_input,
+    conv_groups,
+    taps_input,
+    taps_groups,
+    decay_rate,
+    step_bias,
+    skip_gain,
+    norm_gain,
+    out_mixer,
+    ssm_state,
+    attn_gain,
+    w_qkv,
+    w_out,
+    kv_cache,
+    page_table,
+    lengths,
+):
+    count = lax.axis_size("seq")
+    position = lax.axis_index("seq").astype(jnp.int32).reshape(1)
+    requests, width = hidden.shape
+    columns = width // count
+    head_width = in_gate_input.shape[1] // 2
+    pages = kv_cache.shape[0]
+    chunks = SUB // pages
+    gcols = in_groups.shape[1]
+    group_conv, normed = call(
+        group_kernel,
+        (shape((requests, gcols), bf16), shape((requests, width), bf16)),
+        [VMEM] * 5,
+    )(
+        hidden,
+        mix_gain.reshape(1, width),
+        in_groups,
+        conv_groups.transpose(1, 0, 2),
+        taps_groups,
+    )
+    swap = [(i, (i + GROUPS) % count) for i in range(count)]
+    other = lax.ppermute(group_conv, "seq", swap)
+    gate, conv, step, decay = call(
+        gate_kernel,
+        (
+            shape((requests, head_width), f32),
+            shape((requests, head_width), f32),
+            shape((requests, LANES), f32),
+            shape((requests, LANES), f32),
+        ),
+        [VMEM] * 5 + [SMEM] * 2,
+    )(
+        normed,
+        in_gate_input,
+        in_step.T,
+        conv_input.transpose(1, 0, 2),
+        taps_input,
+        decay_rate,
+        step_bias,
+    )
+    state = ssm_state.reshape(requests, head_width, STATE)
+    sent = call(
+        mixer_kernel,
+        shape((count, requests, columns + LANES), bf16),
+        [SMEM] * 2 + [VMEM] * 9,
+    )(
+        position,
+        skip_gain,
+        group_conv,
+        other,
+        gate,
+        conv,
+        step,
+        decay,
+        state,
+        out_mixer,
+        norm_gain.reshape(1, head_width),
+    )
+    received = lax.all_to_all(sent, "seq", 0, 0)
+    new_state = call(state_kernel, shape(state.shape, f32), [SMEM] + [VMEM] * 6)(
+        position, group_conv, other, conv, step, decay, state
+    )
+    chunk = w_qkv.shape[1] // chunks
+    sent, middle = call(
+        functools.partial(project_kernel, chunks, head_width),
+        (
+            shape((count, SUB, chunk + LANES), bf16),
+            shape((requests, columns), f32),
+        ),
+        [SMEM] + [VMEM] * 5,
+    )(position, received, hidden, attn_gain.reshape(1, columns), w_qkv, page_table.T)
+    received = lax.all_to_all(sent, "seq", 0, 0)
+    package = pages * (QH + 2 * KVH) + SUB
+    sent = call(
+        functools.partial(attend_kernel, width),
+        shape((count, package, HD), bf16),
+        [SMEM] + [VMEM] * 4,
+        [pltpu.VMEM((chunk // HD * SUB, HD), f32)],
+    )(position, received, kv_cache, page_table.T, lengths.reshape(1, requests))
+    received = lax.all_to_all(sent, "seq", 0, 0)
+    final, new_kv = call(
+        functools.partial(merge_kernel, pages),
+        (
+            shape((requests, columns), bf16),
+            shape((requests, 2 * KVH * HD), bf16),
+        ),
+        [SMEM] + [VMEM] * 3,
+        [
+            pltpu.VMEM((count, LANES, LANES), f32),
+            pltpu.VMEM((requests * QH, HD), f32),
+            pltpu.VMEM((requests * 2 * KVH, HD), f32),
+        ],
+    )(page_table, received, w_out, middle)
+    return (final, new_state.reshape(ssm_state.shape), new_kv)
+
+
+def shards(*args):
+    hidden, in_step, in_groups = args[0], args[3], args[4]
+    kv_cache, page_table = args[18], args[19]
+    count = lax.axis_size("seq")
+    whole_tiles = (
+        in_step.shape[1] == 1
+        and in_groups.shape[1] == STATE
+        and count == 2 * GROUPS
+        and hidden.shape[0] == SUB
+        and (hidden.shape[1] // count) % LANES == 0
+        and SUB % kv_cache.shape[0] == 0
+        and kv_cache.shape[0] * QH <= LANES
+        and kv_cache.shape[1] == LANES
+    )
+    return (fused_shards if whole_tiles else plain_shards)(*args)
+
+
 def solution(mesh):
     placed = (
         P("grp", None),

time: 93.7 us -> 70 us (0.75)
  blocking collectives: 0 us -> 28.4 us
  other arithmetic: 19.1 us -> 0 us
  Pallas kernels: 0 us -> 18.7 us
  local copies, waits for them, and re-layouts: 17.5 us -> 1.99 us
  waiting for transfers between devices: 24.6 us -> 10.1 us
  matrix products: 12.4 us -> 0 us
  starting transfers between devices: 15.9 us -> 7.62 us
    all_to_all x0 -> x2, blocking collectives: none -> 28.4 us  [fused_shards(): received = lax.all_to_all(sent, 'seq', 0, 0)]
    pallas_call x0 -> x7, Pallas kernels: none -> 18.7 us  [the longest x1 3.54 us: fused_shards(): call(functools.partial(project_kernel, chunks, head_width), (shape((count...]
    all_to_all x3 -> x1, waiting for transfers between devices: 24.6 us -> 10.1 us  [fused_shards(): received = lax.all_to_all(sent, 'seq', 0, 0)]
    dot_general x8 -> x0, matrix products: 12.4 us -> none  [the longest x1 2.57 us: shards(): jnp.dot(attended.reshape(requests, QH * HD), w_out, preferred_element_typ...]
    all_to_all x3 -> x1, starting transfers between devices: 11.8 us -> 3.56 us  [fused_shards(): received = lax.all_to_all(sent, 'seq', 0, 0)]
    reduce_sum x16 -> x0, other arithmetic: 7.43 us -> none  [the longest x1 1.8 us: shards(): jnp.sum(new_state * readout_heads[:, :, None, :], axis=-1)]
    slice x7 -> x0, local copies, waits for them, and re-layouts: 4.77 us -> none  [the longest x1 1.67 us: shards(): all_values = everything[:, :value_rows].reshape(pages_all, QH, HD)]
    convert_element_type x12 -> x0, other arithmetic: 4.48 us -> none  [the longest x1 1.49 us: shards(): stream = hidden.astype(jnp.float32)]
  transfers between devices with their start and end apart: 4 -> 2, of which waited for: 3 -> 1; matrix products, arithmetic and copies ran while one was open for 16% -> 1% of each run, Pallas kernels for 0% -> 6%
where the time goes in v2:
time: 70 us; the launch traced here: 69.5 us
  blocking collectives  28.4 us (41%)
  Pallas kernels  18.7 us (27%)
  waiting for transfers between devices  10.1 us (14%)
  starting transfers between devices  7.62 us (11%)
  between operations  2.61 us (4%)
  local copies, waits for them, and re-layouts  1.99 us (3%)
    all_to_all x2, blocking collectives, fused_shards(): received = lax.all_to_all(sent, 'seq', 0, 0)  28.4 us
    all_to_all x1, waiting for transfers between devices, fused_shards(): received = lax.all_to_all(sent, 'seq', 0, 0)  10.1 us
    ppermute x1, starting transfers between devices, fused_shards(): other = lax.ppermute(group_conv, 'seq', swap)  4.06 us
    all_to_all x1, starting transfers between devices, fused_shards(): received = lax.all_to_all(sent, 'seq', 0, 0)  3.56 us
    pallas_call x1, Pallas kernels, fused_shards(): call(functools.partial(project_kernel, chunks, head_width), (shape((count...  3.54 us
    pallas_call x1, Pallas kernels, fused_shards(): call(functools.partial(merge_kernel, pages), (shape((requests, columns),...  3.18 us
    pallas_call x1, Pallas kernels, fused_shards(): call(functools.partial(attend_kernel, width), shape((count, package, HD),...  3.15 us
    pallas_call x1, Pallas kernels, fused_shards(): call(mixer_kernel, shape((count, requests, columns + LANES), bf16), [SMEM...  2.52 us
  transfers between devices with their start and end apart: 2, of which 1 were waited for; matrix products, arithmetic and copies ran while one was open for 1% of the time, Pallas kernels for 6%

profile of v2, /device:TPU:0, one launch (start us, length us, event | category | flops | bytes accessed | tf_op | source)
XLA Modules:
  0.0 69.5 jit_solution(12726334593665034326)
XLA Ops:
  0.6 2.3 %shard_map.220 = (bf16[8,128]{1,0:T(8,128)(2,1)}, bf16[8,4096]{1,0:T(8,128)(2,1)}) custom-call(bf16[8,4096]{1,0:T(8,128)(2,1)} %hidden.3, f32[1,4096]{1,0:T(1,128)} %bitcast.18, bf16[4096,128]{1,0:T(8,128)(2,1)} %weights.5, bf16[3,8,128]{2,1,0:T(8,128)(2,1)} %bitcast.20, f32[5,128]{1,0:T(8,128)} %taps.2), custom_call_target="tpu_custom_call" | custom-call | tf_op jit(solution)/shard_map/pallas_call | solution.py:568
  2.9 4.1 %collective-permute-start = (bf16[8,128]{1,0:T(8,128)(2,1)}, bf16[8,128]{1,0:T(8,128)(2,1)S(1)}, u32[]{:S(2)}, u32[]{:S(2)}) collective-permute-start(bf16[8,128]{1,0:T(8,128)(2,1)} %get-tuple-element.13.own), channel_id=1, source_target_pairs={{0,8},{1,9},{2,10},{3,11},{4,12},{5,13},{6,14},{7,15},{8,0},{9,1},... | collective-permute-start | bytes 6152 | tf_op jit(solution)/shard_map/ppermute | solution.py:580
  8.9 2.2 %shard_map.221 = (f32[8,64]{1,0:T(8,128)}, f32[8,64]{1,0:T(8,128)}, f32[8,128]{1,0:T(8,128)}, f32[8,128]{1,0:T(8,128)}) custom-call(bf16[8,4096]{1,0:T(8,128)(2,1)} %get-tuple-element.14.normed_ref, bf16[4096,128]{1,0:T(8,128)(2,1)} %weights.6, bf16[1,4096]{1,0:T(2,128)(2,1)} %bitcast.19, bf16[3,8,64]{2,1,0:T(8,128)(2,1)} %bitcast.21, f32[5,64]{1,0:T(8,128)} %taps.3, ...), custom_call_target="tpu_custom_call" | custom-call | tf_op jit(solution)/shard_map/pallas_call | solution.py:581
  11.1 0.0 collective-permute-done.other
  11.1 0.0 copy-start.2
  11.1 0.6 copy-done.2
  11.6 2.5 %shard_map.222 = bf16[16,8,384]{2,1,0:T(8,128)(2,1)} custom-call(s32[1]{0:T(128)} %bitcast.position, f32[1]{0:T(128)S(6)} %copy.28.skip, bf16[8,128]{1,0:T(8,128)(2,1)} %get-tuple-element.13.own, bf16[8,128]{1,0:T(8,128)(2,1)} %copy-done.2, f32[8,64]{1,0:T(8,128)} %get-tuple-element.15.gate, f32[8,64]{1,0:T(8,128)} %get-tuple-element.16.conv, ...), custom_call_target="tpu_custom_call" | custom-call | tf_op jit(solution)/shard_map/pallas_call | solution.py:600
  14.2 11.5 %all_to_all.15.received = bf16[16,8,384]{2,1,0:T(8,128)(2,1)} all-to-all(bf16[16,8,384]{2,1,0:T(8,128)(2,1)} %shard_map.222), channel_id=1, replica_groups=mesh['grp'=2,'seq'=16] {'seq'}, dimensions={0} | all-to-all | bytes 196608 | tf_op jit(solution)/shard_map/all_to_all | solution.py:617
  25.7 0.0 copy-start.1
  25.7 3.5 %shard_map.223 = (bf16[16,8,1664]{2,1,0:T(8,128)(2,1)}, f32[8,256]{1,0:T(8,128)}) custom-call(s32[1]{0:T(128)} %bitcast.position, bf16[16,8,384]{2,1,0:T(8,128)(2,1)} %all_to_all.15.received, bf16[8,4096]{1,0:T(8,128)(2,1)} %hidden.3, f32[1,256]{1,0:T(1,128)} %bitcast.22, bf16[256,6144]{1,0:T(8,128)(2,1)} %weights.8, s32[4,8]{1,0:T(4,128)} %bitcast.16), custom_call_target="tpu_custom_call" | custom-call | tf_op jit(solution)/shard_map/pallas_call | solution.py:622
  29.2 16.9 %all_to_all.16.received = bf16[16,8,1664]{2,1,0:T(8,128)(2,1)} all-to-all(bf16[16,8,1664]{2,1,0:T(8,128)(2,1)} %get-tuple-element.19), channel_id=1, replica_groups=mesh['grp'=2,'seq'=16] {'seq'}, dimensions={0} | all-to-all | bytes 851968 | tf_op jit(solution)/shard_map/all_to_all | solution.py:630
  46.2 3.1 %shard_map.224 = bf16[16,104,128]{2,1,0:T(8,128)(2,1)} custom-call(s32[1]{0:T(128)} %bitcast.position, bf16[16,8,1664]{2,1,0:T(8,128)(2,1)} %all_to_all.16.received, bf16[2,128,2048]{2,1,0:T(8,128)(2,1)} %cache.1, s32[4,8]{1,0:T(4,128)} %bitcast.17, s32[1,8]{1,0:T(1,128)} %bitcast.24), custom_call_target="tpu_custom_call" | custom-call | tf_op jit(solution)/shard_map/pallas_call | solution.py:632
  49.3 3.6 %all-to-all-start.2 = ((bf16[16,104,128]{2,1,0:T(8,128)(2,1)}), bf16[16,104,128]{2,1,0:T(8,128)(2,1)S(1)}, u32[]{:S(2)}, u32[]{:S(2)}) async-start(bf16[16,104,128]{2,1,0:T(8,128)(2,1)} %shard_map.224), calls=%async_computation.2 | async-start | bytes 851968 | tf_op jit(solution)/shard_map/all_to_all | solution.py:638
  52.9 0.0 copy-done.1
  52.9 0.7 copy.24.table
  53.6 1.9 %shard_map.226 = f32[8,64,128]{2,1,0:T(8,128)} custom-call(s32[1]{0:T(128)} %bitcast.position, bf16[8,128]{1,0:T(8,128)(2,1)} %get-tuple-element.13.own, bf16[8,128]{1,0:T(8,128)(2,1)} %copy-done.2, f32[8,64]{1,0:T(8,128)} %get-tuple-element.16.conv, f32[8,128]{1,0:T(8,128)} %get-tuple-element.17.step, f32[8,128]{1,0:T(8,128)} %get-tuple-element.18.decay, ...), custom_call_target="tpu_custom_call" | custom-call | tf_op jit(solution)/shard_map/pallas_call | solution.py:618
  55.4 10.1 %all-to-all-done.2.received = bf16[16,104,128]{2,1,0:T(8,128)(2,1)S(1)} async-done(((bf16[16,104,128]{2,1,0:T(8,128)(2,1)}), bf16[16,104,128]{2,1,0:T(8,128)(2,1)S(1)}, u32[]{:S(2)}, u32[]{:S(2)}) %all-to-all-start.2) | async-done | bytes 426016 | tf_op jit(solution)/shard_map/all_to_all | solution.py:638
  65.5 0.0 copy-start
  65.5 0.8 %copy-done = bf16[16,104,128]{2,1,0:T(8,128)(2,1)} copy-done((bf16[16,104,128]{2,1,0:T(8,128)(2,1)}, bf16[16,104,128]{2,1,0:T(8,128)(2,1)S(1)}, u32[]{:S(2)}) %copy-start) | copy-done | bytes 426008
  66.3 3.2 %shard_map.225 = (bf16[8,256]{1,0:T(8,128)(2,1)}, bf16[8,2048]{1,0:T(8,128)(2,1)}) custom-call(s32[8,4]{1,0:T(8,128)} %copy.24.table, bf16[16,104,128]{2,1,0:T(8,128)(2,1)} %copy-done, bf16[4096,256]{1,0:T(8,128)(2,1)} %weights.9, f32[8,256]{1,0:T(8,128)} %get-tuple-element.20.middle), custom_call_target="tpu_custom_call" | custom-call | tf_op jit(solution)/shard_map/pallas_call | solution.py:639
Async XLA Ops:
  2.9 8.2 %collective-permute-start = (bf16[8,128]{1,0:T(8,128)(2,1)}, bf16[8,128]{1,0:T(8,128)(2,1)S(1)}, u32[]{:S(2)}, u32[]{:S(2)}) collective-permute-start(bf16[8,128]{1,0:T(8,128)(2,1)} %get-tuple-element.13.own), channel_id=1, source_target_pairs={{0,8},{1,9},{2,10},{3,11},{4,12},{5,13},{6,14},{7,15},{8,0},{9,1},... | collective-permute-start | bytes 6152 | tf_op jit(solution)/shard_map/ppermute | solution.py:580
  11.1 0.6 copy-start.2
  25.7 27.2 %copy-start.1 = (s32[8,4]{0,1:T(4,128)S(1)}, s32[8,4]{0,1:T(4,128)}, u32[]{:S(2)}) copy-start(s32[8,4]{0,1:T(4,128)} %param.40) | copy-start | bytes 388
  49.3 16.2 %all-to-all-start.2 = ((bf16[16,104,128]{2,1,0:T(8,128)(2,1)}), bf16[16,104,128]{2,1,0:T(8,128)(2,1)S(1)}, u32[]{:S(2)}, u32[]{:S(2)}) async-start(bf16[16,104,128]{2,1,0:T(8,128)(2,1)} %shard_map.224), calls=%async_computation.2 | async-start | bytes 851968 | tf_op jit(solution)/shard_map/all_to_all | solution.py:638
  65.5 0.8 %copy-start = (bf16[16,104,128]{2,1,0:T(8,128)(2,1)}, bf16[16,104,128]{2,1,0:T(8,128)(2,1)S(1)}, u32[]{:S(2)}) copy-start(bf16[16,104,128]{2,1,0:T(8,128)(2,1)S(1)} %all-to-all-done.2.received) | copy-start | bytes 1277956

commit v3 on v2

--- a/solution.py
+++ b/solution.py
@@ -230,22 +230,41 @@
 bf16 = jnp.bfloat16
 SUB = 8
 PARTS = 3
+SCOPED = 16 << 20
+BLOCKS = 4
 VMEM = pl.BlockSpec(memory_space=pltpu.VMEM)
+NEAR = pl.BlockSpec(memory_space=pltpu.VMEM)
 SMEM = pl.BlockSpec(memory_space=pltpu.SMEM)
+FAR = pl.BlockSpec(memory_space=pltpu.HBM)
 
 
 def call(kernel, outs, specs, scratch=()):
-    return pl.pallas_call(
+    grid_free = pl.pallas_call(
         kernel,
         out_shape=outs,
         in_specs=specs,
-        out_specs=jax.tree.map(lambda _: VMEM, outs),
+        out_specs=jax.tree.map(lambda _: VMEM, outs, is_leaf=lambda x: hasattr(x, "shape")),
         scratch_shapes=scratch,
-    )
+        compiler_params=pltpu.CompilerParams(vmem_limit_bytes=SCOPED),
+    )
+
+    def run(*args):
+        spaces = {id(NEAR): pltpu.VMEM, id(FAR): pltpu.HBM}
+        placed = [
+            pltpu.with_memory_space_constraint(arg, spaces[id(spec)]) if id(spec) in spaces else arg
+            for arg, spec in zip(args, specs)
+        ]
+        return grid_free(*placed)
+
+    return run
 
 
 def shape(dims, kind):
     return jax.ShapeDtypeStruct(dims, kind)
+
+
+def near(dims, kind):
+    return pltpu.VMEM(dims, kind)
 
 
 def silu(x):
@@ -277,29 +296,92 @@
     return silu(total)
 
 
-def group_kernel(hidden, gain, weights, state, taps, group_out, normed_out):
+def fetch_all(pairs, sems):
+    copies = [
+        pltpu.make_async_copy(source, target, sems.at[k])
+        for k, (source, target) in enumerate(pairs)
+    ]
+    for copy in copies:
+        copy.start()
+    return copies
+
+
+def group_kernel(
+    hidden_far,
+    gain_far,
+    weights_far,
+    state_far,
+    taps_far,
+    group_out,
+    normed_out,
+    hidden,
+    gain,
+    weights,
+    state,
+    taps,
+    sems,
+):
+    depth = weights.shape[0] // BLOCKS
+    rows = [pl.ds(k * depth, depth) for k in range(BLOCKS)]
+    copies = fetch_all(
+        [(hidden_far, hidden), (gain_far, gain)]
+        + [(weights_far.at[r], weights.at[r]) for r in rows]
+        + [(state_far, state), (taps_far, taps)],
+        sems,
+    )
+    copies[0].wait()
+    copies[1].wait()
     stream = hidden[...].astype(f32)
     mean = jnp.mean(stream * stream, axis=-1, keepdims=True)
-    normed = (stream * lax.rsqrt(mean + epsilon) * gain[...]).astype(bf16)
-    normed_out[...] = normed
-    raw = jnp.dot(normed, weights[...], preferred_element_type=f32)
+    normed_out[...] = (stream * lax.rsqrt(mean + epsilon) * gain[...]).astype(bf16)
+    raw = jnp.zeros(group_out.shape, f32)
+    for k in range(BLOCKS):
+        copies[2 + k].wait()
+        span = slice(k * depth, (k + 1) * depth)
+        raw = raw + jnp.dot(normed_out[:, span], weights[span, :], preferred_element_type=f32)
+    copies[-2].wait()
+    copies[-1].wait()
     group_out[...] = convolve(state, raw, taps).astype(bf16)
 
 
-def gate_kernel(
-    normed_ref, weights, step_row, state, taps, rate, bias, gate_out, conv_out, step_out, decay_out
-):
-    normed = normed_ref[...]
-    both = jnp.dot(normed, weights[...], preferred_element_type=f32)
-    half = both.shape[1] // 2
+def gate_kernel(carried, position, normed_ref, *refs):
+    weights_far, step_far, state_far, taps_far, numbers, hidden_far = refs[:6]
+    inputs, outputs, scratch = refs[6 : 6 + carried], refs[6 + carried : -5], refs[-5:]
+    gate_out, conv_out, step_out, decay_out, columns_out = outputs[:5]
+    weights, step_row, state, taps, sems = scratch
+    columns = columns_out.shape[1]
+    start = pl.multiple_of(position[0] * columns, columns)
+    depth = weights.shape[0] // BLOCKS
+    rows = [pl.ds(k * depth, depth) for k in range(BLOCKS)]
+    copies = fetch_all(
+        [(weights_far.at[r], weights.at[r]) for r in rows]
+        + [
+            (step_far, step_row),
+            (state_far, state),
+            (taps_far, taps),
+            (hidden_far.at[:, pl.ds(start, columns)], columns_out),
+        ]
+        + list(zip(inputs, outputs[5:])),
+        sems,
+    )
+    half = gate_out.shape[1]
+    both = jnp.zeros((gate_out.shape[0], weights.shape[1]), f32)
+    for k in range(BLOCKS):
+        copies[k].wait()
+        span = slice(k * depth, (k + 1) * depth)
+        both = both + jnp.dot(normed_ref[:, span], weights[span, :], preferred_element_type=f32)
+    for copy in copies[BLOCKS : BLOCKS + 3]:
+        copy.wait()
     gate_out[...] = silu(both[:, :half])
-    conv_out[...] = convolve(state, both[:, half:], taps)
-    raw = jnp.sum(
-        normed.astype(f32) * step_row[...].astype(f32), axis=-1, keepdims=True
-    )
-    step = jax.nn.softplus(raw + bias[0])
+    fresh = convolve(state, both[:, half:], taps)
+    conv_out[:, :half] = fresh
+    conv_out[:, half:] = numbers[2] * fresh
+    raw = jnp.sum(normed_ref[...].astype(f32) * step_row[...].astype(f32), axis=-1, keepdims=True)
+    step = jax.nn.softplus(raw + numbers[1])
     step_out[...] = jnp.broadcast_to(step, step_out.shape)
-    decay_out[...] = jnp.broadcast_to(jnp.exp(-rate[0] * step), decay_out.shape)
+    decay_out[...] = jnp.broadcast_to(jnp.exp(-numbers[0] * step), decay_out.shape)
+    for copy in copies[BLOCKS + 3 :]:
+        copy.wait()
 
 
 def chosen(position, own, other):
@@ -308,13 +390,12 @@
     return jnp.where(first, mine, theirs), jnp.where(first, theirs, mine)
 
 
-def mixer_kernel(
-    position, skip, own, other, gate, conv, step, decay, state, weights, gain, sent
-):
+def mixer_kernel(position, own, other, gate, conv, step, decay, state, weights, gain, sent):
     requests = own.shape[0]
     inject, readout = chosen(position, own, other)
-    row = lax.broadcasted_iota(jnp.int32, conv.shape, 0)
-    read = jnp.zeros(conv.shape, f32)
+    half = gate.shape[1]
+    row = lax.broadcasted_iota(jnp.int32, gate.shape, 0)
+    read = jnp.zeros(gate.shape, f32)
     for r in range(requests):
         part = lax.dot_general(
             readout,
@@ -325,12 +406,8 @@
         )
         read = jnp.where(row == r, part, read)
     along = jnp.sum(inject * readout, axis=-1, keepdims=True)
-    fresh = conv[...]
-    out = (
-        decay[:, :1] * read
-        + step[:, :1] * fresh * along
-        + skip[0] * fresh
-    )
+    fresh = conv[:, :half]
+    out = decay[:, :1] * read + step[:, :1] * fresh * along + conv[:, half:]
     gated = out * gate[...]
     marks = marked(jnp.sum(gated * gated, axis=-1, keepdims=True), 2).astype(bf16)
     weighted = (gated * gain[...]).astype(bf16)
@@ -346,14 +423,14 @@
 
 def state_kernel(position, own, other, conv, step, decay, state, new_state):
     inject, _ = chosen(position, own, other)
-    fresh = step[:, :1] * conv[...]
+    fresh = step[:, :1] * conv[:, : state.shape[1]]
     new_state[...] = (
         decay[:, :1][:, :, None] * state[...] + fresh[:, :, None] * inject[:, None, :]
     )
 
 
 def project_kernel(
-    chunks, head_width, position, received, hidden, gain, weights, table, sent, middle_out
+    chunks, head_width, position, received, hidden, gain, weights, table, keep, give, middle_out
 ):
     count, requests, _ = received.shape
     columns = weights.shape[0]
@@ -366,15 +443,18 @@
         scale = lax.rsqrt(total / (len(members) * head_width) + epsilon)
         products = sum(received[k, :, :columns].astype(f32) for k in members)
         mixer = mixer + scale * products
-    start = pl.multiple_of(position[0] * columns, columns)
-    middle = (hidden[:, pl.ds(start, columns)].astype(f32) + mixer).astype(bf16).astype(f32)
+    middle = (hidden[...].astype(f32) + mixer).astype(bf16).astype(f32)
     middle_out[...] = middle
     marks = marked(jnp.sum(middle * middle, axis=-1, keepdims=True), 2)
     extended = jnp.concatenate([middle * gain[...], marks], axis=-1).astype(bf16)
     rows = count * SUB
     pages = SUB // chunks
+    chips = count // 2
+    core = position[0] % 2
     index = lax.broadcasted_iota(jnp.int32, (rows, requests), 0)
-    page = (index // SUB) * pages + index % pages
+    line = index % (chips * SUB)
+    parity = jnp.where(index < chips * SUB, core, 1 - core)
+    page = ((line // SUB) * 2 + parity) * pages + index % pages
     hits = page == table[0:1, :]
     for j in range(1, table.shape[0]):
         hits = jnp.logical_or(hits, page == table[j : j + 1, :])
@@ -394,10 +474,23 @@
                 preferred_element_type=f32,
             )
             total = part if total is None else total + part
-        for e in range(count):
-            sent[e, :, n : n + tile] = total[e * SUB : (e + 1) * SUB].astype(bf16)
-    for e in range(count):
-        sent[e, :, chunk:] = spread[e * SUB : (e + 1) * SUB, columns:].astype(bf16)
+        for e in range(chips):
+            keep[e, :, n : n + tile] = total[e * SUB : (e + 1) * SUB]
+            first = (chips + e) * SUB
+            give[e, :, n : n + tile] = total[first : first + SUB].astype(bf16)
+    for e in range(chips):
+        keep[e, :, chunk:] = spread[e * SUB : (e + 1) * SUB, columns:]
+        first = (chips + e) * SUB
+        give[e, :, chunk:] = spread[first : first + SUB, columns:].astype(bf16)
+
+
+def pair_kernel(keep, taken, sent):
+    chunk = keep.shape[2] - LANES
+    for e in range(keep.shape[0]):
+        total = keep[e] + taken[e].astype(f32)
+        marks = total[:, chunk : chunk + 1] + total[:, chunk + 1 : chunk + 2]
+        sent[e, :, :chunk] = total[:, :chunk].astype(bf16)
+        sent[e, :, chunk:] = marked(marks, 2).astype(bf16)
 
 
 def attend_kernel(width, position, received, cache, table, lengths, sent, lines):
@@ -489,27 +582,41 @@
         sent[e, value_rows + pages * fresh_rows :, :] = terms
 
 
-def merge_kernel(pages, table, received, weights, middle, final, new_kv, spread, rows, fresh):
-    count, package, _ = received.shape
-    requests, pages_req = table.shape
+def merge_kernel(
+    pages, position, table, near, far, weights, middle, final, new_kv, spread, rows, fresh
+):
+    chips, package, _ = near.shape
+    pages_req, requests = table.shape
     value_rows = pages * QH
     kv_rows = 2 * KVH
     last = value_rows + pages * kv_rows
-    logs = jnp.concatenate([received[k, last:, :] for k in range(count)], axis=0)
-    source = lax.broadcasted_iota(jnp.int32, (count * SUB, LANES), 0) // SUB
-    for k in range(count):
-        mask = jnp.where(source == k, 1.0, 0.0).astype(bf16)
-        spread[k] = lax.dot_general(
-            logs, mask, (((0,), (0,)), ((), ())), preferred_element_type=f32
-        )
+    source = lax.broadcasted_iota(jnp.int32, (chips * SUB, LANES), 0) // SUB
+    masks = [jnp.where(source == k, 1.0, 0.0).astype(bf16) for k in range(chips)]
+    for side, packages in enumerate((near, far)):
+        logs = jnp.concatenate([packages[k, last:, :] for k in range(chips)], axis=0)
+        for k in range(chips):
+            spread[side * chips + k] = lax.dot_general(
+                logs, masks[k], (((0,), (0,)), ((), ())), preferred_element_type=f32
+            )
+    core = position[0] % 2
+
+    def fetch(chip, side, first, many):
+        both = near[chip, pl.ds(first, many), :], far[chip, pl.ds(first, many), :]
+        return jnp.where(side == 0, both[0].astype(f32), both[1].astype(f32))
+
     for r in range(requests):
         peaks, values = [], []
         for j in range(pages_req):
-            page = table[r, j]
+            page = table[j, r]
             device, slot = page // pages, page % pages
+            chip = device // 2
+            side = lax.rem(device + core, 2)
             first = pl.multiple_of(slot * QH, QH)
-            peaks.append(spread[device, pl.ds(first, QH), :])
-            values.append(received[device, pl.ds(first, QH), :].astype(f32))
+            peaks.append(spread[side * chips + chip, pl.ds(first, QH), :])
+            values.append(fetch(chip, side, first, QH))
+            if j == 0:
+                first = pl.multiple_of(value_rows + slot * kv_rows, kv_rows)
+                fresh[r * kv_rows : (r + 1) * kv_rows, :] = fetch(chip, side, first, kv_rows)
         top = functools.reduce(jnp.maximum, peaks)
         mass = jnp.zeros(top.shape, f32)
         summed = jnp.zeros(top.shape, f32)
@@ -518,11 +625,6 @@
             mass = mass + factor
             summed = summed + factor * value
         rows[r * QH : (r + 1) * QH, :] = summed / mass
-        page = table[r, 0]
-        first = pl.multiple_of(value_rows + (page % pages) * kv_rows, kv_rows)
-        fresh[r * kv_rows : (r + 1) * kv_rows, :] = received[
-            page // pages, pl.ds(first, kv_rows), :
-        ].astype(f32)
     for c in range(kv_rows):
         new_kv[:, c * HD : (c + 1) * HD] = fresh[pl.ds(c, requests, stride=kv_rows), :].astype(
             bf16
@@ -564,91 +666,100 @@
     head_width = in_gate_input.shape[1] // 2
     pages = kv_cache.shape[0]
     chunks = SUB // pages
+    chips = count // 2
     gcols = in_groups.shape[1]
-    group_conv, normed = call(
-        group_kernel,
-        (shape((requests, gcols), bf16), shape((requests, width), bf16)),
-        [VMEM] * 5,
-    )(
+    state = ssm_state.reshape(requests, head_width, STATE)
+    same_core = [list(range(core, count, 2)) for core in range(2)]
+    cores = [(i, i ^ 1) for i in range(count)]
+    group_args = (
         hidden,
         mix_gain.reshape(1, width),
         in_groups,
         conv_groups.transpose(1, 0, 2),
         taps_groups,
     )
+    group_conv, normed = call(
+        group_kernel,
+        (near((requests, gcols), bf16), near((requests, width), bf16)),
+        [FAR] * 5,
+        [pltpu.VMEM(x.shape, x.dtype) for x in group_args]
+        + [pltpu.SemaphoreType.DMA((len(group_args) - 1 + BLOCKS,))],
+    )(*group_args)
     swap = [(i, (i + GROUPS) % count) for i in range(count)]
     other = lax.ppermute(group_conv, "seq", swap)
-    gate, conv, step, decay = call(
-        gate_kernel,
-        (
-            shape((requests, head_width), f32),
-            shape((requests, head_width), f32),
-            shape((requests, LANES), f32),
-            shape((requests, LANES), f32),
-        ),
-        [VMEM] * 5 + [SMEM] * 2,
-    )(
-        normed,
+    carried = (
+        state,
+        out_mixer,
+        norm_gain.reshape(1, head_width),
+        attn_gain.reshape(1, columns),
+        page_table.T,
+        lengths.reshape(1, requests),
+    )
+    gate_args = (
         in_gate_input,
         in_step.T,
         conv_input.transpose(1, 0, 2),
         taps_input,
-        decay_rate,
-        step_bias,
-    )
-    state = ssm_state.reshape(requests, head_width, STATE)
+    )
+    numbers = jnp.concatenate([decay_rate, step_bias, skip_gain])
+    gate, conv, step, decay, stream, state_in, mixer, gain, scale, table, spans = call(
+        functools.partial(gate_kernel, len(carried)),
+        (
+            near((requests, head_width), f32),
+            near((requests, 2 * head_width), f32),
+            near((requests, LANES), f32),
+            near((requests, LANES), f32),
+            near((requests, columns), bf16),
+        )
+        + tuple(near(x.shape, x.dtype) for x in carried),
+        [SMEM, NEAR] + [FAR] * 4 + [SMEM] + [FAR] * (1 + len(carried)),
+        [pltpu.VMEM(x.shape, x.dtype) for x in gate_args]
+        + [pltpu.SemaphoreType.DMA((BLOCKS + 4 + len(carried),))],
+    )(position, normed, *gate_args, numbers, hidden, *carried)
     sent = call(
         mixer_kernel,
-        shape((count, requests, columns + LANES), bf16),
-        [SMEM] * 2 + [VMEM] * 9,
-    )(
-        position,
-        skip_gain,
-        group_conv,
-        other,
-        gate,
-        conv,
-        step,
-        decay,
-        state,
-        out_mixer,
-        norm_gain.reshape(1, head_width),
-    )
+        near((count, requests, columns + LANES), bf16),
+        [SMEM] + [NEAR] * 9,
+    )(position, group_conv, other, gate, conv, step, decay, state_in, mixer, gain)
     received = lax.all_to_all(sent, "seq", 0, 0)
-    new_state = call(state_kernel, shape(state.shape, f32), [SMEM] + [VMEM] * 6)(
-        position, group_conv, other, conv, step, decay, state
+    new_state = call(state_kernel, shape(state.shape, f32), [SMEM] + [NEAR] * 6)(
+        position, group_conv, other, conv, step, decay, state_in
     )
     chunk = w_qkv.shape[1] // chunks
-    sent, middle = call(
+    keep, give, middle = call(
         functools.partial(project_kernel, chunks, head_width),
         (
-            shape((count, SUB, chunk + LANES), bf16),
-            shape((requests, columns), f32),
+            near((chips, SUB, chunk + LANES), f32),
+            near((chips, SUB, chunk + LANES), bf16),
+            near((requests, columns), f32),
         ),
-        [SMEM] + [VMEM] * 5,
-    )(position, received, hidden, attn_gain.reshape(1, columns), w_qkv, page_table.T)
-    received = lax.all_to_all(sent, "seq", 0, 0)
+        [SMEM] + [NEAR] * 5,
+    )(position, received, stream, scale, w_qkv, table)
+    taken = lax.ppermute(give, "seq", cores)
+    sent = call(pair_kernel, near(give.shape, bf16), [NEAR] * 2)(keep, taken)
+    received = lax.all_to_all(sent, "seq", 0, 0, axis_index_groups=same_core)
     package = pages * (QH + 2 * KVH) + SUB
     sent = call(
         functools.partial(attend_kernel, width),
-        shape((count, package, HD), bf16),
-        [SMEM] + [VMEM] * 4,
+        near((chips, package, HD), bf16),
+        [SMEM] + [NEAR] * 4,
         [pltpu.VMEM((chunk // HD * SUB, HD), f32)],
-    )(position, received, kv_cache, page_table.T, lengths.reshape(1, requests))
-    received = lax.all_to_all(sent, "seq", 0, 0)
+    )(position, received, kv_cache, table, spans)
+    received = lax.all_to_all(sent, "seq", 0, 0, axis_index_groups=same_core)
+    far = lax.ppermute(received, "seq", cores)
     final, new_kv = call(
         functools.partial(merge_kernel, pages),
         (
             shape((requests, columns), bf16),
             shape((requests, 2 * KVH * HD), bf16),
         ),
-        [SMEM] + [VMEM] * 3,
+        [SMEM] * 2 + [NEAR] * 4,
         [
             pltpu.VMEM((count, LANES, LANES), f32),
             pltpu.VMEM((requests * QH, HD), f32),
             pltpu.VMEM((requests * 2 * KVH, HD), f32),
         ],
-    )(page_table, received, w_out, middle)
+    )(position, page_table.T, received, far, w_out, middle)
     return (final, new_state.reshape(ssm_state.shape), new_kv)
 
 

time: 70 us -> 53 us (0.76)
  Pallas kernels: 18.7 us -> 10.2 us
  waiting for transfers between devices: 10.1 us -> 2.01 us
  blocking collectives: 28.4 us -> 33.5 us
  starting transfers between devices: 7.62 us -> 4.2 us
  local copies, waits for them, and re-layouts: 1.99 us -> 0.02 us
    all_to_all x0 -> x2, blocking collectives: none -> 22.4 us  [fused_shards(): received = lax.all_to_all(sent, 'seq', 0, 0, axis_index_groups=same_core)]
    all_to_all x2 -> x1, blocking collectives: 28.4 us -> 11.1 us  [fused_shards(): received = lax.all_to_all(sent, 'seq', 0, 0)]
    all_to_all x1 -> x0, waiting for transfers between devices: 10.1 us -> none  [fused_shards(): received = lax.all_to_all(sent, 'seq', 0, 0)]
    pallas_call x7 -> x8, Pallas kernels: 18.7 us -> 10.2 us  [run(): return grid_free(*placed)]
    all_to_all x1 -> x0, starting transfers between devices: 3.56 us -> none  [fused_shards(): received = lax.all_to_all(sent, 'seq', 0, 0)]
    ppermute x0 -> x2, waiting for transfers between devices: none -> 2 us  [the longest x1 1.45 us: fused_shards(): taken = lax.ppermute(give, 'seq', cores)]
    unnamed x7 -> x8, local copies, waits for them, and re-layouts: 1.99 us -> 0.02 us
  transfers between devices with their start and end apart: 2 -> 3, of which waited for: 1 -> 2; matrix products, arithmetic and copies ran while one was open for 1% -> 0% of each run, Pallas kernels for 6% -> 6%
where the time goes in v3:
time: 53 us; the launch traced here: 52.7 us
  blocking collectives  33.5 us (63%)
  Pallas kernels  10.2 us (19%)
  starting transfers between devices  4.2 us (8%)
  between operations  2.66 us (5%)
  waiting for transfers between devices  2.01 us (4%)
    all_to_all x2, blocking collectives, fused_shards(): received = lax.all_to_all(sent, 'seq', 0, 0, axis_index_groups=same_core)  22.4 us
    all_to_all x1, blocking collectives, fused_shards(): received = lax.all_to_all(sent, 'seq', 0, 0)  11.1 us
    pallas_call x8, Pallas kernels, run(): return grid_free(*placed)  10.2 us
    ppermute x1, starting transfers between devices, fused_shards(): other = lax.ppermute(group_conv, 'seq', swap)  4.13 us
    ppermute x1, waiting for transfers between devices, fused_shards(): taken = lax.ppermute(give, 'seq', cores)  1.45 us
  transfers between devices with their start and end apart: 3, of which 2 were waited for; matrix products, arithmetic and copies ran while one was open for 0% of the time, Pallas kernels for 6%

profile of v3, /device:TPU:0, one launch (start us, length us, event | category | flops | bytes accessed | tf_op | source)
XLA Modules:
  0.0 52.7 jit_solution(9883143619059929515)
XLA Ops:
  0.6 0.0 copy-start
  0.6 1.8 %shard_map.220 = (bf16[8,128]{1,0:T(8,128)(2,1)S(1)}, bf16[8,4096]{1,0:T(8,128)(2,1)S(1)}) custom-call(bf16[8,4096]{1,0:T(8,128)(2,1)} %refs_5_.1, f32[1,4096]{1,0:T(1,128)} %bitcast.17, bf16[4096,128]{1,0:T(8,128)(2,1)} %weights_far.1, bf16[3,8,128]{2,1,0:T(8,128)(2,1)} %bitcast.19, f32[5,128]{1,0:T(8,128)} %taps_far.1), custom_call_target="tpu_custom_call" | custom-call | tf_op jit(solution)/shard_map/pallas_call | solution.py:257
  2.5 4.1 %collective-permute-start = (bf16[8,128]{1,0:T(8,128)(2,1)S(1)}, bf16[8,128]{1,0:T(8,128)(2,1)S(1)}, u32[]{:S(2)}, u32[]{:S(2)}) collective-permute-start(bf16[8,128]{1,0:T(8,128)(2,1)S(1)} %get-tuple-element.21.own), channel_id=1, source_target_pairs={{0,8},{1,9},{2,10},{3,11},{4,12},{5,13},{6,14},{7,15},{8,0},{9,1},... | collective-permute-start | bytes 6152 | tf_op jit(solution)/shard_map/ppermute | solution.py:689
  8.5 0.1 pad_maximum_fusion.refs_4_
  8.6 2.4 %shard_map.221 = (f32[8,64]{1,0:T(8,128)S(1)}, f32[8,128]{1,0:T(8,128)S(1)}, f32[8,128]{1,0:T(8,128)S(1)}, f32[8,128]{1,0:T(8,128)S(1)}, bf16[8,256]{1,0:T(8,128...) custom-call(s32[1]{0:T(128)} %bitcast.position, ...), custom_call_target="tpu_custom_call" | custom-call | tf_op jit(solution)/shard_map/pallas_call | solution.py:257
  11.0 0.0 copy-start.2
  11.0 0.0 collective-permute-done.other
  11.0 0.7 %shard_map.222 = bf16[16,8,384]{2,1,0:T(8,128)(2,1)S(1)} custom-call(s32[1]{0:T(128)} %bitcast.position, bf16[8,128]{1,0:T(8,128)(2,1)S(1)} %get-tuple-element.21.own, bf16[8,128]{1,0:T(8,128)(2,1)S(1)} %collective-permute-done.other, f32[8,64]{1,0:T(8,128)S(1)} %get-tuple-element.23.gate, f32[8,128]{1,0:T(8,128)S(1)} %get-tuple-element.24.conv, ...), custom_call_target="tpu_custom_call" | custom-call | tf_op jit(solution)/shard_map/pallas_call | solution.py:257
  11.7 11.1 %all_to_all.15.received = bf16[16,8,384]{2,1,0:T(8,128)(2,1)S(1)} all-to-all(bf16[16,8,384]{2,1,0:T(8,128)(2,1)S(1)} %shard_map.222), channel_id=1, replica_groups=mesh['grp'=2,'seq'=16] {'seq'}, dimensions={0} | all-to-all | bytes 196608 | tf_op jit(solution)/shard_map/all_to_all | solution.py:724
  22.8 0.0 copy-done
  22.8 0.0 copy-start.1
  22.8 0.0 copy-start.3
  22.8 0.8 %shard_map.223 = (f32[8,8,1664]{2,1,0:T(8,128)S(1)}, bf16[8,8,1664]{2,1,0:T(8,128)(2,1)S(1)}, f32[8,256]{1,0:T(8,128)S(1)}) custom-call(s32[1]{0:T(128)} %bitcast.position, bf16[16,8,384]{2,1,0:T(8,128)(2,1)S(1)} %all_to_all.15.received, bf16[8,256]{1,0:T(8,128)(2,1)S(1)} %get-tuple-element.30.hidden, f32[1,256]{1,0:T(1,128)S(1)} %get-tuple-element.31.gain, ...), custom_call_target="tpu_custom_call" | custom-call | tf_op jit(solution)/shard_map/pallas_call | solution.py:257
  23.6 0.1 collective-permute-start.1
  23.7 1.5 %collective-permute-done.1.taken = bf16[8,8,1664]{2,1,0:T(8,128)(2,1)S(1)} collective-permute-done((bf16[8,8,1664]{2,1,0:T(8,128)(2,1)S(1)}, bf16[8,8,1664]{2,1,0:T(8,128)(2,1)S(1)}, u32[]{:S(2)}, u32[]{:S(2)}) %collective-permute-start.1) | collective-permute-done | bytes 213024 | tf_op jit(solution)/shard_map/ppermute | solution.py:738
  25.2 0.2 shard_map.224
  25.4 11.2 %all_to_all.16.received = bf16[8,8,1664]{2,1,0:T(8,128)(2,1)S(1)} all-to-all(bf16[8,8,1664]{2,1,0:T(8,128)(2,1)S(1)} %shard_map.224), channel_id=1, replica_groups={{0,2,4,6,8,10,12,14},{1,3,5,7,9,11,13,15},{16,18,20,22,24,26,28,30},{17..., dimensions={0} | all-to-all | bytes 425984 | tf_op jit(solution)/shard_map/all_to_all | solution.py:740
  36.5 0.0 copy-done.2
  36.5 1.0 %shard_map.225 = bf16[8,104,128]{2,1,0:T(8,128)(2,1)S(1)} custom-call(s32[1]{0:T(128)} %bitcast.position, bf16[8,8,1664]{2,1,0:T(8,128)(2,1)S(1)} %all_to_all.16.received, bf16[2,128,2048]{2,1,0:T(8,128)(2,1)S(1)} %copy-done.2, s32[4,8]{1,0:T(4,128)S(1)} %get-tuple-element.32.table, s32[1,8]{1,0:T(1,128)S(1)} %get-tuple-element.35.lengths), custom_call_target="tpu_custom_call" | custom-call | tf_op jit(solution)/shard_map/pallas_call | solution.py:257
  37.6 11.2 %all_to_all.17.near = bf16[8,104,128]{2,1,0:T(8,128)(2,1)S(1)} all-to-all(bf16[8,104,128]{2,1,0:T(8,128)(2,1)S(1)} %shard_map.225), channel_id=1, replica_groups={{0,2,4,6,8,10,12,14},{1,3,5,7,9,11,13,15},{16,18,20,22,24,26,28,30},{17..., dimensions={0} | all-to-all | bytes 425984 | tf_op jit(solution)/shard_map/all_to_all | solution.py:748
  48.8 0.0 collective-permute-start.2
  48.8 0.9 %shard_map.227 = f32[8,64,128]{2,1,0:T(8,128)} custom-call(s32[1]{0:T(128)} %bitcast.position, bf16[8,128]{1,0:T(8,128)(2,1)S(1)} %get-tuple-element.21.own, bf16[8,128]{1,0:T(8,128)(2,1)S(1)} %collective-permute-done.other, f32[8,128]{1,0:T(8,128)S(1)} %get-tuple-element.24.conv, f32[8,128]{1,0:T(8,128)S(1)} %get-tuple-element.25.step, ...), custom_call_target="tpu_custom_call" | custom-call | tf_op jit(solution)/shard_map/pallas_call | solution.py:257
  49.7 0.6 %collective-permute-done.2.far = bf16[8,104,128]{2,1,0:T(8,128)(2,1)S(1)} collective-permute-done((bf16[8,104,128]{2,1,0:T(8,128)(2,1)S(1)}, bf16[8,104,128]{2,1,0:T(8,128)(2,1)S(1)}, u32[]{:S(2)}, u32[]{:S(2)}) %collective-permute-start.2) | collective-permute-done | bytes 213024 | tf_op jit(solution)/shard_map/ppermute | solution.py:749
  50.3 0.0 copy-done.1
  50.3 0.0 copy-done.3
  50.3 2.4 %shard_map.226 = (bf16[8,256]{1,0:T(8,128)(2,1)}, bf16[8,2048]{1,0:T(8,128)(2,1)}) custom-call(s32[1]{0:T(128)} %bitcast.position, s32[4,8]{1,0:T(4,128)S(1)} %bitcast.14, bf16[8,104,128]{2,1,0:T(8,128)(2,1)S(1)} %all_to_all.17.near, bf16[8,104,128]{2,1,0:T(8,128)(2,1)S(1)} %collective-permute-done.2.far, bf16[4096,256]{1,0:T(8,128)(2,1)S(1)} %copy-done.1, ...), custom_call_target="tpu_custom_call" | custom-call | tf_op jit(solution)/shard_map/pallas_call | solution.py:257
Async XLA Ops:
  0.6 22.1 %copy-start = (bf16[256,6144]{1,0:T(8,128)(2,1)S(1)}, bf16[256,6144]{1,0:T(8,128)(2,1)}, u32[]{:S(2)}) copy-start(bf16[256,6144]{1,0:T(8,128)(2,1)} %weights.2) | copy-start | bytes 9437188
  2.5 8.5 %collective-permute-start = (bf16[8,128]{1,0:T(8,128)(2,1)S(1)}, bf16[8,128]{1,0:T(8,128)(2,1)S(1)}, u32[]{:S(2)}, u32[]{:S(2)}) collective-permute-start(bf16[8,128]{1,0:T(8,128)(2,1)S(1)} %get-tuple-element.21.own), channel_id=1, source_target_pairs={{0,8},{1,9},{2,10},{3,11},{4,12},{5,13},{6,14},{7,15},{8,0},{9,1},... | collective-permute-start | bytes 6152 | tf_op jit(solution)/shard_map/ppermute | solution.py:689
  11.0 25.6 %copy-start.2 = (bf16[2,128,2048]{2,1,0:T(8,128)(2,1)S(1)}, bf16[2,128,2048]{2,1,0:T(8,128)(2,1)}, u32[]{:S(2)}) copy-start(bf16[2,128,2048]{2,1,0:T(8,128)(2,1)} %cache.1) | copy-start | bytes 3145732
  22.8 27.5 %copy-start.1 = (bf16[4096,256]{1,0:T(8,128)(2,1)S(1)}, bf16[4096,256]{1,0:T(8,128)(2,1)}, u32[]{:S(2)}) copy-start(bf16[4096,256]{1,0:T(8,128)(2,1)} %weights.3) | copy-start | bytes 6291460
  22.8 27.5 %copy-start.3 = (s32[8,4]{0,1:T(4,128)S(1)}, s32[8,4]{0,1:T(4,128)}, u32[]{:S(2)}) copy-start(s32[8,4]{0,1:T(4,128)} %param.40) | copy-start | bytes 388
  23.6 1.5 %collective-permute-start.1 = (bf16[8,8,1664]{2,1,0:T(8,128)(2,1)S(1)}, bf16[8,8,1664]{2,1,0:T(8,128)(2,1)S(1)}, u32[]{:S(2)}, u32[]{:S(2)}) collective-permute-start(bf16[8,8,1664]{2,1,0:T(8,128)(2,1)S(1)} %get-tuple-element.34), channel_id=1, source_target_pairs={{0,1},{1,0},{2,3},{3,2},{4,5},{5,4},{6,7},{7,6},{8,9},{9,8},{10,11... | collective-permute-start | bytes 638984 | tf_op jit(solution)/shard_map/ppermute | solution.py:738
  48.8 1.5 %collective-permute-start.2 = (bf16[8,104,128]{2,1,0:T(8,128)(2,1)S(1)}, bf16[8,104,128]{2,1,0:T(8,128)(2,1)S(1)}, u32[]{:S(2)}, u32[]{:S(2)}) collective-permute-start(bf16[8,104,128]{2,1,0:T(8,128)(2,1)S(1)} %all_to_all.17.near), channel_id=1, source_target_pairs={{0,1},{1,0},{2,3},{3,2},{4,5},{5,4},{6,7},{7,6},{8,9},{9,8},{10,11... | collective-permute-start | bytes 638984 | tf_op jit(solution)/shard_map/ppermute | solution.py:749

commit v4 on v3

--- a/solution.py
+++ b/solution.py
@@ -231,6 +231,7 @@
 SUB = 8
 PARTS = 3
 SCOPED = 16 << 20
+MOST = 63500 << 10
 BLOCKS = 4
 VMEM = pl.BlockSpec(memory_space=pltpu.VMEM)
 NEAR = pl.BlockSpec(memory_space=pltpu.VMEM)
@@ -238,14 +239,14 @@
 FAR = pl.BlockSpec(memory_space=pltpu.HBM)
 
 
-def call(kernel, outs, specs, scratch=()):
+def call(kernel, outs, specs, scratch=(), scoped=SCOPED):
     grid_free = pl.pallas_call(
         kernel,
         out_shape=outs,
         in_specs=specs,
         out_specs=jax.tree.map(lambda _: VMEM, outs, is_leaf=lambda x: hasattr(x, "shape")),
         scratch_shapes=scratch,
-        compiler_params=pltpu.CompilerParams(vmem_limit_bytes=SCOPED),
+        compiler_params=pltpu.CompilerParams(vmem_limit_bytes=scoped),
     )
 
     def run(*args):
@@ -280,12 +281,16 @@
     return out
 
 
-def marked(value, parts):
+def marked(value, parts, first=0):
     lane = lax.broadcasted_iota(jnp.int32, (value.shape[0], LANES), 1)
     out = jnp.zeros((value.shape[0], LANES), f32)
     for k, piece in enumerate(pieces(value, parts)):
-        out = jnp.where(lane == k, piece, out)
+        out = jnp.where(lane == first + k, piece, out)
     return out
+
+
+def summed(marks, first=0):
+    return marks[:, first : first + 1] + marks[:, first + 1 : first + 2]
 
 
 def convolve(state_ref, fresh, taps_ref):
@@ -445,8 +450,9 @@
         mixer = mixer + scale * products
     middle = (hidden[...].astype(f32) + mixer).astype(bf16).astype(f32)
     middle_out[...] = middle
-    marks = marked(jnp.sum(middle * middle, axis=-1, keepdims=True), 2)
-    extended = jnp.concatenate([middle * gain[...], marks], axis=-1).astype(bf16)
+    square = jnp.sum(middle * middle, axis=-1, keepdims=True)
+    scaled = middle * gain[...]
+    extended = jnp.concatenate([scaled, marked(square, 2)], axis=-1).astype(bf16)
     rows = count * SUB
     pages = SUB // chunks
     chips = count // 2
@@ -462,48 +468,67 @@
     spread = jnp.dot(onehot, extended, preferred_element_type=f32)
     lines = spread[:, :columns]
     which = (lax.broadcasted_iota(jnp.int32, lines.shape, 0) % SUB) // pages
-    lhs = [jnp.where(which == c, lines, 0.0).astype(bf16) for c in range(chunks)]
     chunk = weights.shape[1] // chunks
-    tile = 256
+    fresh_from = QH * HD
+    zeros = jnp.zeros((SUB, columns), f32)
+    lhs = []
+    for c in range(chunks):
+        own = jnp.where(which == c, lines, 0.0)
+        if (c + 1) * chunk > fresh_from:
+            own = jnp.concatenate([own, scaled, zeros], axis=0)
+        lhs.append(own.astype(bf16))
+    tile = 2 * HD
     for n in range(0, chunk, tile):
         total = None
         for c in range(chunks):
-            part = jnp.dot(
-                lhs[c],
-                weights[:, c * chunk + n : c * chunk + n + tile],
-                preferred_element_type=f32,
-            )
-            total = part if total is None else total + part
+            first = c * chunk + n
+            part = jnp.dot(lhs[c], weights[:, first : first + tile], preferred_element_type=f32)
+            if first >= fresh_from:
+                fresh = part[rows : rows + SUB]
+                chip = (first - fresh_from) // tile
+                low, high = fresh[:, :HD], fresh[:, HD:]
+                keep[chip, :, chunk + LANES :] = jnp.where(core == 0, low, high)
+                give[chip, :, chunk + LANES :] = jnp.where(core == 0, high, low).astype(bf16)
+            total = part[:rows] if total is None else total + part[:rows]
         for e in range(chips):
             keep[e, :, n : n + tile] = total[e * SUB : (e + 1) * SUB]
             first = (chips + e) * SUB
             give[e, :, n : n + tile] = total[first : first + SUB].astype(bf16)
+    marks = spread[:, columns:]
+    request_marks = marked(square, 2, 2)
     for e in range(chips):
-        keep[e, :, chunk:] = spread[e * SUB : (e + 1) * SUB, columns:]
+        keep[e, :, chunk : chunk + LANES] = marks[e * SUB : (e + 1) * SUB] + request_marks
         first = (chips + e) * SUB
-        give[e, :, chunk:] = spread[first : first + SUB, columns:].astype(bf16)
-
-
-def pair_kernel(keep, taken, sent):
-    chunk = keep.shape[2] - LANES
+        give[e, :, chunk : chunk + LANES] = (marks[first : first + SUB] + request_marks).astype(
+            bf16
+        )
+
+
+def pair_kernel(keep, taken, _, sent):
+    chunk = keep.shape[2] - 2 * LANES
     for e in range(keep.shape[0]):
         total = keep[e] + taken[e].astype(f32)
-        marks = total[:, chunk : chunk + 1] + total[:, chunk + 1 : chunk + 2]
+        marks = total[:, chunk : chunk + LANES]
         sent[e, :, :chunk] = total[:, :chunk].astype(bf16)
-        sent[e, :, chunk:] = marked(marks, 2).astype(bf16)
+        sent[e, :, chunk : chunk + LANES] = (
+            marked(summed(marks), 2) + marked(summed(marks, 2), 2, 2)
+        ).astype(bf16)
+        sent[e, :, chunk + LANES :] = total[:, chunk + LANES :].astype(bf16)
 
 
 def attend_kernel(width, position, received, cache, table, lengths, sent, lines):
     count, _, full = received.shape
     pages, page_len, _ = cache.shape
     chunks = SUB // pages
-    chunk = full - LANES
+    chunk = full - 2 * LANES
     tiles = chunk // HD
     total = received[0].astype(f32)
     for k in range(1, count):
         total = total + received[k].astype(f32)
-    squares = total[:, chunk : chunk + 1] + total[:, chunk + 1 : chunk + 2]
-    inverse = lax.rsqrt(squares / width + epsilon)
+    marks = total[:, chunk : chunk + LANES]
+    inverse = lax.rsqrt(summed(marks) / width + epsilon)
+    fresh = total[:, chunk + LANES :] * lax.rsqrt(summed(marks, 2) / width + epsilon)
+    fresh = fresh.astype(bf16)
     for t in range(tiles):
         lines[t * SUB : (t + 1) * SUB, :] = (
             (total[:, t * HD : (t + 1) * HD] * inverse).astype(bf16).astype(f32)
@@ -521,7 +546,6 @@
     eye_lane = lax.broadcasted_iota(jnp.int32, (QH, LANES), 1)
     order = lax.broadcasted_iota(jnp.int32, table.shape, 0)
     value_rows = pages * QH
-    fresh_rows = 2 * KVH
     log_row = jnp.zeros((1, LANES), f32)
     for p in range(pages):
         slot = position[0] * pages + p
@@ -561,74 +585,96 @@
         wide = jnp.dot(
             weights.astype(bf16), cache[p, :, KVH * HD :], preferred_element_type=f32
         )
-        summed = own_weight * value_own
+        mixed = own_weight * value_own
         for g in range(KVH):
-            summed = summed + jnp.where(head_group == g, wide[:, g * HD : (g + 1) * HD], 0.0)
+            mixed = mixed + jnp.where(head_group == g, wide[:, g * HD : (g + 1) * HD], 0.0)
         some = mass > 0.0
         safe = jnp.where(some, mass, 1.0)
-        result = (summed / safe).astype(bf16)
+        result = (mixed / safe).astype(bf16)
         logs = jnp.where(some, peak + jnp.log(safe), lowest)
         log_row = log_row + jnp.sum(
             jnp.where(eye_lane == eye + p * QH, logs, 0.0), axis=0, keepdims=True
         )
-        fresh = jnp.concatenate(keys + values, axis=0).astype(bf16)
         for e in range(count):
             sent[e, p * QH : (p + 1) * QH, :] = result
-            first = value_rows + p * fresh_rows
-            sent[e, first : first + fresh_rows, :] = fresh
     terms = pieces(log_row, PARTS) + [jnp.zeros((SUB - PARTS, LANES), f32)]
     terms = jnp.concatenate(terms, axis=0).astype(bf16)
     for e in range(count):
-        sent[e, value_rows + pages * fresh_rows :, :] = terms
+        sent[e, value_rows : value_rows + SUB, :] = fresh
+        sent[e, value_rows + SUB :, :] = terms
 
 
 def merge_kernel(
-    pages, position, table, near, far, weights, middle, final, new_kv, spread, rows, fresh
+    pages, position, table, near_ref, far_ref, weights, middle, final, new_kv, scaled, rows
 ):
-    chips, package, _ = near.shape
+    chips = near_ref.shape[0]
     pages_req, requests = table.shape
     value_rows = pages * QH
-    kv_rows = 2 * KVH
-    last = value_rows + pages * kv_rows
-    source = lax.broadcasted_iota(jnp.int32, (chips * SUB, LANES), 0) // SUB
-    masks = [jnp.where(source == k, 1.0, 0.0).astype(bf16) for k in range(chips)]
-    for side, packages in enumerate((near, far)):
-        logs = jnp.concatenate([packages[k, last:, :] for k in range(chips)], axis=0)
-        for k in range(chips):
-            spread[side * chips + k] = lax.dot_general(
-                logs, masks[k], (((0,), (0,)), ((), ())), preferred_element_type=f32
-            )
     core = position[0] % 2
-
-    def fetch(chip, side, first, many):
-        both = near[chip, pl.ds(first, many), :], far[chip, pl.ds(first, many), :]
-        return jnp.where(side == 0, both[0].astype(f32), both[1].astype(f32))
-
+    packages = (near_ref, far_ref)
+    logs = jnp.concatenate(
+        [
+            jnp.sum(ref[:, value_rows + SUB :, :].astype(f32), axis=1)
+            for ref in packages
+        ],
+        axis=0,
+    )
+    row = lax.broadcasted_iota(jnp.int32, logs.shape, 0)
+    slot = lax.broadcasted_iota(jnp.int32, logs.shape, 1) // QH
+    parity = jnp.where(row < chips, core, 1 - core)
+    page = jnp.where(slot < pages, ((row % chips) * 2 + parity) * pages + slot, -1)
+    hits = []
     for r in range(requests):
-        peaks, values = [], []
+        hit = page == table[0, r]
+        for j in range(1, pages_req):
+            hit = jnp.logical_or(hit, page == table[j, r])
+        hits.append(hit)
+
+    def over_slots(value, combine):
+        out = value
+        for k in range(1, pages):
+            out = combine(out, pltpu.roll(value, k * QH, 1))
+            out = combine(out, pltpu.roll(value, LANES - k * QH, 1))
+        return out
+
+    def back(per_request):
+        out = jnp.zeros(logs.shape, f32)
+        for r in range(requests):
+            out = jnp.where(hits[r], per_request[r : r + 1, :], out)
+        return out
+
+    tops = jnp.concatenate(
+        [jnp.max(jnp.where(hit, logs, lowest), axis=0, keepdims=True) for hit in hits], axis=0
+    )
+    factors = jnp.exp(jnp.where(slot < pages, logs - back(over_slots(tops, jnp.maximum)), lowest))
+    masses = jnp.concatenate(
+        [jnp.sum(jnp.where(hit, factors, 0.0), axis=0, keepdims=True) for hit in hits], axis=0
+    )
+    masses = over_slots(masses, jnp.add)
+    inverse = 1.0 / jnp.where(masses > 0.0, masses, 1.0)
+    shares = factors * back(inverse)
+    turned = jnp.concatenate([shares, jnp.zeros((LANES - 2 * chips, LANES), f32)], axis=0).T
+    for side, ref in enumerate(packages):
+        for chip in range(chips):
+            device = side * chips + chip
+            scaled[device] = ref[chip, :value_rows, :].astype(f32) * turned[
+                :value_rows, device : device + 1
+            ]
+    for r in range(requests):
+        total = None
         for j in range(pages_req):
-            page = table[j, r]
-            device, slot = page // pages, page % pages
-            chip = device // 2
+            device = lax.div(table[j, r], pages)
             side = lax.rem(device + core, 2)
-            first = pl.multiple_of(slot * QH, QH)
-            peaks.append(spread[side * chips + chip, pl.ds(first, QH), :])
-            values.append(fetch(chip, side, first, QH))
-            if j == 0:
-                first = pl.multiple_of(value_rows + slot * kv_rows, kv_rows)
-                fresh[r * kv_rows : (r + 1) * kv_rows, :] = fetch(chip, side, first, kv_rows)
-        top = functools.reduce(jnp.maximum, peaks)
-        mass = jnp.zeros(top.shape, f32)
-        summed = jnp.zeros(top.shape, f32)
-        for peak, value in zip(peaks, values):
-            factor = jnp.exp(peak - top)
-            mass = mass + factor
-            summed = summed + factor * value
-        rows[r * QH : (r + 1) * QH, :] = summed / mass
-    for c in range(kv_rows):
-        new_kv[:, c * HD : (c + 1) * HD] = fresh[pl.ds(c, requests, stride=kv_rows), :].astype(
-            bf16
-        )
+            place = side * chips + lax.div(device, 2)
+            first = pl.multiple_of(lax.rem(table[j, r], pages) * QH, QH)
+            part = scaled[place, pl.ds(first, QH), :]
+            total = part if total is None else total + part
+        rows[r * QH : (r + 1) * QH, :] = total
+    for chip in range(chips):
+        mine, theirs = (ref[chip, value_rows : value_rows + SUB, :].astype(f32) for ref in packages)
+        first = 2 * chip * HD
+        new_kv[:, first : first + HD] = jnp.where(core == 0, mine, theirs).astype(bf16)
+        new_kv[:, first + HD : first + 2 * HD] = jnp.where(core == 0, theirs, mine).astype(bf16)
     attended = jnp.concatenate(
         [rows[pl.ds(h, requests, stride=QH), :].astype(bf16) for h in range(QH)], axis=-1
     )
@@ -684,6 +730,7 @@
         [FAR] * 5,
         [pltpu.VMEM(x.shape, x.dtype) for x in group_args]
         + [pltpu.SemaphoreType.DMA((len(group_args) - 1 + BLOCKS,))],
+        MOST,
     )(*group_args)
     swap = [(i, (i + GROUPS) % count) for i in range(count)]
     other = lax.ppermute(group_conv, "seq", swap)
@@ -729,16 +776,16 @@
     keep, give, middle = call(
         functools.partial(project_kernel, chunks, head_width),
         (
-            near((chips, SUB, chunk + LANES), f32),
-            near((chips, SUB, chunk + LANES), bf16),
+            near((chips, SUB, chunk + 2 * LANES), f32),
+            near((chips, SUB, chunk + 2 * LANES), bf16),
             near((requests, columns), f32),
         ),
         [SMEM] + [NEAR] * 5,
     )(position, received, stream, scale, w_qkv, table)
     taken = lax.ppermute(give, "seq", cores)
-    sent = call(pair_kernel, near(give.shape, bf16), [NEAR] * 2)(keep, taken)
+    sent = call(pair_kernel, near(give.shape, bf16), [NEAR] * 2 + [FAR])(keep, taken, new_state)
     received = lax.all_to_all(sent, "seq", 0, 0, axis_index_groups=same_core)
-    package = pages * (QH + 2 * KVH) + SUB
+    package = pages * QH + 2 * SUB
     sent = call(
         functools.partial(attend_kernel, width),
         near((chips, package, HD), bf16),
@@ -755,9 +802,8 @@
         ),
         [SMEM] * 2 + [NEAR] * 4,
         [
-            pltpu.VMEM((count, LANES, LANES), f32),
+            pltpu.VMEM((count, pages * QH, HD), f32),
             pltpu.VMEM((requests * QH, HD), f32),
-            pltpu.VMEM((requests * 2 * KVH, HD), f32),
         ],
     )(position, page_table.T, received, far, w_out, middle)
     return (final, new_state.reshape(ssm_state.shape), new_kv)
@@ -776,6 +822,7 @@
         and SUB % kv_cache.shape[0] == 0
         and kv_cache.shape[0] * QH <= LANES
         and kv_cache.shape[1] == LANES
+        and 2 * KVH == count
     )
     return (fused_shards if whole_tiles else plain_shards)(*args)
 

time: 53 us -> 52.4 us (0.989)
    ppermute x1, waiting for transfers between devices: 1.45 us -> 0.56 us  [fused_shards(): taken = lax.ppermute(give, 'seq', cores)]
    ppermute x1, waiting for transfers between devices: 0.55 us -> 1.39 us  [fused_shards(): far = lax.ppermute(received, 'seq', cores)]
where the time goes in v4:
time: 52.4 us; the launch traced here: 52.1 us
  blocking collectives  33.2 us (63%)
  Pallas kernels  10 us (19%)
  starting transfers between devices  4.2 us (8%)
  between operations  2.66 us (5%)
  waiting for transfers between devices  1.96 us (4%)
    all_to_all x2, blocking collectives, fused_shards(): received = lax.all_to_all(sent, 'seq', 0, 0, axis_index_groups=same_core)  22.1 us
    all_to_all x1, blocking collectives, fused_shards(): received = lax.all_to_all(sent, 'seq', 0, 0)  11.1 us
    pallas_call x8, Pallas kernels, run(): return grid_free(*placed)  10 us
    ppermute x1, starting transfers between devices, fused_shards(): other = lax.ppermute(group_conv, 'seq', swap)  4.13 us
    ppermute x1, waiting for transfers between devices, fused_shards(): far = lax.ppermute(received, 'seq', cores)  1.39 us
  transfers between devices with their start and end apart: 3, of which 2 were waited for; matrix products, arithmetic and copies ran while one was open for 0% of the time, Pallas kernels for 6%

profile of v4, /device:TPU:0, one launch (start us, length us, event | category | flops | bytes accessed | tf_op | source)
XLA Modules:
  0.0 52.1 jit_solution(11322253960398296320)
XLA Ops:
  0.6 1.7 %shard_map.220 = (bf16[8,128]{1,0:T(8,128)(2,1)S(1)}, bf16[8,4096]{1,0:T(8,128)(2,1)S(1)}) custom-call(bf16[8,4096]{1,0:T(8,128)(2,1)} %refs_5_.1, f32[1,4096]{1,0:T(1,128)} %bitcast.17, bf16[4096,128]{1,0:T(8,128)(2,1)} %weights_far.1, bf16[3,8,128]{2,1,0:T(8,128)(2,1)} %bitcast.19, f32[5,128]{1,0:T(8,128)} %taps_far.1), custom_call_target="tpu_custom_call" | custom-call | tf_op jit(solution)/shard_map/pallas_call | solution.py:258
  2.3 0.0 copy-start
  2.3 4.1 %collective-permute-start = (bf16[8,128]{1,0:T(8,128)(2,1)S(1)}, bf16[8,128]{1,0:T(8,128)(2,1)S(1)}, u32[]{:S(2)}, u32[]{:S(2)}) collective-permute-start(bf16[8,128]{1,0:T(8,128)(2,1)S(1)} %get-tuple-element.21.own), channel_id=1, source_target_pairs={{0,8},{1,9},{2,10},{3,11},{4,12},{5,13},{6,14},{7,15},{8,0},{9,1},... | collective-permute-start | bytes 6152 | tf_op jit(solution)/shard_map/ppermute | solution.py:736
  8.4 0.1 pad_maximum_fusion.refs_4_
  8.5 2.4 %shard_map.221 = (f32[8,64]{1,0:T(8,128)S(1)}, f32[8,128]{1,0:T(8,128)S(1)}, f32[8,128]{1,0:T(8,128)S(1)}, f32[8,128]{1,0:T(8,128)S(1)}, bf16[8,256]{1,0:T(8,128...) custom-call(s32[1]{0:T(128)} %bitcast.position, ...), custom_call_target="tpu_custom_call" | custom-call | tf_op jit(solution)/shard_map/pallas_call | solution.py:258
  10.8 0.0 collective-permute-done.other
  10.8 0.0 copy-start.2
  10.9 0.7 %shard_map.222 = bf16[16,8,384]{2,1,0:T(8,128)(2,1)S(1)} custom-call(s32[1]{0:T(128)} %bitcast.position, bf16[8,128]{1,0:T(8,128)(2,1)S(1)} %get-tuple-element.21.own, bf16[8,128]{1,0:T(8,128)(2,1)S(1)} %collective-permute-done.other, f32[8,64]{1,0:T(8,128)S(1)} %get-tuple-element.23.gate, f32[8,128]{1,0:T(8,128)S(1)} %get-tuple-element.24.conv, ...), custom_call_target="tpu_custom_call" | custom-call | tf_op jit(solution)/shard_map/pallas_call | solution.py:258
  11.6 11.1 %all_to_all.15.received = bf16[16,8,384]{2,1,0:T(8,128)(2,1)S(1)} all-to-all(bf16[16,8,384]{2,1,0:T(8,128)(2,1)S(1)} %shard_map.222), channel_id=1, replica_groups=mesh['grp'=2,'seq'=16] {'seq'}, dimensions={0} | all-to-all | bytes 196608 | tf_op jit(solution)/shard_map/all_to_all | solution.py:771
  22.6 0.0 copy-done
  22.6 0.0 copy-start.1
  22.6 0.0 copy-start.3
  22.6 0.9 %shard_map.223 = (f32[8,8,1792]{2,1,0:T(8,128)S(1)}, bf16[8,8,1792]{2,1,0:T(8,128)(2,1)S(1)}, f32[8,256]{1,0:T(8,128)S(1)}) custom-call(s32[1]{0:T(128)} %bitcast.position, bf16[16,8,384]{2,1,0:T(8,128)(2,1)S(1)} %all_to_all.15.received, bf16[8,256]{1,0:T(8,128)(2,1)S(1)} %get-tuple-element.30.hidden, f32[1,256]{1,0:T(1,128)S(1)} %get-tuple-element.31.gain, ...), custom_call_target="tpu_custom_call" | custom-call | tf_op jit(solution)/shard_map/pallas_call | solution.py:258
  23.5 0.1 collective-permute-start.1
  23.6 0.9 %shard_map.224._ = f32[8,64,128]{2,1,0:T(8,128)} custom-call(s32[1]{0:T(128)} %bitcast.position, bf16[8,128]{1,0:T(8,128)(2,1)S(1)} %get-tuple-element.21.own, bf16[8,128]{1,0:T(8,128)(2,1)S(1)} %collective-permute-done.other, f32[8,128]{1,0:T(8,128)S(1)} %get-tuple-element.24.conv, f32[8,128]{1,0:T(8,128)S(1)} %get-tuple-element.25.step, ...), custom_call_target="tpu_custom_call" | custom-call | tf_op jit(solution)/shard_map/pallas_call | solution.py:258
  24.5 0.6 %collective-permute-done.1.taken = bf16[8,8,1792]{2,1,0:T(8,128)(2,1)S(1)} collective-permute-done((bf16[8,8,1792]{2,1,0:T(8,128)(2,1)S(1)}, bf16[8,8,1792]{2,1,0:T(8,128)(2,1)S(1)}, u32[]{:S(2)}, u32[]{:S(2)}) %collective-permute-start.1) | collective-permute-done | bytes 229408 | tf_op jit(solution)/shard_map/ppermute | solution.py:785
  25.0 0.2 shard_map.225
  25.2 11.4 %all_to_all.16.received = bf16[8,8,1792]{2,1,0:T(8,128)(2,1)S(1)} all-to-all(bf16[8,8,1792]{2,1,0:T(8,128)(2,1)S(1)} %shard_map.225), channel_id=1, replica_groups={{0,2,4,6,8,10,12,14},{1,3,5,7,9,11,13,15},{16,18,20,22,24,26,28,30},{17..., dimensions={0} | all-to-all | bytes 458752 | tf_op jit(solution)/shard_map/all_to_all | solution.py:787
  36.7 0.0 copy-done.2
  36.7 1.1 %shard_map.226 = bf16[8,80,128]{2,1,0:T(8,128)(2,1)S(1)} custom-call(s32[1]{0:T(128)} %bitcast.position, bf16[8,8,1792]{2,1,0:T(8,128)(2,1)S(1)} %all_to_all.16.received, bf16[2,128,2048]{2,1,0:T(8,128)(2,1)S(1)} %copy-done.2, s32[4,8]{1,0:T(4,128)S(1)} %get-tuple-element.32.table, s32[1,8]{1,0:T(1,128)S(1)} %get-tuple-element.35.lengths), custom_call_target="tpu_custom_call" | custom-call | tf_op jit(solution)/shard_map/pallas_call | solution.py:258
  37.7 10.7 %all_to_all.17.near_ref = bf16[8,80,128]{2,1,0:T(8,128)(2,1)S(1)} all-to-all(bf16[8,80,128]{2,1,0:T(8,128)(2,1)S(1)} %shard_map.226), channel_id=1, replica_groups={{0,2,4,6,8,10,12,14},{1,3,5,7,9,11,13,15},{16,18,20,22,24,26,28,30},{17..., dimensions={0} | all-to-all | bytes 327680 | tf_op jit(solution)/shard_map/all_to_all | solution.py:795
  48.4 0.0 collective-permute-start.2
  48.5 1.4 %collective-permute-done.2.far_ref = bf16[8,80,128]{2,1,0:T(8,128)(2,1)S(1)} collective-permute-done((bf16[8,80,128]{2,1,0:T(8,128)(2,1)S(1)}, bf16[8,80,128]{2,1,0:T(8,128)(2,1)S(1)}, u32[]{:S(2)}, u32[]{:S(2)}) %collective-permute-start.2) | collective-permute-done | bytes 163872 | tf_op jit(solution)/shard_map/ppermute | solution.py:796
  49.8 0.0 copy-done.1
  49.8 0.0 copy-done.3
  49.9 2.3 %shard_map.227 = (bf16[8,256]{1,0:T(8,128)(2,1)}, bf16[8,2048]{1,0:T(8,128)(2,1)}) custom-call(s32[1]{0:T(128)} %bitcast.position, s32[4,8]{1,0:T(4,128)S(1)} %bitcast.14, bf16[8,80,128]{2,1,0:T(8,128)(2,1)S(1)} %all_to_all.17.near_ref, bf16[8,80,128]{2,1,0:T(8,128)(2,1)S(1)} %collective-permute-done.2.far_ref, bf16[4096,256]{1,0:T(8,128)(2,1)S(1)} %copy-done.1, ...), custom_call_target="tpu_custom_call" | custom-call | tf_op jit(solution)/shard_map/pallas_call | solution.py:258
Async XLA Ops:
  2.3 20.3 %copy-start = (bf16[256,6144]{1,0:T(8,128)(2,1)S(1)}, bf16[256,6144]{1,0:T(8,128)(2,1)}, u32[]{:S(2)}) copy-start(bf16[256,6144]{1,0:T(8,128)(2,1)} %weights.2) | copy-start | bytes 9437188
  2.3 8.5 %collective-permute-start = (bf16[8,128]{1,0:T(8,128)(2,1)S(1)}, bf16[8,128]{1,0:T(8,128)(2,1)S(1)}, u32[]{:S(2)}, u32[]{:S(2)}) collective-permute-start(bf16[8,128]{1,0:T(8,128)(2,1)S(1)} %get-tuple-element.21.own), channel_id=1, source_target_pairs={{0,8},{1,9},{2,10},{3,11},{4,12},{5,13},{6,14},{7,15},{8,0},{9,1},... | collective-permute-start | bytes 6152 | tf_op jit(solution)/shard_map/ppermute | solution.py:736
  10.8 25.8 %copy-start.2 = (bf16[2,128,2048]{2,1,0:T(8,128)(2,1)S(1)}, bf16[2,128,2048]{2,1,0:T(8,128)(2,1)}, u32[]{:S(2)}) copy-start(bf16[2,128,2048]{2,1,0:T(8,128)(2,1)} %cache.1) | copy-start | bytes 3145732
  22.6 27.2 %copy-start.1 = (bf16[4096,256]{1,0:T(8,128)(2,1)S(1)}, bf16[4096,256]{1,0:T(8,128)(2,1)}, u32[]{:S(2)}) copy-start(bf16[4096,256]{1,0:T(8,128)(2,1)} %weights.3) | copy-start | bytes 6291460
  22.6 27.2 %copy-start.3 = (s32[8,4]{0,1:T(4,128)S(1)}, s32[8,4]{0,1:T(4,128)}, u32[]{:S(2)}) copy-start(s32[8,4]{0,1:T(4,128)} %param.40) | copy-start | bytes 388
  23.5 1.6 %collective-permute-start.1 = (bf16[8,8,1792]{2,1,0:T(8,128)(2,1)S(1)}, bf16[8,8,1792]{2,1,0:T(8,128)(2,1)S(1)}, u32[]{:S(2)}, u32[]{:S(2)}) collective-permute-start(bf16[8,8,1792]{2,1,0:T(8,128)(2,1)S(1)} %get-tuple-element.34), channel_id=1, source_target_pairs={{0,1},{1,0},{2,3},{3,2},{4,5},{5,4},{6,7},{7,6},{8,9},{9,8},{10,11... | collective-permute-start | bytes 688136 | tf_op jit(solution)/shard_map/ppermute | solution.py:785
  48.4 1.4 %collective-permute-start.2 = (bf16[8,80,128]{2,1,0:T(8,128)(2,1)S(1)}, bf16[8,80,128]{2,1,0:T(8,128)(2,1)S(1)}, u32[]{:S(2)}, u32[]{:S(2)}) collective-permute-start(bf16[8,80,128]{2,1,0:T(8,128)(2,1)S(1)} %all_to_all.17.near_ref), channel_id=1, source_target_pairs={{0,1},{1,0},{2,3},{3,2},{4,5},{5,4},{6,7},{7,6},{8,9},{9,8},{10,11... | collective-permute-start | bytes 491528 | tf_op jit(solution)/shard_map/ppermute | solution.py:796

commit v5 on v4

--- a/solution.py
+++ b/solution.py
@@ -543,9 +543,10 @@
     lane = lax.broadcasted_iota(jnp.int32, (1, page_len), 1)
     head_group = lax.broadcasted_iota(jnp.int32, (QH, HD), 0) // group
     eye = lax.broadcasted_iota(jnp.int32, (QH, LANES), 0)
-    eye_lane = lax.broadcasted_iota(jnp.int32, (QH, LANES), 1)
+    value_rows = pages * QH
+    place = (position[0] // 2) % (LANES // value_rows) * value_rows
+    eye_lane = lax.broadcasted_iota(jnp.int32, (QH, LANES), 1) - place
     order = lax.broadcasted_iota(jnp.int32, table.shape, 0)
-    value_rows = pages * QH
     log_row = jnp.zeros((1, LANES), f32)
     for p in range(pages):
         slot = position[0] * pages + p
@@ -604,80 +605,75 @@
         sent[e, value_rows + SUB :, :] = terms
 
 
-def merge_kernel(
-    pages, position, table, near_ref, far_ref, weights, middle, final, new_kv, scaled, rows
-):
+def owner_kernel(chips, pages, position, table, _, owner):
+    pages_req, requests = table.shape
+    core = position[0] % 2
+    span = pages * QH
+    rows_each = owner.shape[0] // 2
+    row = lax.broadcasted_iota(jnp.int32, owner.shape, 0)
+    lane = lax.broadcasted_iota(jnp.int32, owner.shape, 1)
+    chip = (row % rows_each) * (LANES // span) + lane // span
+    parity = jnp.where(row < rows_each, core, 1 - core)
+    page = (chip * 2 + parity) * pages + (lane % span) // QH
+    found = jnp.zeros(owner.shape, jnp.int32)
+    for r in range(requests):
+        for j in range(pages_req):
+            found = jnp.where(page == table[j, r], r, found)
+    owner[...] = found
+
+
+def merge_kernel(pages, position, near_ref, far_ref, owner, weights, middle, final, new_kv):
     chips = near_ref.shape[0]
-    pages_req, requests = table.shape
+    requests, width = middle.shape
     value_rows = pages * QH
     core = position[0] % 2
     packages = (near_ref, far_ref)
-    logs = jnp.concatenate(
-        [
-            jnp.sum(ref[:, value_rows + SUB :, :].astype(f32), axis=1)
-            for ref in packages
-        ],
-        axis=0,
-    )
-    row = lax.broadcasted_iota(jnp.int32, logs.shape, 0)
-    slot = lax.broadcasted_iota(jnp.int32, logs.shape, 1) // QH
-    parity = jnp.where(row < chips, core, 1 - core)
-    page = jnp.where(slot < pages, ((row % chips) * 2 + parity) * pages + slot, -1)
-    hits = []
-    for r in range(requests):
-        hit = page == table[0, r]
-        for j in range(1, pages_req):
-            hit = jnp.logical_or(hit, page == table[j, r])
-        hits.append(hit)
-
-    def over_slots(value, combine):
-        out = value
-        for k in range(1, pages):
-            out = combine(out, pltpu.roll(value, k * QH, 1))
-            out = combine(out, pltpu.roll(value, LANES - k * QH, 1))
-        return out
-
-    def back(per_request):
-        out = jnp.zeros(logs.shape, f32)
-        for r in range(requests):
-            out = jnp.where(hits[r], per_request[r : r + 1, :], out)
-        return out
-
-    tops = jnp.concatenate(
-        [jnp.max(jnp.where(hit, logs, lowest), axis=0, keepdims=True) for hit in hits], axis=0
-    )
-    factors = jnp.exp(jnp.where(slot < pages, logs - back(over_slots(tops, jnp.maximum)), lowest))
-    masses = jnp.concatenate(
-        [jnp.sum(jnp.where(hit, factors, 0.0), axis=0, keepdims=True) for hit in hits], axis=0
-    )
-    masses = over_slots(masses, jnp.add)
-    inverse = 1.0 / jnp.where(masses > 0.0, masses, 1.0)
-    shares = factors * back(inverse)
-    turned = jnp.concatenate([shares, jnp.zeros((LANES - 2 * chips, LANES), f32)], axis=0).T
-    for side, ref in enumerate(packages):
-        for chip in range(chips):
-            device = side * chips + chip
-            scaled[device] = ref[chip, :value_rows, :].astype(f32) * turned[
-                :value_rows, device : device + 1
-            ]
-    for r in range(requests):
-        total = None
-        for j in range(pages_req):
-            device = lax.div(table[j, r], pages)
-            side = lax.rem(device + core, 2)
-            place = side * chips + lax.div(device, 2)
-            first = pl.multiple_of(lax.rem(table[j, r], pages) * QH, QH)
-            part = scaled[place, pl.ds(first, QH), :]
-            total = part if total is None else total + part
-        rows[r * QH : (r + 1) * QH, :] = total
     for chip in range(chips):
         mine, theirs = (ref[chip, value_rows : value_rows + SUB, :].astype(f32) for ref in packages)
         first = 2 * chip * HD
         new_kv[:, first : first + HD] = jnp.where(core == 0, mine, theirs).astype(bf16)
         new_kv[:, first + HD : first + 2 * HD] = jnp.where(core == 0, theirs, mine).astype(bf16)
+    each = LANES // value_rows
+    request = lax.broadcasted_iota(jnp.int32, (requests, LANES), 0)
+    lane = lax.broadcasted_iota(jnp.int32, (requests, LANES), 1)
+    logs, hits = [], []
+    for ref in packages:
+        for chip in range(0, chips, each):
+            terms = sum(ref[chip + k, value_rows + SUB :, :].astype(f32) for k in range(each))
+            log = sum(terms[k : k + 1, :] for k in range(PARTS))
+            logs.append(jnp.broadcast_to(log, (requests, LANES)))
+            row = len(hits)
+            hits.append(jnp.broadcast_to(owner[row : row + 1, :], (requests, LANES)) == request)
+
+    def over_pages(value, combine):
+        out = value
+        for k in range(QH, LANES, QH):
+            out = combine(out, pltpu.roll(value, k, 1))
+        return out
+
+    tops = functools.reduce(
+        jnp.maximum, [jnp.where(hit, log, lowest) for hit, log in zip(hits, logs)]
+    )
+    tops = over_pages(tops, jnp.maximum)
+    factors = [jnp.where(hit, jnp.exp(log - tops), 0.0) for hit, log in zip(hits, logs)]
+    inverse = 1.0 / over_pages(functools.reduce(jnp.add, factors), jnp.add)
+    shares = []
+    for factor in factors:
+        share = factor * inverse
+        heads = [jnp.where(lane % QH == h, share, 0.0) for h in range(QH)]
+        shares.append(jnp.concatenate(heads, axis=0).astype(bf16))
+    half = len(shares) // 2
+    mixed = None
+    for side, ref in enumerate(packages):
+        part = jnp.dot(
+            jnp.concatenate(shares[side * half : (side + 1) * half], axis=1),
+            jnp.concatenate([ref[chip, :value_rows, :] for chip in range(chips)], axis=0),
+            preferred_element_type=f32,
+        )
+        mixed = part if mixed is None else mixed + part
     attended = jnp.concatenate(
-        [rows[pl.ds(h, requests, stride=QH), :].astype(bf16) for h in range(QH)], axis=-1
-    )
+        [mixed[h * requests : (h + 1) * requests] for h in range(QH)], axis=1
+    ).astype(bf16)
     total = jnp.dot(attended, weights[...], preferred_element_type=f32)
     final[...] = (middle[...] + total).astype(bf16)
 
@@ -794,18 +790,20 @@
     )(position, received, kv_cache, table, spans)
     received = lax.all_to_all(sent, "seq", 0, 0, axis_index_groups=same_core)
     far = lax.ppermute(received, "seq", cores)
+    owner_rows = count * pages * QH // LANES
+    owner = call(
+        functools.partial(owner_kernel, chips, pages),
+        near((owner_rows, LANES), jnp.int32),
+        [SMEM] * 2 + [NEAR],
+    )(position, page_table.T, received)
     final, new_kv = call(
         functools.partial(merge_kernel, pages),
         (
             shape((requests, columns), bf16),
             shape((requests, 2 * KVH * HD), bf16),
         ),
-        [SMEM] * 2 + [NEAR] * 4,
-        [
-            pltpu.VMEM((count, pages * QH, HD), f32),
-            pltpu.VMEM((requests * QH, HD), f32),
-        ],
-    )(position, page_table.T, received, far, w_out, middle)
+        [SMEM] + [NEAR] * 5,
+    )(position, received, far, owner, w_out, middle)
     return (final, new_state.reshape(ssm_state.shape), new_kv)
 
 
@@ -820,7 +818,8 @@
         and hidden.shape[0] == SUB
         and (hidden.shape[1] // count) % LANES == 0
         and SUB % kv_cache.shape[0] == 0
-        and kv_cache.shape[0] * QH <= LANES
+        and LANES % (kv_cache.shape[0] * QH) == 0
+        and (count // 2) % (LANES // (kv_cache.shape[0] * QH)) == 0
         and kv_cache.shape[1] == LANES
         and 2 * KVH == count
     )

time: 52.4 us -> 51.5 us (0.983)
  waiting for transfers between devices: 1.96 us -> 1.35 us
    ppermute x1, waiting for transfers between devices: 1.39 us -> 0.79 us  [fused_shards(): far = lax.ppermute(received, 'seq', cores)]
    pallas_call x8 -> x9, Pallas kernels: 10 us -> 9.67 us  [run(): return grid_free(*placed)]
  transfers between devices with their start and end apart: 3 -> 3, of which waited for: 2 -> 2; matrix products, arithmetic and copies ran while one was open for 0% -> 0% of each run, Pallas kernels for 6% -> 8%
where the time goes in v5:
time: 51.5 us; the launch traced here: 51.2 us
  blocking collectives  33.2 us (64%)
  Pallas kernels  9.67 us (19%)
  starting transfers between devices  4.2 us (8%)
  between operations  2.66 us (5%)
  waiting for transfers between devices  1.35 us (3%)
    all_to_all x2, blocking collectives, fused_shards(): received = lax.all_to_all(sent, 'seq', 0, 0, axis_index_groups=same_core)  22.1 us
    all_to_all x1, blocking collectives, fused_shards(): received = lax.all_to_all(sent, 'seq', 0, 0)  11.1 us
    pallas_call x9, Pallas kernels, run(): return grid_free(*placed)  9.67 us
    ppermute x1, starting transfers between devices, fused_shards(): other = lax.ppermute(group_conv, 'seq', swap)  4.13 us
  transfers between devices with their start and end apart: 3, of which 2 were waited for; matrix products, arithmetic and copies ran while one was open for 0% of the time, Pallas kernels for 8%

profile of v5, /device:TPU:0, one launch (start us, length us, event | category | flops | bytes accessed | tf_op | source)
XLA Modules:
  0.0 51.2 jit_solution(14975485195722401783)
XLA Ops:
  0.6 1.7 %shard_map.220 = (bf16[8,128]{1,0:T(8,128)(2,1)S(1)}, bf16[8,4096]{1,0:T(8,128)(2,1)S(1)}) custom-call(bf16[8,4096]{1,0:T(8,128)(2,1)} %refs_5_.1, f32[1,4096]{1,0:T(1,128)} %bitcast.17, bf16[4096,128]{1,0:T(8,128)(2,1)} %weights_far.1, bf16[3,8,128]{2,1,0:T(8,128)(2,1)} %bitcast.19, f32[5,128]{1,0:T(8,128)} %taps_far.1), custom_call_target="tpu_custom_call" | custom-call | tf_op jit(solution)/shard_map/pallas_call | solution.py:258
  2.3 0.0 copy-start
  2.3 4.1 %collective-permute-start = (bf16[8,128]{1,0:T(8,128)(2,1)S(1)}, bf16[8,128]{1,0:T(8,128)(2,1)S(1)}, u32[]{:S(2)}, u32[]{:S(2)}) collective-permute-start(bf16[8,128]{1,0:T(8,128)(2,1)S(1)} %get-tuple-element.21.own), channel_id=1, source_target_pairs={{0,8},{1,9},{2,10},{3,11},{4,12},{5,13},{6,14},{7,15},{8,0},{9,1},... | collective-permute-start | bytes 6152 | tf_op jit(solution)/shard_map/ppermute | solution.py:732
  8.4 0.1 pad_maximum_fusion.refs_4_
  8.5 2.4 %shard_map.221 = (f32[8,64]{1,0:T(8,128)S(1)}, f32[8,128]{1,0:T(8,128)S(1)}, f32[8,128]{1,0:T(8,128)S(1)}, f32[8,128]{1,0:T(8,128)S(1)}, bf16[8,256]{1,0:T(8,128...) custom-call(s32[1]{0:T(128)} %bitcast.position, ...), custom_call_target="tpu_custom_call" | custom-call | tf_op jit(solution)/shard_map/pallas_call | solution.py:258
  10.8 0.0 collective-permute-done.other
  10.8 0.0 copy-start.2
  10.9 0.7 %shard_map.222 = bf16[16,8,384]{2,1,0:T(8,128)(2,1)S(1)} custom-call(s32[1]{0:T(128)} %bitcast.position, bf16[8,128]{1,0:T(8,128)(2,1)S(1)} %get-tuple-element.21.own, bf16[8,128]{1,0:T(8,128)(2,1)S(1)} %collective-permute-done.other, f32[8,64]{1,0:T(8,128)S(1)} %get-tuple-element.23.gate, f32[8,128]{1,0:T(8,128)S(1)} %get-tuple-element.24.conv, ...), custom_call_target="tpu_custom_call" | custom-call | tf_op jit(solution)/shard_map/pallas_call | solution.py:258
  11.6 11.1 %all_to_all.15.received = bf16[16,8,384]{2,1,0:T(8,128)(2,1)S(1)} all-to-all(bf16[16,8,384]{2,1,0:T(8,128)(2,1)S(1)} %shard_map.222), channel_id=1, replica_groups=mesh['grp'=2,'seq'=16] {'seq'}, dimensions={0} | all-to-all | bytes 196608 | tf_op jit(solution)/shard_map/all_to_all | solution.py:767
  22.6 0.0 copy-done
  22.6 0.0 copy-start.3
  22.6 0.0 copy-start.1
  22.6 0.9 %shard_map.223 = (f32[8,8,1792]{2,1,0:T(8,128)S(1)}, bf16[8,8,1792]{2,1,0:T(8,128)(2,1)S(1)}, f32[8,256]{1,0:T(8,128)S(1)}) custom-call(s32[1]{0:T(128)} %bitcast.position, bf16[16,8,384]{2,1,0:T(8,128)(2,1)S(1)} %all_to_all.15.received, bf16[8,256]{1,0:T(8,128)(2,1)S(1)} %get-tuple-element.30.hidden, f32[1,256]{1,0:T(1,128)S(1)} %get-tuple-element.31.gain, ...), custom_call_target="tpu_custom_call" | custom-call | tf_op jit(solution)/shard_map/pallas_call | solution.py:258
  23.5 0.1 collective-permute-start.1
  23.6 0.9 %shard_map.224._ = f32[8,64,128]{2,1,0:T(8,128)} custom-call(s32[1]{0:T(128)} %bitcast.position, bf16[8,128]{1,0:T(8,128)(2,1)S(1)} %get-tuple-element.21.own, bf16[8,128]{1,0:T(8,128)(2,1)S(1)} %collective-permute-done.other, f32[8,128]{1,0:T(8,128)S(1)} %get-tuple-element.24.conv, f32[8,128]{1,0:T(8,128)S(1)} %get-tuple-element.25.step, ...), custom_call_target="tpu_custom_call" | custom-call | tf_op jit(solution)/shard_map/pallas_call | solution.py:258
  24.5 0.6 %collective-permute-done.1.taken = bf16[8,8,1792]{2,1,0:T(8,128)(2,1)S(1)} collective-permute-done((bf16[8,8,1792]{2,1,0:T(8,128)(2,1)S(1)}, bf16[8,8,1792]{2,1,0:T(8,128)(2,1)S(1)}, u32[]{:S(2)}, u32[]{:S(2)}) %collective-permute-start.1) | collective-permute-done | bytes 229408 | tf_op jit(solution)/shard_map/ppermute | solution.py:781
  25.0 0.2 shard_map.225
  25.2 11.4 %all_to_all.16.received = bf16[8,8,1792]{2,1,0:T(8,128)(2,1)S(1)} all-to-all(bf16[8,8,1792]{2,1,0:T(8,128)(2,1)S(1)} %shard_map.225), channel_id=1, replica_groups={{0,2,4,6,8,10,12,14},{1,3,5,7,9,11,13,15},{16,18,20,22,24,26,28,30},{17..., dimensions={0} | all-to-all | bytes 458752 | tf_op jit(solution)/shard_map/all_to_all | solution.py:783
  36.7 0.0 copy-done.2
  36.7 1.1 %shard_map.226 = bf16[8,80,128]{2,1,0:T(8,128)(2,1)S(1)} custom-call(s32[1]{0:T(128)} %bitcast.position, bf16[8,8,1792]{2,1,0:T(8,128)(2,1)S(1)} %all_to_all.16.received, bf16[2,128,2048]{2,1,0:T(8,128)(2,1)S(1)} %copy-done.2, s32[4,8]{1,0:T(4,128)S(1)} %get-tuple-element.32.table, s32[1,8]{1,0:T(1,128)S(1)} %get-tuple-element.35.lengths), custom_call_target="tpu_custom_call" | custom-call | tf_op jit(solution)/shard_map/pallas_call | solution.py:258
  37.7 10.7 %all_to_all.17._.near_ref = bf16[8,80,128]{2,1,0:T(8,128)(2,1)S(1)} all-to-all(bf16[8,80,128]{2,1,0:T(8,128)(2,1)S(1)} %shard_map.226), channel_id=1, replica_groups={{0,2,4,6,8,10,12,14},{1,3,5,7,9,11,13,15},{16,18,20,22,24,26,28,30},{17..., dimensions={0} | all-to-all | bytes 327680 | tf_op jit(solution)/shard_map/all_to_all | solution.py:791
  48.4 0.0 collective-permute-start.2
  48.5 0.0 copy-done.3
  48.5 0.6 %shard_map.227.owner = s32[8,128]{1,0:T(8,128)S(1)} custom-call(s32[1]{0:T(128)} %bitcast.position, s32[4,8]{1,0:T(4,128)S(1)} %bitcast.14, bf16[8,80,128]{2,1,0:T(8,128)(2,1)S(1)} %all_to_all.17._.near_ref), custom_call_target="tpu_custom_call" | custom-call | tf_op jit(solution)/shard_map/pallas_call | solution.py:258
  49.1 0.8 %collective-permute-done.2.far_ref = bf16[8,80,128]{2,1,0:T(8,128)(2,1)S(1)} collective-permute-done((bf16[8,80,128]{2,1,0:T(8,128)(2,1)S(1)}, bf16[8,80,128]{2,1,0:T(8,128)(2,1)S(1)}, u32[]{:S(2)}, u32[]{:S(2)}) %collective-permute-start.2) | collective-permute-done | bytes 163872 | tf_op jit(solution)/shard_map/ppermute | solution.py:792
  49.8 0.0 copy-done.1
  49.8 1.3 %shard_map.228 = (bf16[8,256]{1,0:T(8,128)(2,1)}, bf16[8,2048]{1,0:T(8,128)(2,1)}) custom-call(s32[1]{0:T(128)} %bitcast.position, bf16[8,80,128]{2,1,0:T(8,128)(2,1)S(1)} %all_to_all.17._.near_ref, bf16[8,80,128]{2,1,0:T(8,128)(2,1)S(1)} %collective-permute-done.2.far_ref, s32[8,128]{1,0:T(8,128)S(1)} %shard_map.227.owner, bf16[4096,256]{1,0:T(8,128)(2,1)S(1)} %copy-done.1, ...), custom_call_target="tpu_custom_call" | custom-call | tf_op jit(solution)/shard_map/pallas_call | solution.py:258
Async XLA Ops:
  2.3 20.3 %copy-start = (bf16[256,6144]{1,0:T(8,128)(2,1)S(1)}, bf16[256,6144]{1,0:T(8,128)(2,1)}, u32[]{:S(2)}) copy-start(bf16[256,6144]{1,0:T(8,128)(2,1)} %weights.2) | copy-start | bytes 9437188
  2.3 8.5 %collective-permute-start = (bf16[8,128]{1,0:T(8,128)(2,1)S(1)}, bf16[8,128]{1,0:T(8,128)(2,1)S(1)}, u32[]{:S(2)}, u32[]{:S(2)}) collective-permute-start(bf16[8,128]{1,0:T(8,128)(2,1)S(1)} %get-tuple-element.21.own), channel_id=1, source_target_pairs={{0,8},{1,9},{2,10},{3,11},{4,12},{5,13},{6,14},{7,15},{8,0},{9,1},... | collective-permute-start | bytes 6152 | tf_op jit(solution)/shard_map/ppermute | solution.py:732
  10.8 25.8 %copy-start.2 = (bf16[2,128,2048]{2,1,0:T(8,128)(2,1)S(1)}, bf16[2,128,2048]{2,1,0:T(8,128)(2,1)}, u32[]{:S(2)}) copy-start(bf16[2,128,2048]{2,1,0:T(8,128)(2,1)} %cache.1) | copy-start | bytes 3145732
  22.6 25.8 %copy-start.3 = (s32[8,4]{0,1:T(4,128)S(1)}, s32[8,4]{0,1:T(4,128)}, u32[]{:S(2)}) copy-start(s32[8,4]{0,1:T(4,128)} %param.40) | copy-start | bytes 388
  22.6 27.2 %copy-start.1 = (bf16[4096,256]{1,0:T(8,128)(2,1)S(1)}, bf16[4096,256]{1,0:T(8,128)(2,1)}, u32[]{:S(2)}) copy-start(bf16[4096,256]{1,0:T(8,128)(2,1)} %weights.3) | copy-start | bytes 6291460
  23.5 1.6 %collective-permute-start.1 = (bf16[8,8,1792]{2,1,0:T(8,128)(2,1)S(1)}, bf16[8,8,1792]{2,1,0:T(8,128)(2,1)S(1)}, u32[]{:S(2)}, u32[]{:S(2)}) collective-permute-start(bf16[8,8,1792]{2,1,0:T(8,128)(2,1)S(1)} %get-tuple-element.34), channel_id=1, source_target_pairs={{0,1},{1,0},{2,3},{3,2},{4,5},{5,4},{6,7},{7,6},{8,9},{9,8},{10,11... | collective-permute-start | bytes 688136 | tf_op jit(solution)/shard_map/ppermute | solution.py:781
  48.4 1.4 %collective-permute-start.2 = (bf16[8,80,128]{2,1,0:T(8,128)(2,1)S(1)}, bf16[8,80,128]{2,1,0:T(8,128)(2,1)S(1)}, u32[]{:S(2)}, u32[]{:S(2)}) collective-permute-start(bf16[8,80,128]{2,1,0:T(8,128)(2,1)S(1)} %all_to_all.17._.near_ref), channel_id=1, source_target_pairs={{0,1},{1,0},{2,3},{3,2},{4,5},{5,4},{6,7},{7,6},{8,9},{9,8},{10,11... | collective-permute-start | bytes 491528 | tf_op jit(solution)/shard_map/ppermute | solution.py:792

commit v6 on v5

--- a/solution.py
+++ b/solution.py
@@ -232,7 +232,7 @@
 PARTS = 3
 SCOPED = 16 << 20
 MOST = 63500 << 10
-BLOCKS = 4
+BLOCKS = 2
 VMEM = pl.BlockSpec(memory_space=pltpu.VMEM)
 NEAR = pl.BlockSpec(memory_space=pltpu.VMEM)
 SMEM = pl.BlockSpec(memory_space=pltpu.SMEM)
@@ -380,11 +380,11 @@
     gate_out[...] = silu(both[:, :half])
     fresh = convolve(state, both[:, half:], taps)
     conv_out[:, :half] = fresh
-    conv_out[:, half:] = numbers[2] * fresh
+    conv_out[:, half:] = numbers[:, 2:3] * fresh
     raw = jnp.sum(normed_ref[...].astype(f32) * step_row[...].astype(f32), axis=-1, keepdims=True)
-    step = jax.nn.softplus(raw + numbers[1])
+    step = jax.nn.softplus(raw + numbers[:, 1:2])
     step_out[...] = jnp.broadcast_to(step, step_out.shape)
-    decay_out[...] = jnp.broadcast_to(jnp.exp(-numbers[0] * step), decay_out.shape)
+    decay_out[...] = jnp.broadcast_to(jnp.exp(-numbers[:, 0:1] * step), decay_out.shape)
     for copy in copies[BLOCKS + 3 :]:
         copy.wait()
 
@@ -399,17 +399,22 @@
     requests = own.shape[0]
     inject, readout = chosen(position, own, other)
     half = gate.shape[1]
-    row = lax.broadcasted_iota(jnp.int32, gate.shape, 0)
-    read = jnp.zeros(gate.shape, f32)
-    for r in range(requests):
-        part = lax.dot_general(
-            readout,
-            state[r],
-            (((1,), (1,)), ((), ())),
-            precision=lax.Precision.HIGHEST,
-            preferred_element_type=f32,
-        )
-        read = jnp.where(row == r, part, read)
+    both = 2 * half
+    flat = state[...].reshape(requests * half, state.shape[2])
+    high = flat.astype(bf16)
+    low = (flat - high.astype(f32)).astype(bf16)
+    vectors = readout.astype(bf16)
+    full = sum(
+        lax.dot_general(
+            vectors, term, (((1,), (1,)), ((), ())), preferred_element_type=f32
+        )
+        for term in (high, low)
+    )
+    row = lax.broadcasted_iota(jnp.int32, (requests, both), 0)
+    pairs = jnp.zeros((requests, both), f32)
+    for k in range(requests // 2):
+        pairs = jnp.where(row // 2 == k, full[:, k * both : (k + 1) * both], pairs)
+    read = jnp.where(row[:, :half] % 2 == 0, pairs[:, :half], pairs[:, half:])
     along = jnp.sum(inject * readout, axis=-1, keepdims=True)
     fresh = conv[:, :half]
     out = decay[:, :1] * read + step[:, :1] * fresh * along + conv[:, half:]
@@ -744,7 +749,7 @@
         conv_input.transpose(1, 0, 2),
         taps_input,
     )
-    numbers = jnp.concatenate([decay_rate, step_bias, skip_gain])
+    numbers = jnp.concatenate([decay_rate, step_bias, skip_gain]).reshape(1, 3)
     gate, conv, step, decay, stream, state_in, mixer, gain, scale, table, spans = call(
         functools.partial(gate_kernel, len(carried)),
         (
@@ -755,7 +760,7 @@
             near((requests, columns), bf16),
         )
         + tuple(near(x.shape, x.dtype) for x in carried),
-        [SMEM, NEAR] + [FAR] * 4 + [SMEM] + [FAR] * (1 + len(carried)),
+        [SMEM, NEAR] + [FAR] * 4 + [NEAR] + [FAR] * (1 + len(carried)),
         [pltpu.VMEM(x.shape, x.dtype) for x in gate_args]
         + [pltpu.SemaphoreType.DMA((BLOCKS + 4 + len(carried),))],
     )(position, normed, *gate_args, numbers, hidden, *carried)

time: 51.5 us -> 50.7 us (0.984)
  Pallas kernels: 9.67 us -> 8.83 us
    pallas_call x9, Pallas kernels: 9.67 us -> 8.83 us  [run(): return grid_free(*placed)]
  transfers between devices with their start and end apart: 3 -> 3, of which waited for: 2 -> 2; matrix products, arithmetic and copies ran while one was open for 0% -> 0% of each run, Pallas kernels for 8% -> 7%
where the time goes in v6:
time: 50.7 us; the launch traced here: 50.4 us
  blocking collectives  33.2 us (65%)
  Pallas kernels  8.83 us (17%)
  starting transfers between devices  4.2 us (8%)
  between operations  2.66 us (5%)
  waiting for transfers between devices  1.35 us (3%)
    all_to_all x2, blocking collectives, fused_shards(): received = lax.all_to_all(sent, 'seq', 0, 0, axis_index_groups=same_core)  22.1 us
    all_to_all x1, blocking collectives, fused_shards(): received = lax.all_to_all(sent, 'seq', 0, 0)  11.1 us
    pallas_call x9, Pallas kernels, run(): return grid_free(*placed)  8.83 us
    ppermute x1, starting transfers between devices, fused_shards(): other = lax.ppermute(group_conv, 'seq', swap)  4.13 us
  transfers between devices with their start and end apart: 3, of which 2 were waited for; matrix products, arithmetic and copies ran while one was open for 0% of the time, Pallas kernels for 7%

profile of v6, /device:TPU:0, one launch (start us, length us, event | category | flops | bytes accessed | tf_op | source)
XLA Modules:
  0.0 50.4 jit_solution(14004103652002777973)
XLA Ops:
  0.6 1.6 %shard_map.220 = (bf16[8,128]{1,0:T(8,128)(2,1)S(1)}, bf16[8,4096]{1,0:T(8,128)(2,1)S(1)}) custom-call(bf16[8,4096]{1,0:T(8,128)(2,1)} %refs_5_.1, f32[1,4096]{1,0:T(1,128)} %bitcast.19, bf16[4096,128]{1,0:T(8,128)(2,1)} %weights_far.1, bf16[3,8,128]{2,1,0:T(8,128)(2,1)} %bitcast.21, f32[5,128]{1,0:T(8,128)} %taps_far.1), custom_call_target="tpu_custom_call" | custom-call | tf_op jit(solution)/shard_map/pallas_call | solution.py:258
  2.2 0.0 copy-start
  2.2 4.1 %collective-permute-start = (bf16[8,128]{1,0:T(8,128)(2,1)S(1)}, bf16[8,128]{1,0:T(8,128)(2,1)S(1)}, u32[]{:S(2)}, u32[]{:S(2)}) collective-permute-start(bf16[8,128]{1,0:T(8,128)(2,1)S(1)} %get-tuple-element.21.own), channel_id=1, source_target_pairs={{0,8},{1,9},{2,10},{3,11},{4,12},{5,13},{6,14},{7,15},{8,0},{9,1},... | collective-permute-start | bytes 6152 | tf_op jit(solution)/shard_map/ppermute | solution.py:737
  8.3 0.1 maximum_bitcast_fusion.refs_4_
  8.4 1.9 %shard_map.221 = (f32[8,64]{1,0:T(8,128)S(1)}, f32[8,128]{1,0:T(8,128)S(1)}, f32[8,128]{1,0:T(8,128)S(1)}, f32[8,128]{1,0:T(8,128)S(1)}, bf16[8,256]{1,0:T(8,128...) custom-call(s32[1]{0:T(128)} %bitcast.position, ...), custom_call_target="tpu_custom_call" | custom-call | tf_op jit(solution)/shard_map/pallas_call | solution.py:258
  10.3 0.0 collective-permute-done.other
  10.3 0.0 copy-start.2
  10.3 0.4 shard_map.222
  10.7 11.1 %all_to_all.15.received = bf16[16,8,384]{2,1,0:T(8,128)(2,1)S(1)} all-to-all(bf16[16,8,384]{2,1,0:T(8,128)(2,1)S(1)} %shard_map.222), channel_id=1, replica_groups=mesh['grp'=2,'seq'=16] {'seq'}, dimensions={0} | all-to-all | bytes 196608 | tf_op jit(solution)/shard_map/all_to_all | solution.py:772
  21.8 0.0 copy-done
  21.8 0.0 copy-start.3
  21.8 0.0 copy-start.1
  21.8 0.9 %shard_map.223 = (f32[8,8,1792]{2,1,0:T(8,128)S(1)}, bf16[8,8,1792]{2,1,0:T(8,128)(2,1)S(1)}, f32[8,256]{1,0:T(8,128)S(1)}) custom-call(s32[1]{0:T(128)} %bitcast.position, bf16[16,8,384]{2,1,0:T(8,128)(2,1)S(1)} %all_to_all.15.received, bf16[8,256]{1,0:T(8,128)(2,1)S(1)} %get-tuple-element.30.hidden, f32[1,256]{1,0:T(1,128)S(1)} %get-tuple-element.31.gain, ...), custom_call_target="tpu_custom_call" | custom-call | tf_op jit(solution)/shard_map/pallas_call | solution.py:258
  22.7 0.1 collective-permute-start.1
  22.7 0.9 %shard_map.224._ = f32[8,64,128]{2,1,0:T(8,128)} custom-call(s32[1]{0:T(128)} %bitcast.position, bf16[8,128]{1,0:T(8,128)(2,1)S(1)} %get-tuple-element.21.own, bf16[8,128]{1,0:T(8,128)(2,1)S(1)} %collective-permute-done.other, f32[8,128]{1,0:T(8,128)S(1)} %get-tuple-element.24.conv, f32[8,128]{1,0:T(8,128)S(1)} %get-tuple-element.25.step, ...), custom_call_target="tpu_custom_call" | custom-call | tf_op jit(solution)/shard_map/pallas_call | solution.py:258
  23.7 0.6 %collective-permute-done.1.taken = bf16[8,8,1792]{2,1,0:T(8,128)(2,1)S(1)} collective-permute-done((bf16[8,8,1792]{2,1,0:T(8,128)(2,1)S(1)}, bf16[8,8,1792]{2,1,0:T(8,128)(2,1)S(1)}, u32[]{:S(2)}, u32[]{:S(2)}) %collective-permute-start.1) | collective-permute-done | bytes 229408 | tf_op jit(solution)/shard_map/ppermute | solution.py:786
  24.2 0.2 shard_map.225
  24.4 11.4 %all_to_all.16.received = bf16[8,8,1792]{2,1,0:T(8,128)(2,1)S(1)} all-to-all(bf16[8,8,1792]{2,1,0:T(8,128)(2,1)S(1)} %shard_map.225), channel_id=1, replica_groups={{0,2,4,6,8,10,12,14},{1,3,5,7,9,11,13,15},{16,18,20,22,24,26,28,30},{17..., dimensions={0} | all-to-all | bytes 458752 | tf_op jit(solution)/shard_map/all_to_all | solution.py:788
  35.8 0.0 copy-done.2
  35.8 1.1 %shard_map.226 = bf16[8,80,128]{2,1,0:T(8,128)(2,1)S(1)} custom-call(s32[1]{0:T(128)} %bitcast.position, bf16[8,8,1792]{2,1,0:T(8,128)(2,1)S(1)} %all_to_all.16.received, bf16[2,128,2048]{2,1,0:T(8,128)(2,1)S(1)} %copy-done.2, s32[4,8]{1,0:T(4,128)S(1)} %get-tuple-element.32.table, s32[1,8]{1,0:T(1,128)S(1)} %get-tuple-element.35.lengths), custom_call_target="tpu_custom_call" | custom-call | tf_op jit(solution)/shard_map/pallas_call | solution.py:258
  36.9 10.7 %all_to_all.17._.near_ref = bf16[8,80,128]{2,1,0:T(8,128)(2,1)S(1)} all-to-all(bf16[8,80,128]{2,1,0:T(8,128)(2,1)S(1)} %shard_map.226), channel_id=1, replica_groups={{0,2,4,6,8,10,12,14},{1,3,5,7,9,11,13,15},{16,18,20,22,24,26,28,30},{17..., dimensions={0} | all-to-all | bytes 327680 | tf_op jit(solution)/shard_map/all_to_all | solution.py:796
  47.6 0.0 collective-permute-start.2
  47.6 0.0 copy-done.3
  47.6 0.6 %shard_map.227.owner = s32[8,128]{1,0:T(8,128)S(1)} custom-call(s32[1]{0:T(128)} %bitcast.position, s32[4,8]{1,0:T(4,128)S(1)} %bitcast.16, bf16[8,80,128]{2,1,0:T(8,128)(2,1)S(1)} %all_to_all.17._.near_ref), custom_call_target="tpu_custom_call" | custom-call | tf_op jit(solution)/shard_map/pallas_call | solution.py:258
  48.2 0.8 %collective-permute-done.2.far_ref = bf16[8,80,128]{2,1,0:T(8,128)(2,1)S(1)} collective-permute-done((bf16[8,80,128]{2,1,0:T(8,128)(2,1)S(1)}, bf16[8,80,128]{2,1,0:T(8,128)(2,1)S(1)}, u32[]{:S(2)}, u32[]{:S(2)}) %collective-permute-start.2) | collective-permute-done | bytes 163872 | tf_op jit(solution)/shard_map/ppermute | solution.py:797
  49.0 0.0 copy-done.1
  49.0 1.3 %shard_map.228 = (bf16[8,256]{1,0:T(8,128)(2,1)}, bf16[8,2048]{1,0:T(8,128)(2,1)}) custom-call(s32[1]{0:T(128)} %bitcast.position, bf16[8,80,128]{2,1,0:T(8,128)(2,1)S(1)} %all_to_all.17._.near_ref, bf16[8,80,128]{2,1,0:T(8,128)(2,1)S(1)} %collective-permute-done.2.far_ref, s32[8,128]{1,0:T(8,128)S(1)} %shard_map.227.owner, bf16[4096,256]{1,0:T(8,128)(2,1)S(1)} %copy-done.1, ...), custom_call_target="tpu_custom_call" | custom-call | tf_op jit(solution)/shard_map/pallas_call | solution.py:258
Async XLA Ops:
  2.2 19.6 %copy-start = (bf16[256,6144]{1,0:T(8,128)(2,1)S(1)}, bf16[256,6144]{1,0:T(8,128)(2,1)}, u32[]{:S(2)}) copy-start(bf16[256,6144]{1,0:T(8,128)(2,1)} %weights.2) | copy-start | bytes 9437188
  2.2 8.0 %collective-permute-start = (bf16[8,128]{1,0:T(8,128)(2,1)S(1)}, bf16[8,128]{1,0:T(8,128)(2,1)S(1)}, u32[]{:S(2)}, u32[]{:S(2)}) collective-permute-start(bf16[8,128]{1,0:T(8,128)(2,1)S(1)} %get-tuple-element.21.own), channel_id=1, source_target_pairs={{0,8},{1,9},{2,10},{3,11},{4,12},{5,13},{6,14},{7,15},{8,0},{9,1},... | collective-permute-start | bytes 6152 | tf_op jit(solution)/shard_map/ppermute | solution.py:737
  10.3 25.6 %copy-start.2 = (bf16[2,128,2048]{2,1,0:T(8,128)(2,1)S(1)}, bf16[2,128,2048]{2,1,0:T(8,128)(2,1)}, u32[]{:S(2)}) copy-start(bf16[2,128,2048]{2,1,0:T(8,128)(2,1)} %cache.1) | copy-start | bytes 3145732
  21.8 25.8 %copy-start.3 = (s32[8,4]{0,1:T(4,128)S(1)}, s32[8,4]{0,1:T(4,128)}, u32[]{:S(2)}) copy-start(s32[8,4]{0,1:T(4,128)} %param.40) | copy-start | bytes 388
  21.8 27.2 %copy-start.1 = (bf16[4096,256]{1,0:T(8,128)(2,1)S(1)}, bf16[4096,256]{1,0:T(8,128)(2,1)}, u32[]{:S(2)}) copy-start(bf16[4096,256]{1,0:T(8,128)(2,1)} %weights.3) | copy-start | bytes 6291460
  22.7 1.6 %collective-permute-start.1 = (bf16[8,8,1792]{2,1,0:T(8,128)(2,1)S(1)}, bf16[8,8,1792]{2,1,0:T(8,128)(2,1)S(1)}, u32[]{:S(2)}, u32[]{:S(2)}) collective-permute-start(bf16[8,8,1792]{2,1,0:T(8,128)(2,1)S(1)} %get-tuple-element.34), channel_id=1, source_target_pairs={{0,1},{1,0},{2,3},{3,2},{4,5},{5,4},{6,7},{7,6},{8,9},{9,8},{10,11... | collective-permute-start | bytes 688136 | tf_op jit(solution)/shard_map/ppermute | solution.py:786
  47.6 1.4 %collective-permute-start.2 = (bf16[8,80,128]{2,1,0:T(8,128)(2,1)S(1)}, bf16[8,80,128]{2,1,0:T(8,128)(2,1)S(1)}, u32[]{:S(2)}, u32[]{:S(2)}) collective-permute-start(bf16[8,80,128]{2,1,0:T(8,128)(2,1)S(1)} %all_to_all.17._.near_ref), channel_id=1, source_target_pairs={{0,1},{1,0},{2,3},{3,2},{4,5},{5,4},{6,7},{7,6},{8,9},{9,8},{10,11... | collective-permute-start | bytes 491528 | tf_op jit(solution)/shard_map/ppermute | solution.py:797

commit v7 on v6

--- a/solution.py
+++ b/solution.py
@@ -473,27 +473,35 @@
     spread = jnp.dot(onehot, extended, preferred_element_type=f32)
     lines = spread[:, :columns]
     which = (lax.broadcasted_iota(jnp.int32, lines.shape, 0) % SUB) // pages
-    chunk = weights.shape[1] // chunks
     fresh_from = QH * HD
-    zeros = jnp.zeros((SUB, columns), f32)
+    value_from = fresh_from + KVH * HD
+    chunk = value_from // chunks
+    plain = jnp.concatenate([scaled, jnp.zeros((SUB, columns), f32)], axis=0)
     lhs = []
     for c in range(chunks):
         own = jnp.where(which == c, lines, 0.0)
         if (c + 1) * chunk > fresh_from:
-            own = jnp.concatenate([own, scaled, zeros], axis=0)
+            own = jnp.concatenate([own, plain], axis=0)
         lhs.append(own.astype(bf16))
     tile = 2 * HD
+
+    def share_out(first, fresh):
+        chip = (first - fresh_from) // tile
+        low, high = fresh[:, :HD], fresh[:, HD:]
+        keep[chip, :, chunk + LANES :] = jnp.where(core == 0, low, high)
+        give[chip, :, chunk + LANES :] = jnp.where(core == 0, high, low).astype(bf16)
+
+    plain = plain.astype(bf16)
+    for first in range(value_from, weights.shape[1], tile):
+        fresh = jnp.dot(plain, weights[:, first : first + tile], preferred_element_type=f32)
+        share_out(first, fresh[:SUB])
     for n in range(0, chunk, tile):
         total = None
         for c in range(chunks):
             first = c * chunk + n
             part = jnp.dot(lhs[c], weights[:, first : first + tile], preferred_element_type=f32)
             if first >= fresh_from:
-                fresh = part[rows : rows + SUB]
-                chip = (first - fresh_from) // tile
-                low, high = fresh[:, :HD], fresh[:, HD:]
-                keep[chip, :, chunk + LANES :] = jnp.where(core == 0, low, high)
-                give[chip, :, chunk + LANES :] = jnp.where(core == 0, high, low).astype(bf16)
+                share_out(first, part[rows : rows + SUB])
             total = part[:rows] if total is None else total + part[:rows]
         for e in range(chips):
             keep[e, :, n : n + tile] = total[e * SUB : (e + 1) * SUB]
@@ -540,8 +548,13 @@
         )
 
     def heads(page, first, many):
-        start = (first % tiles) * SUB + (first // tiles) * pages + page
-        return lines[pl.ds(start, many, stride=SUB), :]
+        runs = []
+        while many:
+            run = min(many, tiles - first % tiles)
+            start = (first % tiles) * SUB + (first // tiles) * pages + page
+            runs.append(lines[pl.ds(start, run, stride=SUB), :])
+            first, many = first + run, many - run
+        return runs[0] if len(runs) == 1 else jnp.concatenate(runs, axis=0)
 
     group = QH // KVH
     scale = 1.0 / HD**0.5
@@ -553,6 +566,7 @@
     eye_lane = lax.broadcasted_iota(jnp.int32, (QH, LANES), 1) - place
     order = lax.broadcasted_iota(jnp.int32, table.shape, 0)
     log_row = jnp.zeros((1, LANES), f32)
+    own_row = jnp.zeros((1, LANES), f32)
     for p in range(pages):
         slot = position[0] * pages + p
         hit = table[...] == slot
@@ -566,9 +580,7 @@
         leads = logical == 0
         query = jnp.concatenate([heads(p, g * group, group) for g in range(KVH)], axis=0)
         keys = [heads(p, QH + g, 1) for g in range(KVH)]
-        values = [heads(p, QH + KVH + g, 1) for g in range(KVH)]
         key_rows = jnp.concatenate([jnp.broadcast_to(k, (group, HD)) for k in keys], axis=0)
-        value_own = jnp.concatenate([jnp.broadcast_to(v, (group, HD)) for v in values], axis=0)
         spread = jnp.concatenate(
             [jnp.where(head_group == g, query, 0.0).astype(bf16) for g in range(KVH)], axis=-1
         )
@@ -584,26 +596,26 @@
         own = jnp.sum(query * key_rows, axis=-1, keepdims=True) * scale
         masked = jnp.where(live, scores, lowest)
         own = jnp.where(leads, own, lowest)
-        peak = jnp.maximum(jnp.max(masked, axis=-1, keepdims=True), own)
+        peak = jnp.max(masked, axis=-1, keepdims=True)
         weights = jnp.where(live, jnp.exp(masked - peak), 0.0)
-        own_weight = jnp.where(leads, jnp.exp(own - peak), 0.0)
-        mass = jnp.sum(weights, axis=-1, keepdims=True) + own_weight
+        mass = jnp.sum(weights, axis=-1, keepdims=True)
         wide = jnp.dot(
             weights.astype(bf16), cache[p, :, KVH * HD :], preferred_element_type=f32
         )
-        mixed = own_weight * value_own
+        mixed = jnp.zeros((QH, HD), f32)
         for g in range(KVH):
             mixed = mixed + jnp.where(head_group == g, wide[:, g * HD : (g + 1) * HD], 0.0)
         some = mass > 0.0
         safe = jnp.where(some, mass, 1.0)
         result = (mixed / safe).astype(bf16)
         logs = jnp.where(some, peak + jnp.log(safe), lowest)
-        log_row = log_row + jnp.sum(
-            jnp.where(eye_lane == eye + p * QH, logs, 0.0), axis=0, keepdims=True
-        )
+        here = eye_lane == eye + p * QH
+        log_row = log_row + jnp.sum(jnp.where(here, logs, 0.0), axis=0, keepdims=True)
+        own_row = own_row + jnp.sum(jnp.where(here, own, 0.0), axis=0, keepdims=True)
         for e in range(count):
             sent[e, p * QH : (p + 1) * QH, :] = result
-    terms = pieces(log_row, PARTS) + [jnp.zeros((SUB - PARTS, LANES), f32)]
+    terms = pieces(log_row, PARTS) + pieces(own_row, PARTS)
+    terms.append(jnp.zeros((SUB - 2 * PARTS, LANES), f32))
     terms = jnp.concatenate(terms, axis=0).astype(bf16)
     for e in range(count):
         sent[e, value_rows : value_rows + SUB, :] = fresh
@@ -633,20 +645,22 @@
     value_rows = pages * QH
     core = position[0] % 2
     packages = (near_ref, far_ref)
+    fresh = []
     for chip in range(chips):
         mine, theirs = (ref[chip, value_rows : value_rows + SUB, :].astype(f32) for ref in packages)
-        first = 2 * chip * HD
-        new_kv[:, first : first + HD] = jnp.where(core == 0, mine, theirs).astype(bf16)
-        new_kv[:, first + HD : first + 2 * HD] = jnp.where(core == 0, theirs, mine).astype(bf16)
+        fresh += [jnp.where(core == 0, mine, theirs), jnp.where(core == 0, theirs, mine)]
+    for k, part in enumerate(fresh):
+        new_kv[:, k * HD : (k + 1) * HD] = part.astype(bf16)
     each = LANES // value_rows
     request = lax.broadcasted_iota(jnp.int32, (requests, LANES), 0)
     lane = lax.broadcasted_iota(jnp.int32, (requests, LANES), 1)
-    logs, hits = [], []
+    logs, own_logs, hits = [], [], []
     for ref in packages:
         for chip in range(0, chips, each):
             terms = sum(ref[chip + k, value_rows + SUB :, :].astype(f32) for k in range(each))
-            log = sum(terms[k : k + 1, :] for k in range(PARTS))
-            logs.append(jnp.broadcast_to(log, (requests, LANES)))
+            for first, rows in ((0, logs), (PARTS, own_logs)):
+                log = sum(terms[first + k : first + k + 1, :] for k in range(PARTS))
+                rows.append(jnp.broadcast_to(log, (requests, LANES)))
             row = len(hits)
             hits.append(jnp.broadcast_to(owner[row : row + 1, :], (requests, LANES)) == request)
 
@@ -657,11 +671,18 @@
         return out
 
     tops = functools.reduce(
-        jnp.maximum, [jnp.where(hit, log, lowest) for hit, log in zip(hits, logs)]
+        jnp.maximum,
+        [
+            jnp.where(hit, jnp.maximum(log, own), lowest)
+            for hit, log, own in zip(hits, logs, own_logs)
+        ],
     )
     tops = over_pages(tops, jnp.maximum)
     factors = [jnp.where(hit, jnp.exp(log - tops), 0.0) for hit, log in zip(hits, logs)]
-    inverse = 1.0 / over_pages(functools.reduce(jnp.add, factors), jnp.add)
+    own = sum(jnp.where(hit, jnp.exp(log - tops), 0.0) for hit, log in zip(hits, own_logs))
+    own = over_pages(own, jnp.add)
+    inverse = 1.0 / (over_pages(functools.reduce(jnp.add, factors), jnp.add) + own)
+    own_share = own * inverse
     shares = []
     for factor in factors:
         share = factor * inverse
@@ -677,7 +698,12 @@
         )
         mixed = part if mixed is None else mixed + part
     attended = jnp.concatenate(
-        [mixed[h * requests : (h + 1) * requests] for h in range(QH)], axis=1
+        [
+            mixed[h * requests : (h + 1) * requests]
+            + own_share[:, h : h + 1] * fresh[KVH + h // (QH // KVH)]
+            for h in range(QH)
+        ],
+        axis=1,
     ).astype(bf16)
     total = jnp.dot(attended, weights[...], preferred_element_type=f32)
     final[...] = (middle[...] + total).astype(bf16)
@@ -773,7 +799,7 @@
     new_state = call(state_kernel, shape(state.shape, f32), [SMEM] + [NEAR] * 6)(
         position, group_conv, other, conv, step, decay, state_in
     )
-    chunk = w_qkv.shape[1] // chunks
+    chunk = (QH + KVH) * HD // chunks
     keep, give, middle = call(
         functools.partial(project_kernel, chunks, head_width),
         (
@@ -827,6 +853,7 @@
         and (count // 2) % (LANES // (kv_cache.shape[0] * QH)) == 0
         and kv_cache.shape[1] == LANES
         and 2 * KVH == count
+        and (QH + KVH) * HD % (SUB // kv_cache.shape[0] * 2 * HD) == 0
     )
     return (fused_shards if whole_tiles else plain_shards)(*args)
 

time: 50.7 us -> 49.9 us (0.984)
  blocking collectives: 33.2 us -> 32.5 us
    all_to_all x2, blocking collectives: 22.1 us -> 21.4 us  [fused_shards(): received = lax.all_to_all(sent, 'seq', 0, 0, axis_index_groups=same_core)]
where the time goes in v7:
time: 49.9 us; the launch traced here: 49.6 us
  blocking collectives  32.5 us (65%)
  Pallas kernels  8.79 us (18%)
  starting transfers between devices  4.2 us (8%)
  between operations  2.66 us (5%)
  waiting for transfers between devices  1.31 us (3%)
    all_to_all x2, blocking collectives, fused_shards(): received = lax.all_to_all(sent, 'seq', 0, 0, axis_index_groups=same_core)  21.4 us
    all_to_all x1, blocking collectives, fused_shards(): received = lax.all_to_all(sent, 'seq', 0, 0)  11.1 us
    pallas_call x9, Pallas kernels, run(): return grid_free(*placed)  8.79 us
    ppermute x1, starting transfers between devices, fused_shards(): other = lax.ppermute(group_conv, 'seq', swap)  4.13 us
  transfers between devices with their start and end apart: 3, of which 2 were waited for; matrix products, arithmetic and copies ran while one was open for 0% of the time, Pallas kernels for 7%

profile of v7, /device:TPU:0, one launch (start us, length us, event | category | flops | bytes accessed | tf_op | source)
XLA Modules:
  0.0 49.6 jit_solution(10657007092691957828)
XLA Ops:
  0.6 1.6 %shard_map.220 = (bf16[8,128]{1,0:T(8,128)(2,1)S(1)}, bf16[8,4096]{1,0:T(8,128)(2,1)S(1)}) custom-call(bf16[8,4096]{1,0:T(8,128)(2,1)} %refs_5_.1, f32[1,4096]{1,0:T(1,128)} %bitcast.19, bf16[4096,128]{1,0:T(8,128)(2,1)} %weights_far.1, bf16[3,8,128]{2,1,0:T(8,128)(2,1)} %bitcast.21, f32[5,128]{1,0:T(8,128)} %taps_far.1), custom_call_target="tpu_custom_call" | custom-call | tf_op jit(solution)/shard_map/pallas_call | solution.py:258
  2.2 0.0 copy-start
  2.2 4.1 %collective-permute-start = (bf16[8,128]{1,0:T(8,128)(2,1)S(1)}, bf16[8,128]{1,0:T(8,128)(2,1)S(1)}, u32[]{:S(2)}, u32[]{:S(2)}) collective-permute-start(bf16[8,128]{1,0:T(8,128)(2,1)S(1)} %get-tuple-element.21.own), channel_id=1, source_target_pairs={{0,8},{1,9},{2,10},{3,11},{4,12},{5,13},{6,14},{7,15},{8,0},{9,1},... | collective-permute-start | bytes 6152 | tf_op jit(solution)/shard_map/ppermute | solution.py:763
  8.3 0.1 maximum_bitcast_fusion.refs_4_
  8.4 1.9 %shard_map.221 = (f32[8,64]{1,0:T(8,128)S(1)}, f32[8,128]{1,0:T(8,128)S(1)}, f32[8,128]{1,0:T(8,128)S(1)}, f32[8,128]{1,0:T(8,128)S(1)}, bf16[8,256]{1,0:T(8,128...) custom-call(s32[1]{0:T(128)} %bitcast.position, ...), custom_call_target="tpu_custom_call" | custom-call | tf_op jit(solution)/shard_map/pallas_call | solution.py:258
  10.3 0.0 collective-permute-done.other
  10.3 0.0 copy-start.2
  10.3 0.4 shard_map.222
  10.7 11.1 %all_to_all.15.received = bf16[16,8,384]{2,1,0:T(8,128)(2,1)S(1)} all-to-all(bf16[16,8,384]{2,1,0:T(8,128)(2,1)S(1)} %shard_map.222), channel_id=1, replica_groups=mesh['grp'=2,'seq'=16] {'seq'}, dimensions={0} | all-to-all | bytes 196608 | tf_op jit(solution)/shard_map/all_to_all | solution.py:798
  21.8 0.0 copy-done
  21.8 0.0 copy-start.3
  21.8 0.0 copy-start.1
  21.8 0.8 %shard_map.223 = (f32[8,8,1536]{2,1,0:T(8,128)S(1)}, bf16[8,8,1536]{2,1,0:T(8,128)(2,1)S(1)}, f32[8,256]{1,0:T(8,128)S(1)}) custom-call(s32[1]{0:T(128)} %bitcast.position, bf16[16,8,384]{2,1,0:T(8,128)(2,1)S(1)} %all_to_all.15.received, bf16[8,256]{1,0:T(8,128)(2,1)S(1)} %get-tuple-element.30.hidden, f32[1,256]{1,0:T(1,128)S(1)} %get-tuple-element.31.gain, ...), custom_call_target="tpu_custom_call" | custom-call | tf_op jit(solution)/shard_map/pallas_call | solution.py:258
  22.6 0.1 collective-permute-start.1
  22.7 0.9 %shard_map.224._ = f32[8,64,128]{2,1,0:T(8,128)} custom-call(s32[1]{0:T(128)} %bitcast.position, bf16[8,128]{1,0:T(8,128)(2,1)S(1)} %get-tuple-element.21.own, bf16[8,128]{1,0:T(8,128)(2,1)S(1)} %collective-permute-done.other, f32[8,128]{1,0:T(8,128)S(1)} %get-tuple-element.24.conv, f32[8,128]{1,0:T(8,128)S(1)} %get-tuple-element.25.step, ...), custom_call_target="tpu_custom_call" | custom-call | tf_op jit(solution)/shard_map/pallas_call | solution.py:258
  23.6 0.5 %collective-permute-done.1.taken = bf16[8,8,1536]{2,1,0:T(8,128)(2,1)S(1)} collective-permute-done((bf16[8,8,1536]{2,1,0:T(8,128)(2,1)S(1)}, bf16[8,8,1536]{2,1,0:T(8,128)(2,1)S(1)}, u32[]{:S(2)}, u32[]{:S(2)}) %collective-permute-start.1) | collective-permute-done | bytes 196640 | tf_op jit(solution)/shard_map/ppermute | solution.py:812
  24.1 0.2 shard_map.225
  24.3 10.9 %all_to_all.16.received = bf16[8,8,1536]{2,1,0:T(8,128)(2,1)S(1)} all-to-all(bf16[8,8,1536]{2,1,0:T(8,128)(2,1)S(1)} %shard_map.225), channel_id=1, replica_groups={{0,2,4,6,8,10,12,14},{1,3,5,7,9,11,13,15},{16,18,20,22,24,26,28,30},{17..., dimensions={0} | all-to-all | bytes 393216 | tf_op jit(solution)/shard_map/all_to_all | solution.py:814
  35.3 0.0 copy-done.2
  35.3 1.1 %shard_map.226 = bf16[8,80,128]{2,1,0:T(8,128)(2,1)S(1)} custom-call(s32[1]{0:T(128)} %bitcast.position, bf16[8,8,1536]{2,1,0:T(8,128)(2,1)S(1)} %all_to_all.16.received, bf16[2,128,2048]{2,1,0:T(8,128)(2,1)S(1)} %copy-done.2, s32[4,8]{1,0:T(4,128)S(1)} %get-tuple-element.32.table, s32[1,8]{1,0:T(1,128)S(1)} %get-tuple-element.35.lengths), custom_call_target="tpu_custom_call" | custom-call | tf_op jit(solution)/shard_map/pallas_call | solution.py:258
  36.3 10.5 %all_to_all.17._.near_ref = bf16[8,80,128]{2,1,0:T(8,128)(2,1)S(1)} all-to-all(bf16[8,80,128]{2,1,0:T(8,128)(2,1)S(1)} %shard_map.226), channel_id=1, replica_groups={{0,2,4,6,8,10,12,14},{1,3,5,7,9,11,13,15},{16,18,20,22,24,26,28,30},{17..., dimensions={0} | all-to-all | bytes 327680 | tf_op jit(solution)/shard_map/all_to_all | solution.py:822
  46.8 0.0 collective-permute-start.2
  46.8 0.0 copy-done.3
  46.8 0.6 %shard_map.227.owner = s32[8,128]{1,0:T(8,128)S(1)} custom-call(s32[1]{0:T(128)} %bitcast.position, s32[4,8]{1,0:T(4,128)S(1)} %bitcast.16, bf16[8,80,128]{2,1,0:T(8,128)(2,1)S(1)} %all_to_all.17._.near_ref), custom_call_target="tpu_custom_call" | custom-call | tf_op jit(solution)/shard_map/pallas_call | solution.py:258
  47.4 0.8 %collective-permute-done.2.far_ref = bf16[8,80,128]{2,1,0:T(8,128)(2,1)S(1)} collective-permute-done((bf16[8,80,128]{2,1,0:T(8,128)(2,1)S(1)}, bf16[8,80,128]{2,1,0:T(8,128)(2,1)S(1)}, u32[]{:S(2)}, u32[]{:S(2)}) %collective-permute-start.2) | collective-permute-done | bytes 163872 | tf_op jit(solution)/shard_map/ppermute | solution.py:823
  48.2 0.0 copy-done.1
  48.2 1.4 %shard_map.228 = (bf16[8,256]{1,0:T(8,128)(2,1)}, bf16[8,2048]{1,0:T(8,128)(2,1)}) custom-call(s32[1]{0:T(128)} %bitcast.position, bf16[8,80,128]{2,1,0:T(8,128)(2,1)S(1)} %all_to_all.17._.near_ref, bf16[8,80,128]{2,1,0:T(8,128)(2,1)S(1)} %collective-permute-done.2.far_ref, s32[8,128]{1,0:T(8,128)S(1)} %shard_map.227.owner, bf16[4096,256]{1,0:T(8,128)(2,1)S(1)} %copy-done.1, ...), custom_call_target="tpu_custom_call" | custom-call | tf_op jit(solution)/shard_map/pallas_call | solution.py:258
Async XLA Ops:
  2.2 19.6 %copy-start = (bf16[256,6144]{1,0:T(8,128)(2,1)S(1)}, bf16[256,6144]{1,0:T(8,128)(2,1)}, u32[]{:S(2)}) copy-start(bf16[256,6144]{1,0:T(8,128)(2,1)} %weights.2) | copy-start | bytes 9437188
  2.2 8.0 %collective-permute-start = (bf16[8,128]{1,0:T(8,128)(2,1)S(1)}, bf16[8,128]{1,0:T(8,128)(2,1)S(1)}, u32[]{:S(2)}, u32[]{:S(2)}) collective-permute-start(bf16[8,128]{1,0:T(8,128)(2,1)S(1)} %get-tuple-element.21.own), channel_id=1, source_target_pairs={{0,8},{1,9},{2,10},{3,11},{4,12},{5,13},{6,14},{7,15},{8,0},{9,1},... | collective-permute-start | bytes 6152 | tf_op jit(solution)/shard_map/ppermute | solution.py:763
  10.3 25.0 %copy-start.2 = (bf16[2,128,2048]{2,1,0:T(8,128)(2,1)S(1)}, bf16[2,128,2048]{2,1,0:T(8,128)(2,1)}, u32[]{:S(2)}) copy-start(bf16[2,128,2048]{2,1,0:T(8,128)(2,1)} %cache.1) | copy-start | bytes 3145732
  21.8 25.0 %copy-start.3 = (s32[8,4]{0,1:T(4,128)S(1)}, s32[8,4]{0,1:T(4,128)}, u32[]{:S(2)}) copy-start(s32[8,4]{0,1:T(4,128)} %param.40) | copy-start | bytes 388
  21.8 26.4 %copy-start.1 = (bf16[4096,256]{1,0:T(8,128)(2,1)S(1)}, bf16[4096,256]{1,0:T(8,128)(2,1)}, u32[]{:S(2)}) copy-start(bf16[4096,256]{1,0:T(8,128)(2,1)} %weights.3) | copy-start | bytes 6291460
  22.6 1.5 %collective-permute-start.1 = (bf16[8,8,1536]{2,1,0:T(8,128)(2,1)S(1)}, bf16[8,8,1536]{2,1,0:T(8,128)(2,1)S(1)}, u32[]{:S(2)}, u32[]{:S(2)}) collective-permute-start(bf16[8,8,1536]{2,1,0:T(8,128)(2,1)S(1)} %get-tuple-element.34), channel_id=1, source_target_pairs={{0,1},{1,0},{2,3},{3,2},{4,5},{5,4},{6,7},{7,6},{8,9},{9,8},{10,11... | collective-permute-start | bytes 589832 | tf_op jit(solution)/shard_map/ppermute | solution.py:812
  46.8 1.4 %collective-permute-start.2 = (bf16[8,80,128]{2,1,0:T(8,128)(2,1)S(1)}, bf16[8,80,128]{2,1,0:T(8,128)(2,1)S(1)}, u32[]{:S(2)}, u32[]{:S(2)}) collective-permute-start(bf16[8,80,128]{2,1,0:T(8,128)(2,1)S(1)} %all_to_all.17._.near_ref), channel_id=1, source_target_pairs={{0,1},{1,0},{2,3},{3,2},{4,5},{5,4},{6,7},{7,6},{8,9},{9,8},{10,11... | collective-permute-start | bytes 491528 | tf_op jit(solution)/shard_map/ppermute | solution.py:823

commit v8 on v7

--- a/solution.py
+++ b/solution.py
@@ -431,7 +431,18 @@
         sent[e, :, columns:] = marks
 
 
-def state_kernel(position, own, other, conv, step, decay, state, new_state):
+def state_kernel(
+    pages, page_len, position, own, other, conv, step, decay, state, table, lengths, new_state, bounds
+):
+    order = lax.broadcasted_iota(jnp.int32, table.shape, 0)
+    spans = jnp.broadcast_to(lengths[...], table.shape)
+    for p in range(pages):
+        hit = table[...] == position[0] * pages + p
+        logical = jnp.sum(jnp.where(hit, order, 0), axis=(0, 1), keepdims=True)
+        length = jnp.sum(jnp.where(hit, spans, 0), axis=(0, 1), keepdims=True)
+        lane = jnp.zeros((1, LANES), jnp.int32)
+        bounds[p : p + 1, :] = lane + (length - logical * page_len)
+        bounds[pages + p : pages + p + 1, :] = lane + jnp.where(logical == 0, 1, 0)
     inject, _ = chosen(position, own, other)
     fresh = step[:, :1] * conv[:, : state.shape[1]]
     new_state[...] = (
@@ -529,7 +540,7 @@
         sent[e, :, chunk + LANES :] = total[:, chunk + LANES :].astype(bf16)
 
 
-def attend_kernel(width, position, received, cache, table, lengths, sent, lines):
+def attend_kernel(width, position, received, cache, bounds, sent, lines):
     count, _, full = received.shape
     pages, page_len, _ = cache.shape
     chunks = SUB // pages
@@ -564,20 +575,11 @@
     value_rows = pages * QH
     place = (position[0] // 2) % (LANES // value_rows) * value_rows
     eye_lane = lax.broadcasted_iota(jnp.int32, (QH, LANES), 1) - place
-    order = lax.broadcasted_iota(jnp.int32, table.shape, 0)
     log_row = jnp.zeros((1, LANES), f32)
     own_row = jnp.zeros((1, LANES), f32)
     for p in range(pages):
-        slot = position[0] * pages + p
-        hit = table[...] == slot
-        logical = jnp.sum(jnp.where(hit, order, 0), axis=(0, 1), keepdims=True)
-        length = jnp.sum(
-            jnp.where(hit, jnp.broadcast_to(lengths[...], hit.shape), 0),
-            axis=(0, 1),
-            keepdims=True,
-        )
-        live = logical * page_len + lane < length
-        leads = logical == 0
+        live = lane < bounds[p : p + 1, :]
+        leads = bounds[pages + p : pages + p + 1, :1] == 1
         query = jnp.concatenate([heads(p, g * group, group) for g in range(KVH)], axis=0)
         keys = [heads(p, QH + g, 1) for g in range(KVH)]
         key_rows = jnp.concatenate([jnp.broadcast_to(k, (group, HD)) for k in keys], axis=0)
@@ -796,9 +798,11 @@
         [SMEM] + [NEAR] * 9,
     )(position, group_conv, other, gate, conv, step, decay, state_in, mixer, gain)
     received = lax.all_to_all(sent, "seq", 0, 0)
-    new_state = call(state_kernel, shape(state.shape, f32), [SMEM] + [NEAR] * 6)(
-        position, group_conv, other, conv, step, decay, state_in
-    )
+    new_state, bounds = call(
+        functools.partial(state_kernel, pages, kv_cache.shape[1]),
+        (shape(state.shape, f32), near((SUB, LANES), jnp.int32)),
+        [SMEM] + [NEAR] * 8,
+    )(position, group_conv, other, conv, step, decay, state_in, table, spans)
     chunk = (QH + KVH) * HD // chunks
     keep, give, middle = call(
         functools.partial(project_kernel, chunks, head_width),
@@ -816,9 +820,9 @@
     sent = call(
         functools.partial(attend_kernel, width),
         near((chips, package, HD), bf16),
-        [SMEM] + [NEAR] * 4,
+        [SMEM] + [NEAR] * 3,
         [pltpu.VMEM((chunk // HD * SUB, HD), f32)],
-    )(position, received, kv_cache, table, spans)
+    )(position, received, kv_cache, bounds)
     received = lax.all_to_all(sent, "seq", 0, 0, axis_index_groups=same_core)
     far = lax.ppermute(received, "seq", cores)
     owner_rows = count * pages * QH // LANES

time: 49.9 us -> 49.8 us (level)
  no operation moved by 1% of the time
where the time goes in v8:
time: 49.8 us; the launch traced here: 49.5 us
  blocking collectives  32.5 us (65%)
  Pallas kernels  8.81 us (18%)
  starting transfers between devices  4.2 us (8%)
  between operations  2.66 us (5%)
  waiting for transfers between devices  1.26 us (3%)
    all_to_all x2, blocking collectives, fused_shards(): received = lax.all_to_all(sent, 'seq', 0, 0, axis_index_groups=same_core)  21.4 us
    all_to_all x1, blocking collectives, fused_shards(): received = lax.all_to_all(sent, 'seq', 0, 0)  11.1 us
    pallas_call x9, Pallas kernels, run(): return grid_free(*placed)  8.81 us
    ppermute x1, starting transfers between devices, fused_shards(): other = lax.ppermute(group_conv, 'seq', swap)  4.13 us
  transfers between devices with their start and end apart: 3, of which 2 were waited for; matrix products, arithmetic and copies ran while one was open for 0% of the time, Pallas kernels for 7%

profile of v8, /device:TPU:0, one launch (start us, length us, event | category | flops | bytes accessed | tf_op | source)
XLA Modules:
  0.0 49.5 jit_solution(6009629679726127279)
XLA Ops:
  0.6 1.6 %shard_map.220 = (bf16[8,128]{1,0:T(8,128)(2,1)S(1)}, bf16[8,4096]{1,0:T(8,128)(2,1)S(1)}) custom-call(bf16[8,4096]{1,0:T(8,128)(2,1)} %refs_5_.1, f32[1,4096]{1,0:T(1,128)} %bitcast.19, bf16[4096,128]{1,0:T(8,128)(2,1)} %weights_far.1, bf16[3,8,128]{2,1,0:T(8,128)(2,1)} %bitcast.21, f32[5,128]{1,0:T(8,128)} %taps_far.1), custom_call_target="tpu_custom_call" | custom-call | tf_op jit(solution)/shard_map/pallas_call | solution.py:258
  2.2 0.0 copy-start
  2.2 4.1 %collective-permute-start = (bf16[8,128]{1,0:T(8,128)(2,1)S(1)}, bf16[8,128]{1,0:T(8,128)(2,1)S(1)}, u32[]{:S(2)}, u32[]{:S(2)}) collective-permute-start(bf16[8,128]{1,0:T(8,128)(2,1)S(1)} %get-tuple-element.23.own), channel_id=1, source_target_pairs={{0,8},{1,9},{2,10},{3,11},{4,12},{5,13},{6,14},{7,15},{8,0},{9,1},... | collective-permute-start | bytes 6152 | tf_op jit(solution)/shard_map/ppermute | solution.py:765
  8.3 0.1 maximum_bitcast_fusion.refs_4_
  8.4 1.9 %shard_map.221 = (f32[8,64]{1,0:T(8,128)S(1)}, f32[8,128]{1,0:T(8,128)S(1)}, f32[8,128]{1,0:T(8,128)S(1)}, f32[8,128]{1,0:T(8,128)S(1)}, bf16[8,256]{1,0:T(8,128...) custom-call(s32[1]{0:T(128)} %bitcast.position, ...), custom_call_target="tpu_custom_call" | custom-call | tf_op jit(solution)/shard_map/pallas_call | solution.py:258
  10.3 0.0 copy-start.2
  10.3 0.0 collective-permute-done.other
  10.3 0.4 shard_map.222
  10.7 11.1 %all_to_all.15.received = bf16[16,8,384]{2,1,0:T(8,128)(2,1)S(1)} all-to-all(bf16[16,8,384]{2,1,0:T(8,128)(2,1)S(1)} %shard_map.222), channel_id=1, replica_groups=mesh['grp'=2,'seq'=16] {'seq'}, dimensions={0} | all-to-all | bytes 196608 | tf_op jit(solution)/shard_map/all_to_all | solution.py:800
  21.8 0.0 copy-done
  21.8 0.0 copy-start.3
  21.8 0.0 copy-start.1
  21.8 0.8 %shard_map.223 = (f32[8,8,1536]{2,1,0:T(8,128)S(1)}, bf16[8,8,1536]{2,1,0:T(8,128)(2,1)S(1)}, f32[8,256]{1,0:T(8,128)S(1)}) custom-call(s32[1]{0:T(128)} %bitcast.position, bf16[16,8,384]{2,1,0:T(8,128)(2,1)S(1)} %all_to_all.15.received, bf16[8,256]{1,0:T(8,128)(2,1)S(1)} %get-tuple-element.32.hidden, f32[1,256]{1,0:T(1,128)S(1)} %get-tuple-element.33.gain, ...), custom_call_target="tpu_custom_call" | custom-call | tf_op jit(solution)/shard_map/pallas_call | solution.py:258
  22.6 0.1 collective-permute-start.1
  22.7 1.0 %shard_map.224 = (f32[8,64,128]{2,1,0:T(8,128)}, s32[8,128]{1,0:T(8,128)S(1)}) custom-call(s32[1]{0:T(128)} %bitcast.position, bf16[8,128]{1,0:T(8,128)(2,1)S(1)} %get-tuple-element.23.own, bf16[8,128]{1,0:T(8,128)(2,1)S(1)} %collective-permute-done.other, f32[8,128]{1,0:T(8,128)S(1)} %get-tuple-element.26.conv, f32[8,128]{1,0:T(8,128)S(1)} %get-tuple-element.27.step, ...), custom_call_target="tpu_custom_call" | custom-call | tf_op jit(solution)/shard_map/pallas_call | solution.py:258
  23.7 0.5 collective-permute-done.1.taken
  24.1 0.2 shard_map.225
  24.3 10.9 %all_to_all.16.received = bf16[8,8,1536]{2,1,0:T(8,128)(2,1)S(1)} all-to-all(bf16[8,8,1536]{2,1,0:T(8,128)(2,1)S(1)} %shard_map.225), channel_id=1, replica_groups={{0,2,4,6,8,10,12,14},{1,3,5,7,9,11,13,15},{16,18,20,22,24,26,28,30},{17..., dimensions={0} | all-to-all | bytes 393216 | tf_op jit(solution)/shard_map/all_to_all | solution.py:818
  35.3 0.0 copy-done.2
  35.3 1.0 %shard_map.226 = bf16[8,80,128]{2,1,0:T(8,128)(2,1)S(1)} custom-call(s32[1]{0:T(128)} %bitcast.position, bf16[8,8,1536]{2,1,0:T(8,128)(2,1)S(1)} %all_to_all.16.received, bf16[2,128,2048]{2,1,0:T(8,128)(2,1)S(1)} %copy-done.2, s32[8,128]{1,0:T(8,128)S(1)} %get-tuple-element.39.bounds), custom_call_target="tpu_custom_call" | custom-call | tf_op jit(solution)/shard_map/pallas_call | solution.py:258
  36.3 10.5 %all_to_all.17._.near_ref = bf16[8,80,128]{2,1,0:T(8,128)(2,1)S(1)} all-to-all(bf16[8,80,128]{2,1,0:T(8,128)(2,1)S(1)} %shard_map.226), channel_id=1, replica_groups={{0,2,4,6,8,10,12,14},{1,3,5,7,9,11,13,15},{16,18,20,22,24,26,28,30},{17..., dimensions={0} | all-to-all | bytes 327680 | tf_op jit(solution)/shard_map/all_to_all | solution.py:826
  46.8 0.0 collective-permute-start.2
  46.8 0.0 copy-done.3
  46.8 0.6 %shard_map.227.owner = s32[8,128]{1,0:T(8,128)S(1)} custom-call(s32[1]{0:T(128)} %bitcast.position, s32[4,8]{1,0:T(4,128)S(1)} %bitcast.16, bf16[8,80,128]{2,1,0:T(8,128)(2,1)S(1)} %all_to_all.17._.near_ref), custom_call_target="tpu_custom_call" | custom-call | tf_op jit(solution)/shard_map/pallas_call | solution.py:258
  47.4 0.8 %collective-permute-done.2.far_ref = bf16[8,80,128]{2,1,0:T(8,128)(2,1)S(1)} collective-permute-done((bf16[8,80,128]{2,1,0:T(8,128)(2,1)S(1)}, bf16[8,80,128]{2,1,0:T(8,128)(2,1)S(1)}, u32[]{:S(2)}, u32[]{:S(2)}) %collective-permute-start.2) | collective-permute-done | bytes 163872 | tf_op jit(solution)/shard_map/ppermute | solution.py:827
  48.2 0.0 copy-done.1
  48.2 1.4 %shard_map.228 = (bf16[8,256]{1,0:T(8,128)(2,1)}, bf16[8,2048]{1,0:T(8,128)(2,1)}) custom-call(s32[1]{0:T(128)} %bitcast.position, bf16[8,80,128]{2,1,0:T(8,128)(2,1)S(1)} %all_to_all.17._.near_ref, bf16[8,80,128]{2,1,0:T(8,128)(2,1)S(1)} %collective-permute-done.2.far_ref, s32[8,128]{1,0:T(8,128)S(1)} %shard_map.227.owner, bf16[4096,256]{1,0:T(8,128)(2,1)S(1)} %copy-done.1, ...), custom_call_target="tpu_custom_call" | custom-call | tf_op jit(solution)/shard_map/pallas_call | solution.py:258
Async XLA Ops:
  2.2 19.6 %copy-start = (bf16[256,6144]{1,0:T(8,128)(2,1)S(1)}, bf16[256,6144]{1,0:T(8,128)(2,1)}, u32[]{:S(2)}) copy-start(bf16[256,6144]{1,0:T(8,128)(2,1)} %weights.2) | copy-start | bytes 9437188
  2.2 8.0 %collective-permute-start = (bf16[8,128]{1,0:T(8,128)(2,1)S(1)}, bf16[8,128]{1,0:T(8,128)(2,1)S(1)}, u32[]{:S(2)}, u32[]{:S(2)}) collective-permute-start(bf16[8,128]{1,0:T(8,128)(2,1)S(1)} %get-tuple-element.23.own), channel_id=1, source_target_pairs={{0,8},{1,9},{2,10},{3,11},{4,12},{5,13},{6,14},{7,15},{8,0},{9,1},... | collective-permute-start | bytes 6152 | tf_op jit(solution)/shard_map/ppermute | solution.py:765
  10.3 25.0 %copy-start.2 = (bf16[2,128,2048]{2,1,0:T(8,128)(2,1)S(1)}, bf16[2,128,2048]{2,1,0:T(8,128)(2,1)}, u32[]{:S(2)}) copy-start(bf16[2,128,2048]{2,1,0:T(8,128)(2,1)} %cache.1) | copy-start | bytes 3145732
  21.8 25.0 %copy-start.3 = (s32[8,4]{0,1:T(4,128)S(1)}, s32[8,4]{0,1:T(4,128)}, u32[]{:S(2)}) copy-start(s32[8,4]{0,1:T(4,128)} %param.40) | copy-start | bytes 388
  21.8 26.4 %copy-start.1 = (bf16[4096,256]{1,0:T(8,128)(2,1)S(1)}, bf16[4096,256]{1,0:T(8,128)(2,1)}, u32[]{:S(2)}) copy-start(bf16[4096,256]{1,0:T(8,128)(2,1)} %weights.3) | copy-start | bytes 6291460
  22.6 1.5 %collective-permute-start.1 = (bf16[8,8,1536]{2,1,0:T(8,128)(2,1)S(1)}, bf16[8,8,1536]{2,1,0:T(8,128)(2,1)S(1)}, u32[]{:S(2)}, u32[]{:S(2)}) collective-permute-start(bf16[8,8,1536]{2,1,0:T(8,128)(2,1)S(1)} %get-tuple-element.36), channel_id=1, source_target_pairs={{0,1},{1,0},{2,3},{3,2},{4,5},{5,4},{6,7},{7,6},{8,9},{9,8},{10,11... | collective-permute-start | bytes 589832 | tf_op jit(solution)/shard_map/ppermute | solution.py:816
  46.8 1.4 %collective-permute-start.2 = (bf16[8,80,128]{2,1,0:T(8,128)(2,1)S(1)}, bf16[8,80,128]{2,1,0:T(8,128)(2,1)S(1)}, u32[]{:S(2)}, u32[]{:S(2)}) collective-permute-start(bf16[8,80,128]{2,1,0:T(8,128)(2,1)S(1)} %all_to_all.17._.near_ref), channel_id=1, source_target_pairs={{0,1},{1,0},{2,3},{3,2},{4,5},{5,4},{6,7},{7,6},{8,9},{9,8},{10,11... | collective-permute-start | bytes 491528 | tf_op jit(solution)/shard_map/ppermute | solution.py:827

commit v9 on v8

--- a/solution.py
+++ b/solution.py
@@ -233,6 +233,7 @@
 SCOPED = 16 << 20
 MOST = 63500 << 10
 BLOCKS = 2
+GATE_BLOCKS = 1
 VMEM = pl.BlockSpec(memory_space=pltpu.VMEM)
 NEAR = pl.BlockSpec(memory_space=pltpu.VMEM)
 SMEM = pl.BlockSpec(memory_space=pltpu.SMEM)
@@ -356,8 +357,8 @@
     weights, step_row, state, taps, sems = scratch
     columns = columns_out.shape[1]
     start = pl.multiple_of(position[0] * columns, columns)
-    depth = weights.shape[0] // BLOCKS
-    rows = [pl.ds(k * depth, depth) for k in range(BLOCKS)]
+    depth = weights.shape[0] // GATE_BLOCKS
+    rows = [pl.ds(k * depth, depth) for k in range(GATE_BLOCKS)]
     copies = fetch_all(
         [(weights_far.at[r], weights.at[r]) for r in rows]
         + [
@@ -371,11 +372,11 @@
     )
     half = gate_out.shape[1]
     both = jnp.zeros((gate_out.shape[0], weights.shape[1]), f32)
-    for k in range(BLOCKS):
+    for k in range(GATE_BLOCKS):
         copies[k].wait()
         span = slice(k * depth, (k + 1) * depth)
         both = both + jnp.dot(normed_ref[:, span], weights[span, :], preferred_element_type=f32)
-    for copy in copies[BLOCKS : BLOCKS + 3]:
+    for copy in copies[GATE_BLOCKS : GATE_BLOCKS + 3]:
         copy.wait()
     gate_out[...] = silu(both[:, :half])
     fresh = convolve(state, both[:, half:], taps)
@@ -385,7 +386,7 @@
     step = jax.nn.softplus(raw + numbers[:, 1:2])
     step_out[...] = jnp.broadcast_to(step, step_out.shape)
     decay_out[...] = jnp.broadcast_to(jnp.exp(-numbers[:, 0:1] * step), decay_out.shape)
-    for copy in copies[BLOCKS + 3 :]:
+    for copy in copies[GATE_BLOCKS + 3 :]:
         copy.wait()
 
 
@@ -769,7 +770,6 @@
         norm_gain.reshape(1, head_width),
         attn_gain.reshape(1, columns),
         page_table.T,
-        lengths.reshape(1, requests),
     )
     gate_args = (
         in_gate_input,
@@ -778,7 +778,7 @@
         taps_input,
     )
     numbers = jnp.concatenate([decay_rate, step_bias, skip_gain]).reshape(1, 3)
-    gate, conv, step, decay, stream, state_in, mixer, gain, scale, table, spans = call(
+    gate, conv, step, decay, stream, state_in, mixer, gain, scale, table = call(
         functools.partial(gate_kernel, len(carried)),
         (
             near((requests, head_width), f32),
@@ -790,7 +790,7 @@
         + tuple(near(x.shape, x.dtype) for x in carried),
         [SMEM, NEAR] + [FAR] * 4 + [NEAR] + [FAR] * (1 + len(carried)),
         [pltpu.VMEM(x.shape, x.dtype) for x in gate_args]
-        + [pltpu.SemaphoreType.DMA((BLOCKS + 4 + len(carried),))],
+        + [pltpu.SemaphoreType.DMA((GATE_BLOCKS + 4 + len(carried),))],
     )(position, normed, *gate_args, numbers, hidden, *carried)
     sent = call(
         mixer_kernel,
@@ -801,8 +801,8 @@
     new_state, bounds = call(
         functools.partial(state_kernel, pages, kv_cache.shape[1]),
         (shape(state.shape, f32), near((SUB, LANES), jnp.int32)),
-        [SMEM] + [NEAR] * 8,
-    )(position, group_conv, other, conv, step, decay, state_in, table, spans)
+        [SMEM] + [NEAR] * 7 + [VMEM],
+    )(position, group_conv, other, conv, step, decay, state_in, table, lengths.reshape(1, requests))
     chunk = (QH + KVH) * HD // chunks
     keep, give, middle = call(
         functools.partial(project_kernel, chunks, head_width),

time: 49.8 us -> 49.9 us (level)
  no operation moved by 1% of the time
where the time goes in v9:
time: 49.9 us; the launch traced here: 49.6 us
  blocking collectives  32.5 us (65%)
  Pallas kernels  8.83 us (18%)
  starting transfers between devices  4.2 us (8%)
  between operations  2.67 us (5%)
  waiting for transfers between devices  1.25 us (3%)
    all_to_all x2, blocking collectives, fused_shards(): received = lax.all_to_all(sent, 'seq', 0, 0, axis_index_groups=same_core)  21.4 us
    all_to_all x1, blocking collectives, fused_shards(): received = lax.all_to_all(sent, 'seq', 0, 0)  11.1 us
    pallas_call x9, Pallas kernels, run(): return grid_free(*placed)  8.83 us
    ppermute x1, starting transfers between devices, fused_shards(): other = lax.ppermute(group_conv, 'seq', swap)  4.13 us
  transfers between devices with their start and end apart: 3, of which 2 were waited for; matrix products, arithmetic and copies ran while one was open for 0% of the time, Pallas kernels for 7%

profile of v9, /device:TPU:0, one launch (start us, length us, event | category | flops | bytes accessed | tf_op | source)
XLA Modules:
  0.0 49.6 jit_solution(10247911158120608102)
XLA Ops:
  0.6 1.6 %shard_map.220 = (bf16[8,128]{1,0:T(8,128)(2,1)S(1)}, bf16[8,4096]{1,0:T(8,128)(2,1)S(1)}) custom-call(bf16[8,4096]{1,0:T(8,128)(2,1)} %refs_5_.1, f32[1,4096]{1,0:T(1,128)} %bitcast.20, bf16[4096,128]{1,0:T(8,128)(2,1)} %weights_far.1, bf16[3,8,128]{2,1,0:T(8,128)(2,1)} %bitcast.22, f32[5,128]{1,0:T(8,128)} %taps_far.1), custom_call_target="tpu_custom_call" | custom-call | tf_op jit(solution)/shard_map/pallas_call | solution.py:259
  2.2 0.0 copy-start
  2.2 4.1 %collective-permute-start = (bf16[8,128]{1,0:T(8,128)(2,1)S(1)}, bf16[8,128]{1,0:T(8,128)(2,1)S(1)}, u32[]{:S(2)}, u32[]{:S(2)}) collective-permute-start(bf16[8,128]{1,0:T(8,128)(2,1)S(1)} %get-tuple-element.22.own), channel_id=1, source_target_pairs={{0,8},{1,9},{2,10},{3,11},{4,12},{5,13},{6,14},{7,15},{8,0},{9,1},... | collective-permute-start | bytes 6152 | tf_op jit(solution)/shard_map/ppermute | solution.py:766
  8.3 0.1 maximum_bitcast_fusion.refs_4_
  8.4 0.0 copy-start.4
  8.4 1.9 %shard_map.221 = (f32[8,64]{1,0:T(8,128)S(1)}, f32[8,128]{1,0:T(8,128)S(1)}, f32[8,128]{1,0:T(8,128)S(1)}, f32[8,128]{1,0:T(8,128)S(1)}, bf16[8,256]{1,0:T(8,128...) custom-call(s32[1]{0:T(128)} %bitcast.position, ...), custom_call_target="tpu_custom_call" | custom-call | tf_op jit(solution)/shard_map/pallas_call | solution.py:259
  10.3 0.0 copy-start.2
  10.3 0.0 collective-permute-done.other
  10.3 0.4 shard_map.222
  10.7 11.1 %all_to_all.15.received = bf16[16,8,384]{2,1,0:T(8,128)(2,1)S(1)} all-to-all(bf16[16,8,384]{2,1,0:T(8,128)(2,1)S(1)} %shard_map.222), channel_id=1, replica_groups=mesh['grp'=2,'seq'=16] {'seq'}, dimensions={0} | all-to-all | bytes 196608 | tf_op jit(solution)/shard_map/all_to_all | solution.py:800
  21.8 0.0 copy-done
  21.8 0.0 copy-start.3
  21.8 0.0 copy-start.1
  21.8 0.8 %shard_map.223 = (f32[8,8,1536]{2,1,0:T(8,128)S(1)}, bf16[8,8,1536]{2,1,0:T(8,128)(2,1)S(1)}, f32[8,256]{1,0:T(8,128)S(1)}) custom-call(s32[1]{0:T(128)} %bitcast.position, bf16[16,8,384]{2,1,0:T(8,128)(2,1)S(1)} %all_to_all.15.received, bf16[8,256]{1,0:T(8,128)(2,1)S(1)} %get-tuple-element.31.hidden, f32[1,256]{1,0:T(1,128)S(1)} %get-tuple-element.32.gain, ...), custom_call_target="tpu_custom_call" | custom-call | tf_op jit(solution)/shard_map/pallas_call | solution.py:259
  22.6 0.1 collective-permute-start.1
  22.7 0.0 copy-done.4
  22.7 1.0 %shard_map.224 = (f32[8,64,128]{2,1,0:T(8,128)}, s32[8,128]{1,0:T(8,128)S(1)}) custom-call(s32[1]{0:T(128)} %bitcast.position, bf16[8,128]{1,0:T(8,128)(2,1)S(1)} %get-tuple-element.22.own, bf16[8,128]{1,0:T(8,128)(2,1)S(1)} %collective-permute-done.other, f32[8,128]{1,0:T(8,128)S(1)} %get-tuple-element.25.conv, f32[8,128]{1,0:T(8,128)S(1)} %get-tuple-element.26.step, ...), custom_call_target="tpu_custom_call" | custom-call | tf_op jit(solution)/shard_map/pallas_call | solution.py:259
  23.7 0.5 collective-permute-done.1.taken
  24.2 0.2 shard_map.225
  24.3 10.9 %all_to_all.16.received = bf16[8,8,1536]{2,1,0:T(8,128)(2,1)S(1)} all-to-all(bf16[8,8,1536]{2,1,0:T(8,128)(2,1)S(1)} %shard_map.225), channel_id=1, replica_groups={{0,2,4,6,8,10,12,14},{1,3,5,7,9,11,13,15},{16,18,20,22,24,26,28,30},{17..., dimensions={0} | all-to-all | bytes 393216 | tf_op jit(solution)/shard_map/all_to_all | solution.py:818
  35.3 0.0 copy-done.2
  35.3 1.0 %shard_map.226 = bf16[8,80,128]{2,1,0:T(8,128)(2,1)S(1)} custom-call(s32[1]{0:T(128)} %bitcast.position, bf16[8,8,1536]{2,1,0:T(8,128)(2,1)S(1)} %all_to_all.16.received, bf16[2,128,2048]{2,1,0:T(8,128)(2,1)S(1)} %copy-done.2, s32[8,128]{1,0:T(8,128)S(1)} %get-tuple-element.37.bounds), custom_call_target="tpu_custom_call" | custom-call | tf_op jit(solution)/shard_map/pallas_call | solution.py:259
  36.3 10.5 %all_to_all.17._.near_ref = bf16[8,80,128]{2,1,0:T(8,128)(2,1)S(1)} all-to-all(bf16[8,80,128]{2,1,0:T(8,128)(2,1)S(1)} %shard_map.226), channel_id=1, replica_groups={{0,2,4,6,8,10,12,14},{1,3,5,7,9,11,13,15},{16,18,20,22,24,26,28,30},{17..., dimensions={0} | all-to-all | bytes 327680 | tf_op jit(solution)/shard_map/all_to_all | solution.py:826
  46.8 0.0 collective-permute-start.2
  46.8 0.0 copy-done.3
  46.8 0.6 %shard_map.227.owner = s32[8,128]{1,0:T(8,128)S(1)} custom-call(s32[1]{0:T(128)} %bitcast.position, s32[4,8]{1,0:T(4,128)S(1)} %bitcast.16, bf16[8,80,128]{2,1,0:T(8,128)(2,1)S(1)} %all_to_all.17._.near_ref), custom_call_target="tpu_custom_call" | custom-call | tf_op jit(solution)/shard_map/pallas_call | solution.py:259
  47.4 0.8 %collective-permute-done.2.far_ref = bf16[8,80,128]{2,1,0:T(8,128)(2,1)S(1)} collective-permute-done((bf16[8,80,128]{2,1,0:T(8,128)(2,1)S(1)}, bf16[8,80,128]{2,1,0:T(8,128)(2,1)S(1)}, u32[]{:S(2)}, u32[]{:S(2)}) %collective-permute-start.2) | collective-permute-done | bytes 163872 | tf_op jit(solution)/shard_map/ppermute | solution.py:827
  48.2 0.0 copy-done.1
  48.2 1.4 %shard_map.228 = (bf16[8,256]{1,0:T(8,128)(2,1)}, bf16[8,2048]{1,0:T(8,128)(2,1)}) custom-call(s32[1]{0:T(128)} %bitcast.position, bf16[8,80,128]{2,1,0:T(8,128)(2,1)S(1)} %all_to_all.17._.near_ref, bf16[8,80,128]{2,1,0:T(8,128)(2,1)S(1)} %collective-permute-done.2.far_ref, s32[8,128]{1,0:T(8,128)S(1)} %shard_map.227.owner, bf16[4096,256]{1,0:T(8,128)(2,1)S(1)} %copy-done.1, ...), custom_call_target="tpu_custom_call" | custom-call | tf_op jit(solution)/shard_map/pallas_call | solution.py:259
Async XLA Ops:
  2.2 19.6 %copy-start = (bf16[256,6144]{1,0:T(8,128)(2,1)S(1)}, bf16[256,6144]{1,0:T(8,128)(2,1)}, u32[]{:S(2)}) copy-start(bf16[256,6144]{1,0:T(8,128)(2,1)} %weights.2) | copy-start | bytes 9437188
  2.2 8.1 %collective-permute-start = (bf16[8,128]{1,0:T(8,128)(2,1)S(1)}, bf16[8,128]{1,0:T(8,128)(2,1)S(1)}, u32[]{:S(2)}, u32[]{:S(2)}) collective-permute-start(bf16[8,128]{1,0:T(8,128)(2,1)S(1)} %get-tuple-element.22.own), channel_id=1, source_target_pairs={{0,8},{1,9},{2,10},{3,11},{4,12},{5,13},{6,14},{7,15},{8,0},{9,1},... | collective-permute-start | bytes 6152 | tf_op jit(solution)/shard_map/ppermute | solution.py:766
  8.4 14.3 %copy-start.4 = (s32[8]{0:T(128)S(1)}, s32[8]{0:T(128)}, u32[]{:S(2)}) copy-start(s32[8]{0:T(128)} %param.41) | copy-start | bytes 100
  10.3 25.0 %copy-start.2 = (bf16[2,128,2048]{2,1,0:T(8,128)(2,1)S(1)}, bf16[2,128,2048]{2,1,0:T(8,128)(2,1)}, u32[]{:S(2)}) copy-start(bf16[2,128,2048]{2,1,0:T(8,128)(2,1)} %cache.1) | copy-start | bytes 3145732
  21.8 25.0 %copy-start.3 = (s32[8,4]{0,1:T(4,128)S(1)}, s32[8,4]{0,1:T(4,128)}, u32[]{:S(2)}) copy-start(s32[8,4]{0,1:T(4,128)} %param.40) | copy-start | bytes 388
  21.8 26.4 %copy-start.1 = (bf16[4096,256]{1,0:T(8,128)(2,1)S(1)}, bf16[4096,256]{1,0:T(8,128)(2,1)}, u32[]{:S(2)}) copy-start(bf16[4096,256]{1,0:T(8,128)(2,1)} %weights.3) | copy-start | bytes 6291460
  22.6 1.5 %collective-permute-start.1 = (bf16[8,8,1536]{2,1,0:T(8,128)(2,1)S(1)}, bf16[8,8,1536]{2,1,0:T(8,128)(2,1)S(1)}, u32[]{:S(2)}, u32[]{:S(2)}) collective-permute-start(bf16[8,8,1536]{2,1,0:T(8,128)(2,1)S(1)} %get-tuple-element.35), channel_id=1, source_target_pairs={{0,1},{1,0},{2,3},{3,2},{4,5},{5,4},{6,7},{7,6},{8,9},{9,8},{10,11... | collective-permute-start | bytes 589832 | tf_op jit(solution)/shard_map/ppermute | solution.py:816
  46.8 1.4 %collective-permute-start.2 = (bf16[8,80,128]{2,1,0:T(8,128)(2,1)S(1)}, bf16[8,80,128]{2,1,0:T(8,128)(2,1)S(1)}, u32[]{:S(2)}, u32[]{:S(2)}) collective-permute-start(bf16[8,80,128]{2,1,0:T(8,128)(2,1)S(1)} %all_to_all.17._.near_ref), channel_id=1, source_target_pairs={{0,1},{1,0},{2,3},{3,2},{4,5},{5,4},{6,7},{7,6},{8,9},{9,8},{10,11... | collective-permute-start | bytes 491528 | tf_op jit(solution)/shard_map/ppermute | solution.py:827
